TPU v7x, 256 devices: a whole 4x4x8 slice. The times are simulated.
256 devices in a mesh: tm: 2 (over x_hi), space: 128 (over z, x_lo, y, core).
Axes of the slice: x: 4 (x_hi: 2, x_lo: 2; x = x_hi * 2 + x_lo), y: 4, z: 8, core: 2. Of those that a mesh axis runs over, the one named last changes fastest.
Arguments:
- states: float32 [4, 1024, 64, 128], P('tm', 'space'), may hold values from -1.2 to 1.2
- kappa: float32 [1024, 64, 128], P('space'), may hold values from 0.02 to 0.15
- rate: float32 [1024, 64, 128], P('space'), may hold values from 0.02 to 0.2
Outputs:
- ends: float32 [4, 1024, 64, 128], P('tm', 'space')
All inputs are finite; a program needn't handle non-finite values.
Results may differ from a plain program's by a relative error of at most 0.00013.
Values sent between devices are 32-bit elements; how exact they have to be, the bound alone decides.
No kernel may reach another device: no remote copies, remote signals or barrier semaphores. Data moves between devices by JAX's collectives and lax.ppermute only.
A program may use at most 64 MiB of HBM per device.

v0:
```python
import jax
import jax.numpy as jnp
from jax import lax
from jax.sharding import PartitionSpec as P

STEPS = 12


def extended_2(cells, sides, width):
    for axis, dim in sides:
        count = lax.axis_size(axis)
        ends = count - 1
        head = lax.slice_in_dim(cells, 0, width, axis=dim)
        tail = lax.slice_in_dim(cells, cells.shape[dim] - width, cells.shape[dim], axis=dim)
        cells = jnp.concatenate(
            [
                lax.ppermute(tail, axis, [(i, (i + 1) % count) for i in range(ends)]),
                cells,
                lax.ppermute(head, axis, [((i + 1) % count, i) for i in range(ends)]),
            ],
            axis=dim,
        )
    return cells


def passed_along(value, axis, steps):
    count = lax.axis_size(axis)
    initial, last = (max(0, -steps), min(count, count - steps))
    return lax.ppermute(value, axis, [(source, source + steps) for source in range(initial, last)])


def shifted(array, offset):
    lead = array.ndim - 3
    sizes = array.shape[-3:]
    picks = tuple(
        (slice(1 + offset[axis_no], sizes[axis_no] - 1 + offset[axis_no]) for axis_no in range(3))
    )
    return array[(slice(None),) * lead + picks]


def grid_step(field_ext, kappa_ext, rate_mid):
    padded = jnp.pad(field_ext, ((0, 0), (0, 0), (1, 1), (1, 1)))
    kappa_pad = jnp.pad(kappa_ext, ((0, 0), (1, 1), (1, 1)))
    centre = padded[:, 1:-1, 1:-1, 1:-1]
    kappa_mid = kappa_pad[1:-1, 1:-1, 1:-1]
    change = jnp.zeros_like(centre)
    for offset in ((1, 0, 0), (-1, 0, 0), (0, 1, 0), (0, -1, 0), (0, 0, 1), (0, 0, -1)):
        change = change + 0.5 * (kappa_mid + shifted(kappa_pad, offset)) * (
            shifted(padded, offset) - centre
        )
    return centre + change + rate_mid * (centre - centre * centre * centre)


def deep_run(padded, kappa_ext, rate_ext, offset_rows, total_rows, slab_rows):
    for substep in range(3):
        extent = 3 - substep
        kappa_part = kappa_ext[3 - extent : 3 + slab_rows + extent]
        rate_part = rate_ext[4 - extent : 2 + slab_rows + extent]
        padded = grid_step(padded, kappa_part, rate_part)
        positions = offset_rows - (extent - 1) + jnp.arange(slab_rows + 2 * extent - 2)
        inside = ((positions >= 0) & (positions < total_rows)).astype(jnp.float32)
        padded = padded * inside[None, :, None, None]
    return padded


def pair_table(width):
    fine_index = jnp.arange(width)[:, None] // 2
    coarse_index = jnp.arange(width // 2)[None, :]
    return (fine_index == coarse_index).astype(jnp.float32)


def restrict(field_now):
    lead = field_now.shape[:-3]
    sizes = field_now.shape[-3:]
    blocks = field_now.reshape(lead + (sizes[0] // 2, 2, sizes[1] // 2, 2, sizes[2]))
    summed = jnp.sum(blocks, axis=(-4, -2))
    folded = jnp.matmul(summed, pair_table(sizes[2]), precision=lax.Precision.HIGHEST)
    return folded * 0.125


def prolong(coarse_field):
    width = coarse_field.shape[-1] * 2
    spread = jnp.matmul(coarse_field, pair_table(width).T, precision=lax.Precision.HIGHEST)
    return jnp.repeat(jnp.repeat(spread, 2, axis=-3), 2, axis=-2)


def shards(states, kappa, rate):
    slab_rows = kappa.shape[0]
    offset_rows = lax.axis_index("space") * slab_rows
    total_rows = slab_rows * lax.axis_size("space")
    field_now = states
    kappa_ext, rate_ext = (
        extended_2(kappa, (("space", 0),), 3),
        extended_2(rate, (("space", 0),), 3),
    )
    for rim_block in range(STEPS // 3):
        padded = extended_2(field_now, (("space", 1),), 3)
        field_now = deep_run(padded, kappa_ext, rate_ext, offset_rows, total_rows, slab_rows)
    coarse_rows = slab_rows // 2
    coarse_offset = lax.axis_index("space") * coarse_rows
    coarse_total = coarse_rows * lax.axis_size("space")
    kappa_small = restrict(kappa)
    rate_small = 4.0 * restrict(rate)
    kappa_wide, rate_wide = (
        extended_2(kappa_small, (("space", 0),), 3),
        extended_2(rate_small, (("space", 0),), 3),
    )

    def coarse_prop(coarse_field):
        extended = extended_2(coarse_field, (("space", 1),), 3)
        return deep_run(extended, kappa_wide, rate_wide, coarse_offset, coarse_total, coarse_rows)

    old_coarse = coarse_prop(restrict(states))
    deltas = restrict(field_now) - old_coarse
    carried = restrict(states[0:1])
    newer = jnp.zeros_like(old_coarse)
    group = lax.axis_index("tm")
    sections = lax.axis_size("tm")
    for section in range(sections):
        for window in range(states.shape[0]):
            moved = coarse_prop(carried)
            newer = newer.at[window].set(jnp.where(group == section, moved[0], newer[window]))
            carried = deltas[window : window + 1] + moved
        if section + 1 < sections:
            carried = passed_along(carried, "tm", 1)
    return field_now + prolong(newer - old_coarse)


def solution(mesh):
    in_specs = (P("tm", "space", None, None), P("space", None, None), P("space", None, None))
    out_specs = P("tm", "space", None, None)
    return jax.shard_map(shards, mesh=mesh, in_specs=in_specs, out_specs=out_specs, check_vma=False)
```

profile of v0, /device:TPU:127, one launch (start us, length us, event | category | flops | bytes accessed | tf_op | source)
XLA Modules:
  0.0 181.5 jit_solution(4680120740949891224)
XLA Ops:
  1.0 5.2 %collective-permute-start.2 = (f32[3,64,128]{2,1,0:T(8,128)S(1)}, f32[3,64,128]{2,1,0:T(8,128)S(1)}, u32[]{:S(2)}, u32[]{:S(2)}) collective-permute-start(f32[3,64,128]{2,1,0:T(8,128)S(1)} %get-tuple-element.115), channel_id=1, source_target_pairs={{0,1},{1,2},{2,3},{3,4},{4,5},{5,6},{6,7},{7,8},{8,9},{9,10},{10,1... | collective-permute-start | bytes 294920 | tf_op jit(solution)/shard_map/ppermute | solution.py:17
  6.3 1.9 %collective-permute-start.3 = (f32[3,64,128]{2,1,0:T(8,128)S(1)}, f32[3,64,128]{2,1,0:T(8,128)S(1)}, u32[]{:S(2)}, u32[]{:S(2)}) collective-permute-start(f32[3,64,128]{2,1,0:T(8,128)S(1)} %get-tuple-element.114), channel_id=1, source_target_pairs={{1,0},{2,1},{3,2},{4,3},{5,4},{6,5},{7,6},{8,7},{9,8},{10,9},{11,1... | collective-permute-start | bytes 294920 | tf_op jit(solution)/shard_map/ppermute | solution.py:19
  9.9 7.8 %collective-permute-start.4 = (f32[3,64,128]{2,1,0:T(8,128)}, f32[3,64,128]{2,1,0:T(8,128)S(1)}, u32[]{:S(2)}, u32[]{:S(2)}) collective-permute-start(f32[3,64,128]{2,1,0:T(8,128)} %get-tuple-element.117), channel_id=1, source_target_pairs={{0,1},{1,2},{2,3},{3,4},{4,5},{5,6},{6,7},{7,8},{8,9},{9,10},{10,1... | collective-permute-start | bytes 294920 | tf_op jit(solution)/shard_map/ppermute | solution.py:17
  18.2 1.9 %collective-permute-start.16 = (f32[3,32,64]{2,1,0:T(8,128)S(1)}, f32[3,32,64]{2,1,0:T(8,128)S(1)}, u32[]{:S(2)}, u32[]{:S(2)}) collective-permute-start(f32[3,32,64]{2,1,0:T(8,128)S(1)} %get-tuple-element.134), channel_id=1, source_target_pairs={{0,1},{1,2},{2,3},{3,4},{4,5},{5,6},{6,7},{7,8},{8,9},{9,10},{10,1... | collective-permute-start | bytes 73736 | tf_op jit(solution)/shard_map/ppermute | solution.py:17
  20.1 2.4 %collective-permute-start.17 = (f32[3,32,64]{2,1,0:T(8,128)S(1)}, f32[3,32,64]{2,1,0:T(8,128)S(1)}, u32[]{:S(2)}, u32[]{:S(2)}) collective-permute-start(f32[3,32,64]{2,1,0:T(8,128)S(1)} %get-tuple-element.135), channel_id=1, source_target_pairs={{1,0},{2,1},{3,2},{4,3},{5,4},{6,5},{7,6},{8,7},{9,8},{10,9},{11,1... | collective-permute-start | bytes 73736 | tf_op jit(solution)/shard_map/ppermute | solution.py:19
  25.5 7.4 %collective-permute-start.14 = (f32[3,32,64]{2,1,0:T(8,128)S(1)}, f32[3,32,64]{2,1,0:T(8,128)S(1)}, u32[]{:S(2)}, u32[]{:S(2)}) collective-permute-start(f32[3,32,64]{2,1,0:T(8,128)S(1)} %get-tuple-element.130), channel_id=1, source_target_pairs={{0,1},{1,2},{2,3},{3,4},{4,5},{5,6},{6,7},{7,8},{8,9},{9,10},{10,1... | collective-permute-start | bytes 73736 | tf_op jit(solution)/shard_map/ppermute | solution.py:17
  32.9 1.9 %collective-permute-start.15 = (f32[3,32,64]{2,1,0:T(8,128)S(1)}, f32[3,32,64]{2,1,0:T(8,128)S(1)}, u32[]{:S(2)}, u32[]{:S(2)}) collective-permute-start(f32[3,32,64]{2,1,0:T(8,128)S(1)} %get-tuple-element.131), channel_id=1, source_target_pairs={{1,0},{2,1},{3,2},{4,3},{5,4},{6,5},{7,6},{8,7},{9,8},{10,9},{11,1... | collective-permute-start | bytes 73736 | tf_op jit(solution)/shard_map/ppermute | solution.py:19
  34.9 7.9 %collective-permute-start.12 = (f32[1,3,32,64]{3,2,1,0:T(8,128)S(1)}, f32[1,3,32,64]{3,2,1,0:T(8,128)S(1)}, u32[]{:S(2)}, u32[]{:S(2)}) collective-permute-start(f32[1,3,32,64]{3,2,1,0:T(8,128)S(1)} %get-tuple-element.132), channel_id=1, source_target_pairs={{0,1},{1,2},{2,3},{3,4},{4,5},{5,6},{6,7},{7,8},{8,9},{9,10},{10,1... | collective-permute-start | bytes 73736 | tf_op jit(solution)/shard_map/ppermute | solution.py:17
  42.8 1.9 %collective-permute-start.13 = (f32[1,3,32,64]{3,2,1,0:T(8,128)S(1)}, f32[1,3,32,64]{3,2,1,0:T(8,128)S(1)}, u32[]{:S(2)}, u32[]{:S(2)}) collective-permute-start(f32[1,3,32,64]{3,2,1,0:T(8,128)S(1)} %get-tuple-element.133), channel_id=1, source_target_pairs={{1,0},{2,1},{3,2},{4,3},{5,4},{6,5},{7,6},{8,7},{9,8},{10,9},{11,1... | collective-permute-start | bytes 73736 | tf_op jit(solution)/shard_map/ppermute | solution.py:19
  44.8 7.9 %collective-permute-start.18 = (f32[2,3,32,64]{3,2,1,0:T(8,128)}, f32[2,3,32,64]{3,2,1,0:T(8,128)S(1)}, u32[]{:S(2)}, u32[]{:S(2)}) collective-permute-start(f32[2,3,32,64]{3,2,1,0:T(8,128)} %get-tuple-element.118), channel_id=1, source_target_pairs={{0,1},{1,2},{2,3},{3,4},{4,5},{5,6},{6,7},{7,8},{8,9},{9,10},{10,1... | collective-permute-start | bytes 147464 | tf_op jit(solution)/shard_map/ppermute | solution.py:17
  58.1 5.0 %collective-permute-done.19 = f32[2,3,32,64]{3,2,1,0:T(8,128)S(1)} collective-permute-done((f32[2,3,32,64]{3,2,1,0:T(8,128)}, f32[2,3,32,64]{3,2,1,0:T(8,128)S(1)}, u32[]{:S(2)}, u32[]{:S(2)}) %collective-permute-start.19) | collective-permute-done | bytes 49184 | tf_op jit(solution)/shard_map/ppermute | solution.py:19
  63.0 2.9 %collective-permute-start = (f32[2,3,64,128]{3,2,1,0:T(8,128)}, f32[2,3,64,128]{3,2,1,0:T(8,128)S(1)}, u32[]{:S(2)}, u32[]{:S(2)}) collective-permute-start(f32[2,3,64,128]{3,2,1,0:T(8,128)} %get-tuple-element.94), channel_id=1, source_target_pairs={{0,1},{1,2},{2,3},{3,4},{4,5},{5,6},{6,7},{7,8},{8,9},{9,10},{10,1... | collective-permute-start | bytes 589832 | tf_op jit(solution)/shard_map/ppermute | solution.py:17
  69.2 8.2 %collective-permute-done.1 = f32[2,3,64,128]{3,2,1,0:T(8,128)S(1)} collective-permute-done((f32[2,3,64,128]{3,2,1,0:T(8,128)}, f32[2,3,64,128]{3,2,1,0:T(8,128)S(1)}, u32[]{:S(2)}, u32[]{:S(2)}) %collective-permute-start.1) | collective-permute-done | bytes 196640 | tf_op jit(solution)/shard_map/ppermute | solution.py:19
  79.5 1.9 %collective-permute-start.6 = (f32[2,3,64,128]{3,2,1,0:T(8,128)S(1)}, f32[2,3,64,128]{3,2,1,0:T(8,128)S(1)}, u32[]{:S(2)}, u32[]{:S(2)}) collective-permute-start(f32[2,3,64,128]{3,2,1,0:T(8,128)S(1)} %get-tuple-element.91), channel_id=1, source_target_pairs={{0,1},{1,2},{2,3},{3,4},{4,5},{5,6},{6,7},{7,8},{8,9},{9,10},{10,1... | collective-permute-start | bytes 589832 | tf_op jit(solution)/shard_map/ppermute | solution.py:17
  81.4 2.4 %collective-permute-start.7 = (f32[2,3,64,128]{3,2,1,0:T(8,128)S(1)}, f32[2,3,64,128]{3,2,1,0:T(8,128)S(1)}, u32[]{:S(2)}, u32[]{:S(2)}) collective-permute-start(f32[2,3,64,128]{3,2,1,0:T(8,128)S(1)} %get-tuple-element.92), channel_id=1, source_target_pairs={{1,0},{2,1},{3,2},{4,3},{5,4},{6,5},{7,6},{8,7},{9,8},{10,9},{11,1... | collective-permute-start | bytes 589832 | tf_op jit(solution)/shard_map/ppermute | solution.py:19
  84.2 8.4 %collective-permute-done.7 = f32[2,3,64,128]{3,2,1,0:T(8,128)S(1)} collective-permute-done((f32[2,3,64,128]{3,2,1,0:T(8,128)S(1)}, f32[2,3,64,128]{3,2,1,0:T(8,128)S(1)}, u32[]{:S(2)}, u32[]{:S(2)}) %collective-permute-start.7) | collective-permute-done | bytes 196640 | tf_op jit(solution)/shard_map/ppermute | solution.py:19
  94.8 1.9 %collective-permute-start.8 = (f32[2,3,64,128]{3,2,1,0:T(8,128)S(1)}, f32[2,3,64,128]{3,2,1,0:T(8,128)S(1)}, u32[]{:S(2)}, u32[]{:S(2)}) collective-permute-start(f32[2,3,64,128]{3,2,1,0:T(8,128)S(1)} %get-tuple-element.89), channel_id=1, source_target_pairs={{0,1},{1,2},{2,3},{3,4},{4,5},{5,6},{6,7},{7,8},{8,9},{9,10},{10,1... | collective-permute-start | bytes 589832 | tf_op jit(solution)/shard_map/ppermute | solution.py:17
  96.8 2.6 %collective-permute-start.9 = (f32[2,3,64,128]{3,2,1,0:T(8,128)S(1)}, f32[2,3,64,128]{3,2,1,0:T(8,128)S(1)}, u32[]{:S(2)}, u32[]{:S(2)}) collective-permute-start(f32[2,3,64,128]{3,2,1,0:T(8,128)S(1)} %get-tuple-element.90), channel_id=1, source_target_pairs={{1,0},{2,1},{3,2},{4,3},{5,4},{6,5},{7,6},{8,7},{9,8},{10,9},{11,1... | collective-permute-start | bytes 589832 | tf_op jit(solution)/shard_map/ppermute | solution.py:19
  99.7 8.3 %collective-permute-done.9 = f32[2,3,64,128]{3,2,1,0:T(8,128)S(1)} collective-permute-done((f32[2,3,64,128]{3,2,1,0:T(8,128)S(1)}, f32[2,3,64,128]{3,2,1,0:T(8,128)S(1)}, u32[]{:S(2)}, u32[]{:S(2)}) %collective-permute-start.9) | collective-permute-done | bytes 196640 | tf_op jit(solution)/shard_map/ppermute | solution.py:19
  110.2 1.9 %collective-permute-start.10 = (f32[2,3,64,128]{3,2,1,0:T(8,128)S(1)}, f32[2,3,64,128]{3,2,1,0:T(8,128)S(1)}, u32[]{:S(2)}, u32[]{:S(2)}) collective-permute-start(f32[2,3,64,128]{3,2,1,0:T(8,128)S(1)} %get-tuple-element.87), channel_id=1, source_target_pairs={{0,1},{1,2},{2,3},{3,4},{4,5},{5,6},{6,7},{7,8},{8,9},{9,10},{10,1... | collective-permute-start | bytes 589832 | tf_op jit(solution)/shard_map/ppermute | solution.py:17
  112.1 2.4 %collective-permute-start.11 = (f32[2,3,64,128]{3,2,1,0:T(8,128)S(1)}, f32[2,3,64,128]{3,2,1,0:T(8,128)S(1)}, u32[]{:S(2)}, u32[]{:S(2)}) collective-permute-start(f32[2,3,64,128]{3,2,1,0:T(8,128)S(1)} %get-tuple-element.88), channel_id=1, source_target_pairs={{1,0},{2,1},{3,2},{4,3},{5,4},{6,5},{7,6},{8,7},{9,8},{10,9},{11,1... | collective-permute-start | bytes 589832 | tf_op jit(solution)/shard_map/ppermute | solution.py:19
  115.4 7.9 %collective-permute-done.11 = f32[2,3,64,128]{3,2,1,0:T(8,128)S(1)} collective-permute-done((f32[2,3,64,128]{3,2,1,0:T(8,128)S(1)}, f32[2,3,64,128]{3,2,1,0:T(8,128)S(1)}, u32[]{:S(2)}, u32[]{:S(2)}) %collective-permute-start.11) | collective-permute-done | bytes 196640 | tf_op jit(solution)/shard_map/ppermute | solution.py:19
  126.2 2.1 %reduce_sum.48 = f32[2,4,32,128]{3,2,1,0:T(8,128)} reduce(f32[2,4,2,32,2,128]{5,4,3,2,1,0:T(2,128)} %bitcast.156, f32[]{:T(128)} %constant.156.clone.1), dimensions={2,4}, to_apply=%region_3.4 | reduce | flops 98304 | bytes 655364 | tf_op jit(solution)/shard_map/reduce_sum | solution.py:76
  134.2 2.4 %collective-permute-start.21 = (f32[1,3,32,64]{3,2,1,0:T(8,128)}, f32[1,3,32,64]{3,2,1,0:T(8,128)}, u32[]{:S(2)}, u32[]{:S(2)}) collective-permute-start(f32[1,3,32,64]{3,2,1,0:T(8,128)} %get-tuple-element.129), channel_id=1, source_target_pairs={{1,0},{2,1},{3,2},{4,3},{5,4},{6,5},{7,6},{8,7},{9,8},{10,9},{11,1... | collective-permute-start | bytes 73736 | tf_op jit(solution)/shard_map/ppermute | solution.py:19
  136.7 7.4 %collective-permute-done.21 = f32[1,3,32,64]{3,2,1,0:T(8,128)} collective-permute-done((f32[1,3,32,64]{3,2,1,0:T(8,128)}, f32[1,3,32,64]{3,2,1,0:T(8,128)}, u32[]{:S(2)}, u32[]{:S(2)}) %collective-permute-start.21) | collective-permute-done | bytes 24608 | tf_op jit(solution)/shard_map/ppermute | solution.py:19
  148.5 5.2 %collective-permute-done.22 = f32[1,4,32,64]{3,2,1,0:T(8,128)S(1)} collective-permute-done((f32[1,4,32,64]{3,2,1,0:T(8,128)S(1)}, f32[1,4,32,64]{3,2,1,0:T(8,128)S(1)}, u32[]{:S(2)}, u32[]{:S(2)}) %collective-permute-start.22) | collective-permute-done | bytes 32800 | tf_op jit(solution)/shard_map/ppermute | solution.py:29
  153.7 3.0 %collective-permute-start.23 = (f32[1,3,32,64]{3,2,1,0:T(8,128)S(1)}, f32[1,3,32,64]{3,2,1,0:T(8,128)S(1)}, u32[]{:S(2)}, u32[]{:S(2)}) collective-permute-start(f32[1,3,32,64]{3,2,1,0:T(8,128)S(1)} %get-tuple-element.127), channel_id=1, source_target_pairs={{0,1},{1,2},{2,3},{3,4},{4,5},{5,6},{6,7},{7,8},{8,9},{9,10},{10,1... | collective-permute-start | bytes 73736 | tf_op jit(solution)/shard_map/ppermute | solution.py:17
  156.8 1.9 %collective-permute-start.24 = (f32[1,3,32,64]{3,2,1,0:T(8,128)S(1)}, f32[1,3,32,64]{3,2,1,0:T(8,128)S(1)}, u32[]{:S(2)}, u32[]{:S(2)}) collective-permute-start(f32[1,3,32,64]{3,2,1,0:T(8,128)S(1)} %get-tuple-element.126), channel_id=1, source_target_pairs={{1,0},{2,1},{3,2},{4,3},{5,4},{6,5},{7,6},{8,7},{9,8},{10,9},{11,1... | collective-permute-start | bytes 73736 | tf_op jit(solution)/shard_map/ppermute | solution.py:19
  158.7 7.7 %collective-permute-done.24 = f32[1,3,32,64]{3,2,1,0:T(8,128)S(1)} collective-permute-done((f32[1,3,32,64]{3,2,1,0:T(8,128)S(1)}, f32[1,3,32,64]{3,2,1,0:T(8,128)S(1)}, u32[]{:S(2)}, u32[]{:S(2)}) %collective-permute-start.24) | collective-permute-done | bytes 24608 | tf_op jit(solution)/shard_map/ppermute | solution.py:19
  166.9 1.9 %collective-permute-start.25 = (f32[1,3,32,64]{3,2,1,0:T(8,128)S(1)}, f32[1,3,32,64]{3,2,1,0:T(8,128)S(1)}, u32[]{:S(2)}, u32[]{:S(2)}) collective-permute-start(f32[1,3,32,64]{3,2,1,0:T(8,128)S(1)} %get-tuple-element.124), channel_id=1, source_target_pairs={{0,1},{1,2},{2,3},{3,4},{4,5},{5,6},{6,7},{7,8},{8,9},{9,10},{10,1... | collective-permute-start | bytes 73736 | tf_op jit(solution)/shard_map/ppermute | solution.py:17
  168.8 2.4 %collective-permute-start.26 = (f32[1,3,32,64]{3,2,1,0:T(8,128)S(1)}, f32[1,3,32,64]{3,2,1,0:T(8,128)S(1)}, u32[]{:S(2)}, u32[]{:S(2)}) collective-permute-start(f32[1,3,32,64]{3,2,1,0:T(8,128)S(1)} %get-tuple-element.125), channel_id=1, source_target_pairs={{1,0},{2,1},{3,2},{4,3},{5,4},{6,5},{7,6},{8,7},{9,8},{10,9},{11,1... | collective-permute-start | bytes 73736 | tf_op jit(solution)/shard_map/ppermute | solution.py:19
  171.2 7.2 %collective-permute-done.26 = f32[1,3,32,64]{3,2,1,0:T(8,128)S(1)} collective-permute-done((f32[1,3,32,64]{3,2,1,0:T(8,128)S(1)}, f32[1,3,32,64]{3,2,1,0:T(8,128)S(1)}, u32[]{:S(2)}, u32[]{:S(2)}) %collective-permute-start.26) | collective-permute-done | bytes 24608 | tf_op jit(solution)/shard_map/ppermute | solution.py:19
  (219 shorter events, 38.6 us)
Async XLA Ops:
  1.0 67.0 %collective-permute-start.2 = (f32[3,64,128]{2,1,0:T(8,128)S(1)}, f32[3,64,128]{2,1,0:T(8,128)S(1)}, u32[]{:S(2)}, u32[]{:S(2)}) collective-permute-start(f32[3,64,128]{2,1,0:T(8,128)S(1)} %get-tuple-element.115), channel_id=1, source_target_pairs={{0,1},{1,2},{2,3},{3,4},{4,5},{5,6},{6,7},{7,8},{8,9},{9,10},{10,1... | collective-permute-start | bytes 294920 | tf_op jit(solution)/shard_map/ppermute | solution.py:17
  6.3 61.9 %collective-permute-start.3 = (f32[3,64,128]{2,1,0:T(8,128)S(1)}, f32[3,64,128]{2,1,0:T(8,128)S(1)}, u32[]{:S(2)}, u32[]{:S(2)}) collective-permute-start(f32[3,64,128]{2,1,0:T(8,128)S(1)} %get-tuple-element.114), channel_id=1, source_target_pairs={{1,0},{2,1},{3,2},{4,3},{5,4},{6,5},{7,6},{8,7},{9,8},{10,9},{11,1... | collective-permute-start | bytes 294920 | tf_op jit(solution)/shard_map/ppermute | solution.py:19
  9.9 56.1 %collective-permute-start.4 = (f32[3,64,128]{2,1,0:T(8,128)}, f32[3,64,128]{2,1,0:T(8,128)S(1)}, u32[]{:S(2)}, u32[]{:S(2)}) collective-permute-start(f32[3,64,128]{2,1,0:T(8,128)} %get-tuple-element.117), channel_id=1, source_target_pairs={{0,1},{1,2},{2,3},{3,4},{4,5},{5,6},{6,7},{7,8},{8,9},{9,10},{10,1... | collective-permute-start | bytes 294920 | tf_op jit(solution)/shard_map/ppermute | solution.py:17
  17.7 110.6 %copy-start.39 = (s32[128]{0:T(128)}, s32[128]{0:T(128)S(1)}, u32[]{:S(2)}) copy-start(s32[128]{0:T(128)S(1)} %and_select_fusion) | copy-start | bytes 1540
  18.2 7.4 %collective-permute-start.16 = (f32[3,32,64]{2,1,0:T(8,128)S(1)}, f32[3,32,64]{2,1,0:T(8,128)S(1)}, u32[]{:S(2)}, u32[]{:S(2)}) collective-permute-start(f32[3,32,64]{2,1,0:T(8,128)S(1)} %get-tuple-element.134), channel_id=1, source_target_pairs={{0,1},{1,2},{2,3},{3,4},{4,5},{5,6},{6,7},{7,8},{8,9},{9,10},{10,1... | collective-permute-start | bytes 73736 | tf_op jit(solution)/shard_map/ppermute | solution.py:17
  20.1 12.8 %collective-permute-start.17 = (f32[3,32,64]{2,1,0:T(8,128)S(1)}, f32[3,32,64]{2,1,0:T(8,128)S(1)}, u32[]{:S(2)}, u32[]{:S(2)}) collective-permute-start(f32[3,32,64]{2,1,0:T(8,128)S(1)} %get-tuple-element.135), channel_id=1, source_target_pairs={{1,0},{2,1},{3,2},{4,3},{5,4},{6,5},{7,6},{8,7},{9,8},{10,9},{11,1... | collective-permute-start | bytes 73736 | tf_op jit(solution)/shard_map/ppermute | solution.py:19
  23.3 101.6 %copy-start.47 = (f32[8]{0:T(128)}, f32[8]{0:T(128)S(1)}, u32[]{:S(2)}) copy-start(f32[8]{0:T(128)S(1)} %and_convert_fusion.3) | copy-start | bytes 100
  23.3 91.2 %copy-start.41 = (f32[4]{0:T(128)}, f32[4]{0:T(128)S(1)}, u32[]{:S(2)}) copy-start(f32[4]{0:T(128)S(1)} %and_convert_fusion) | copy-start | bytes 52
  24.2 59.7 %copy-start.45 = (f32[8]{0:T(128)}, f32[8]{0:T(128)S(1)}, u32[]{:S(2)}) copy-start(f32[8]{0:T(128)S(1)} %and_convert_fusion.2) | copy-start | bytes 100
  25.5 73.8 %copy-start.43 = (f32[6]{0:T(128)}, f32[6]{0:T(128)S(1)}, u32[]{:S(2)}) copy-start(f32[6]{0:T(128)S(1)} %and_convert_fusion.1) | copy-start | bytes 76
  25.5 9.4 %collective-permute-start.14 = (f32[3,32,64]{2,1,0:T(8,128)S(1)}, f32[3,32,64]{2,1,0:T(8,128)S(1)}, u32[]{:S(2)}, u32[]{:S(2)}) collective-permute-start(f32[3,32,64]{2,1,0:T(8,128)S(1)} %get-tuple-element.130), channel_id=1, source_target_pairs={{0,1},{1,2},{2,3},{3,4},{4,5},{5,6},{6,7},{7,8},{8,9},{9,10},{10,1... | collective-permute-start | bytes 73736 | tf_op jit(solution)/shard_map/ppermute | solution.py:17
  32.9 9.8 %collective-permute-start.15 = (f32[3,32,64]{2,1,0:T(8,128)S(1)}, f32[3,32,64]{2,1,0:T(8,128)S(1)}, u32[]{:S(2)}, u32[]{:S(2)}) collective-permute-start(f32[3,32,64]{2,1,0:T(8,128)S(1)} %get-tuple-element.131), channel_id=1, source_target_pairs={{1,0},{2,1},{3,2},{4,3},{5,4},{6,5},{7,6},{8,7},{9,8},{10,9},{11,1... | collective-permute-start | bytes 73736 | tf_op jit(solution)/shard_map/ppermute | solution.py:19
  34.9 9.9 %collective-permute-start.12 = (f32[1,3,32,64]{3,2,1,0:T(8,128)S(1)}, f32[1,3,32,64]{3,2,1,0:T(8,128)S(1)}, u32[]{:S(2)}, u32[]{:S(2)}) collective-permute-start(f32[1,3,32,64]{3,2,1,0:T(8,128)S(1)} %get-tuple-element.132), channel_id=1, source_target_pairs={{0,1},{1,2},{2,3},{3,4},{4,5},{5,6},{6,7},{7,8},{8,9},{9,10},{10,1... | collective-permute-start | bytes 73736 | tf_op jit(solution)/shard_map/ppermute | solution.py:17
  42.8 9.9 %collective-permute-start.13 = (f32[1,3,32,64]{3,2,1,0:T(8,128)S(1)}, f32[1,3,32,64]{3,2,1,0:T(8,128)S(1)}, u32[]{:S(2)}, u32[]{:S(2)}) collective-permute-start(f32[1,3,32,64]{3,2,1,0:T(8,128)S(1)} %get-tuple-element.133), channel_id=1, source_target_pairs={{1,0},{2,1},{3,2},{4,3},{5,4},{6,5},{7,6},{8,7},{9,8},{10,9},{11,1... | collective-permute-start | bytes 73736 | tf_op jit(solution)/shard_map/ppermute | solution.py:19
  44.8 11.2 %collective-permute-start.18 = (f32[2,3,32,64]{3,2,1,0:T(8,128)}, f32[2,3,32,64]{3,2,1,0:T(8,128)S(1)}, u32[]{:S(2)}, u32[]{:S(2)}) collective-permute-start(f32[2,3,32,64]{3,2,1,0:T(8,128)} %get-tuple-element.118), channel_id=1, source_target_pairs={{0,1},{1,2},{2,3},{3,4},{4,5},{5,6},{6,7},{7,8},{8,9},{9,10},{10,1... | collective-permute-start | bytes 147464 | tf_op jit(solution)/shard_map/ppermute | solution.py:17
  52.6 10.4 %collective-permute-start.19 = (f32[2,3,32,64]{3,2,1,0:T(8,128)}, f32[2,3,32,64]{3,2,1,0:T(8,128)S(1)}, u32[]{:S(2)}, u32[]{:S(2)}) collective-permute-start(f32[2,3,32,64]{3,2,1,0:T(8,128)} %get-tuple-element.119), channel_id=1, source_target_pairs={{1,0},{2,1},{3,2},{4,3},{5,4},{6,5},{7,6},{8,7},{9,8},{10,9},{11,1... | collective-permute-start | bytes 147464 | tf_op jit(solution)/shard_map/ppermute | solution.py:19
  56.1 11.8 %collective-permute-start.5 = (f32[3,64,128]{2,1,0:T(8,128)S(1)}, f32[3,64,128]{2,1,0:T(8,128)S(1)}, u32[]{:S(2)}, u32[]{:S(2)}) collective-permute-start(f32[3,64,128]{2,1,0:T(8,128)S(1)} %copy-done.38), channel_id=1, source_target_pairs={{1,0},{2,1},{3,2},{4,3},{5,4},{6,5},{7,6},{8,7},{9,8},{10,9},{11,1... | collective-permute-start | bytes 294920 | tf_op jit(solution)/shard_map/ppermute | solution.py:19
  63.0 6.1 %collective-permute-start = (f32[2,3,64,128]{3,2,1,0:T(8,128)}, f32[2,3,64,128]{3,2,1,0:T(8,128)S(1)}, u32[]{:S(2)}, u32[]{:S(2)}) collective-permute-start(f32[2,3,64,128]{3,2,1,0:T(8,128)} %get-tuple-element.94), channel_id=1, source_target_pairs={{0,1},{1,2},{2,3},{3,4},{4,5},{5,6},{6,7},{7,8},{8,9},{9,10},{10,1... | collective-permute-start | bytes 589832 | tf_op jit(solution)/shard_map/ppermute | solution.py:17
  66.0 11.4 %collective-permute-start.1 = (f32[2,3,64,128]{3,2,1,0:T(8,128)}, f32[2,3,64,128]{3,2,1,0:T(8,128)S(1)}, u32[]{:S(2)}, u32[]{:S(2)}) collective-permute-start(f32[2,3,64,128]{3,2,1,0:T(8,128)} %get-tuple-element.93), channel_id=1, source_target_pairs={{1,0},{2,1},{3,2},{4,3},{5,4},{6,5},{7,6},{8,7},{9,8},{10,9},{11,1... | collective-permute-start | bytes 589832 | tf_op jit(solution)/shard_map/ppermute | solution.py:19
  79.5 4.7 %collective-permute-start.6 = (f32[2,3,64,128]{3,2,1,0:T(8,128)S(1)}, f32[2,3,64,128]{3,2,1,0:T(8,128)S(1)}, u32[]{:S(2)}, u32[]{:S(2)}) collective-permute-start(f32[2,3,64,128]{3,2,1,0:T(8,128)S(1)} %get-tuple-element.91), channel_id=1, source_target_pairs={{0,1},{1,2},{2,3},{3,4},{4,5},{5,6},{6,7},{7,8},{8,9},{9,10},{10,1... | collective-permute-start | bytes 589832 | tf_op jit(solution)/shard_map/ppermute | solution.py:17
  81.4 11.2 %collective-permute-start.7 = (f32[2,3,64,128]{3,2,1,0:T(8,128)S(1)}, f32[2,3,64,128]{3,2,1,0:T(8,128)S(1)}, u32[]{:S(2)}, u32[]{:S(2)}) collective-permute-start(f32[2,3,64,128]{3,2,1,0:T(8,128)S(1)} %get-tuple-element.92), channel_id=1, source_target_pairs={{1,0},{2,1},{3,2},{4,3},{5,4},{6,5},{7,6},{8,7},{9,8},{10,9},{11,1... | collective-permute-start | bytes 589832 | tf_op jit(solution)/shard_map/ppermute | solution.py:19
  94.8 4.8 %collective-permute-start.8 = (f32[2,3,64,128]{3,2,1,0:T(8,128)S(1)}, f32[2,3,64,128]{3,2,1,0:T(8,128)S(1)}, u32[]{:S(2)}, u32[]{:S(2)}) collective-permute-start(f32[2,3,64,128]{3,2,1,0:T(8,128)S(1)} %get-tuple-element.89), channel_id=1, source_target_pairs={{0,1},{1,2},{2,3},{3,4},{4,5},{5,6},{6,7},{7,8},{8,9},{9,10},{10,1... | collective-permute-start | bytes 589832 | tf_op jit(solution)/shard_map/ppermute | solution.py:17
  96.8 11.2 %collective-permute-start.9 = (f32[2,3,64,128]{3,2,1,0:T(8,128)S(1)}, f32[2,3,64,128]{3,2,1,0:T(8,128)S(1)}, u32[]{:S(2)}, u32[]{:S(2)}) collective-permute-start(f32[2,3,64,128]{3,2,1,0:T(8,128)S(1)} %get-tuple-element.90), channel_id=1, source_target_pairs={{1,0},{2,1},{3,2},{4,3},{5,4},{6,5},{7,6},{8,7},{9,8},{10,9},{11,1... | collective-permute-start | bytes 589832 | tf_op jit(solution)/shard_map/ppermute | solution.py:19
  110.2 5.2 %collective-permute-start.10 = (f32[2,3,64,128]{3,2,1,0:T(8,128)S(1)}, f32[2,3,64,128]{3,2,1,0:T(8,128)S(1)}, u32[]{:S(2)}, u32[]{:S(2)}) collective-permute-start(f32[2,3,64,128]{3,2,1,0:T(8,128)S(1)} %get-tuple-element.87), channel_id=1, source_target_pairs={{0,1},{1,2},{2,3},{3,4},{4,5},{5,6},{6,7},{7,8},{8,9},{9,10},{10,1... | collective-permute-start | bytes 589832 | tf_op jit(solution)/shard_map/ppermute | solution.py:17
  112.1 11.2 %collective-permute-start.11 = (f32[2,3,64,128]{3,2,1,0:T(8,128)S(1)}, f32[2,3,64,128]{3,2,1,0:T(8,128)S(1)}, u32[]{:S(2)}, u32[]{:S(2)}) collective-permute-start(f32[2,3,64,128]{3,2,1,0:T(8,128)S(1)} %get-tuple-element.88), channel_id=1, source_target_pairs={{1,0},{2,1},{3,2},{4,3},{5,4},{6,5},{7,6},{8,7},{9,8},{10,9},{11,1... | collective-permute-start | bytes 589832 | tf_op jit(solution)/shard_map/ppermute | solution.py:19
  132.3 4.4 %collective-permute-start.20 = (f32[1,3,32,64]{3,2,1,0:T(8,128)}, f32[1,3,32,64]{3,2,1,0:T(8,128)S(1)}, u32[]{:S(2)}, u32[]{:S(2)}) collective-permute-start(f32[1,3,32,64]{3,2,1,0:T(8,128)} %get-tuple-element.128), channel_id=1, source_target_pairs={{0,1},{1,2},{2,3},{3,4},{4,5},{5,6},{6,7},{7,8},{8,9},{9,10},{10,1... | collective-permute-start | bytes 73736 | tf_op jit(solution)/shard_map/ppermute | solution.py:17
  134.2 9.9 %collective-permute-start.21 = (f32[1,3,32,64]{3,2,1,0:T(8,128)}, f32[1,3,32,64]{3,2,1,0:T(8,128)}, u32[]{:S(2)}, u32[]{:S(2)}) collective-permute-start(f32[1,3,32,64]{3,2,1,0:T(8,128)} %get-tuple-element.129), channel_id=1, source_target_pairs={{1,0},{2,1},{3,2},{4,3},{5,4},{6,5},{7,6},{8,7},{9,8},{10,9},{11,1... | collective-permute-start | bytes 73736 | tf_op jit(solution)/shard_map/ppermute | solution.py:19
  147.2 6.5 %collective-permute-start.22 = (f32[1,4,32,64]{3,2,1,0:T(8,128)S(1)}, f32[1,4,32,64]{3,2,1,0:T(8,128)S(1)}, u32[]{:S(2)}, u32[]{:S(2)}) collective-permute-start(f32[1,4,32,64]{3,2,1,0:T(8,128)S(1)} %get-tuple-element.55), channel_id=1, source_target_pairs={{0,128},{1,129},{2,130},{3,131},{4,132},{5,133},{6,134},{7,135},{8... | collective-permute-start | bytes 98312 | tf_op jit(solution)/shard_map/ppermute | solution.py:29
  153.7 5.0 %collective-permute-start.23 = (f32[1,3,32,64]{3,2,1,0:T(8,128)S(1)}, f32[1,3,32,64]{3,2,1,0:T(8,128)S(1)}, u32[]{:S(2)}, u32[]{:S(2)}) collective-permute-start(f32[1,3,32,64]{3,2,1,0:T(8,128)S(1)} %get-tuple-element.127), channel_id=1, source_target_pairs={{0,1},{1,2},{2,3},{3,4},{4,5},{5,6},{6,7},{7,8},{8,9},{9,10},{10,1... | collective-permute-start | bytes 73736 | tf_op jit(solution)/shard_map/ppermute | solution.py:17
  156.8 9.6 %collective-permute-start.24 = (f32[1,3,32,64]{3,2,1,0:T(8,128)S(1)}, f32[1,3,32,64]{3,2,1,0:T(8,128)S(1)}, u32[]{:S(2)}, u32[]{:S(2)}) collective-permute-start(f32[1,3,32,64]{3,2,1,0:T(8,128)S(1)} %get-tuple-element.126), channel_id=1, source_target_pairs={{1,0},{2,1},{3,2},{4,3},{5,4},{6,5},{7,6},{8,7},{9,8},{10,9},{11,1... | collective-permute-start | bytes 73736 | tf_op jit(solution)/shard_map/ppermute | solution.py:19
  166.9 4.4 %collective-permute-start.25 = (f32[1,3,32,64]{3,2,1,0:T(8,128)S(1)}, f32[1,3,32,64]{3,2,1,0:T(8,128)S(1)}, u32[]{:S(2)}, u32[]{:S(2)}) collective-permute-start(f32[1,3,32,64]{3,2,1,0:T(8,128)S(1)} %get-tuple-element.124), channel_id=1, source_target_pairs={{0,1},{1,2},{2,3},{3,4},{4,5},{5,6},{6,7},{7,8},{8,9},{9,10},{10,1... | collective-permute-start | bytes 73736 | tf_op jit(solution)/shard_map/ppermute | solution.py:17
  168.8 9.6 %collective-permute-start.26 = (f32[1,3,32,64]{3,2,1,0:T(8,128)S(1)}, f32[1,3,32,64]{3,2,1,0:T(8,128)S(1)}, u32[]{:S(2)}, u32[]{:S(2)}) collective-permute-start(f32[1,3,32,64]{3,2,1,0:T(8,128)S(1)} %get-tuple-element.125), channel_id=1, source_target_pairs={{1,0},{2,1},{3,2},{4,3},{5,4},{6,5},{7,6},{8,7},{9,8},{10,9},{11,1... | collective-permute-start | bytes 73736 | tf_op jit(solution)/shard_map/ppermute | solution.py:19
  (47 other events, 915.8 us)
where the time goes:
time: 183 us; the launch traced here: 182 us
  starting transfers between devices  83 us (45%)
  waiting for transfers between devices  65.3 us (36%)
  other arithmetic  20.9 us (11%)
  local copies, waits for them, and re-layouts  8.73 us (5%)
  matrix products  2.13 us (1%)
    ppermute x13, waiting for transfers between devices, extended_2(): lax.ppermute(head, axis, [((i + 1) % count, i) for i in range(ends)])  60.1 us
    ppermute x13, starting transfers between devices, extended_2(): lax.ppermute(tail, axis, [(i, (i + 1) % count) for i in range(ends)])  53.6 us
    ppermute x13, starting transfers between devices, extended_2(): lax.ppermute(head, axis, [((i + 1) % count, i) for i in range(ends)])  28 us
    mul x23, other arithmetic, deep_run(): padded = padded * inside[None, :, None, None]  12.3 us
    ppermute x1, waiting for transfers between devices, passed_along(): lax.ppermute(value, axis, [(source, source + steps) for source in range(i...  5.2 us
  transfers between devices with their start and end apart: 27, of which 9 were waited for; matrix products, arithmetic and copies ran while one was open for 5% of the time, Pallas kernels for 0%

commit v1 on v0

v1 whole, which is shorter than its diff:
```python
import jax
import jax.numpy as jnp
from jax import lax
from jax.experimental import pallas as pl
from jax.experimental.pallas import tpu as pltpu
from jax.sharding import PartitionSpec as P

F32 = jnp.float32
LANES = 128
PAD = 8
ROWS = 8
BASE = 8
EXT = 24
CROWS = 4
CBASE = 8
CEXT = 20
HALO = 6


def lanes_of(shape):
    return lax.broadcasted_iota(jnp.int32, shape, len(shape) - 1)


def spin(value, shift):
    return pltpu.roll(value, shift % LANES, 1)


def coef_row(i, k_ref, r_ref, coefs, height, zs):
    diag, cx, cy, cz, cw = coefs
    for m in range(height // 8):
        y = PAD + 8 * m
        k = k_ref[i, y : y + 8, :]
        k_next = k_ref[i + 1, y : y + 8, :]
        k_prev = k_ref[i - 1, y : y + 8, :]
        lane = lanes_of(k.shape)
        x_next = 0.5 * (k + k_next)
        x_prev = 0.5 * (k + k_prev)
        y_next = 0.5 * (k + k_ref[i, y + 1 : y + 9, :])
        y_prev = 0.5 * (k + k_ref[i, y - 1 : y + 7, :])
        z_next = jnp.where(lane < LANES - zs, 0.5 * (k + spin(k, -zs)), 0.0)
        z_prev = spin(z_next, zs)
        edge = jnp.where((lane < zs) | (lane >= LANES - zs), 0.5 * k, 0.0)
        total = x_next + x_prev + y_next + y_prev + z_next + z_prev + edge
        diag[i, 8 * m : 8 * m + 8, :] = 1.0 + r_ref[i, y : y + 8, :] - total
        cx[i, 8 * m : 8 * m + 8, :] = jnp.where(jnp.minimum(k, k_next) > 0.0, x_next, 0.0)
        cy[i, y : y + 8, :] = y_next
        cz[i, 8 * m : 8 * m + 8, :] = z_next
        cw[i, 8 * m : 8 * m + 8, :] = z_prev


def build_coefs(k_ref, r_ref, coefs, lo, hi, height, zs):
    diag, cx, cy, cz, cw = coefs
    for m in range(height // 8):
        y = PAD + 8 * m
        k = k_ref[lo - 1, y : y + 8, :]
        k_next = k_ref[lo, y : y + 8, :]
        cx[lo - 1, 8 * m : 8 * m + 8, :] = jnp.where(
            jnp.minimum(k, k_next) > 0.0, 0.5 * (k + k_next), 0.0
        )

    def body(i, carry):
        cy[i, 0:PAD, :] = jnp.zeros((PAD, LANES), F32)
        coef_row(i, k_ref, r_ref, coefs, height, zs)
        return carry

    lax.fori_loop(lo, hi, body, 0)


def advance(src, dst, coefs, r_ref, lo, hi, height, zs, windows, unroll=2):
    diag, cx, cy, cz, cw = coefs

    def body(j, carry):
        for part in range(unroll):
            i = lo + unroll * j + part
            for m in range(height // 8):
                y = PAD + 8 * m
                tile = slice(8 * m, 8 * m + 8)
                a = diag[i, tile, :]
                r = r_ref[i, y : y + 8, :]
                x_next, x_prev = cx[i, tile, :], cx[i - 1, tile, :]
                y_next, y_prev = cy[i, y : y + 8, :], cy[i, y - 1 : y + 7, :]
                z_next, z_prev = cz[i, tile, :], cw[i, tile, :]
                for w in range(windows):
                    u = src[w, i, y : y + 8, :]
                    out = u * (a - r * (u * u))
                    out = out + (x_next * src[w, i + 1, y : y + 8, :] + x_prev * src[w, i - 1, y : y + 8, :])
                    out = out + (y_next * src[w, i, y + 1 : y + 9, :] + y_prev * src[w, i, y - 1 : y + 7, :])
                    out = out + (z_next * spin(u, -zs) + z_prev * spin(u, zs))
                    dst[w, i, y : y + 8, :] = out
        return carry

    lax.fori_loop(0, (hi - lo) // unroll, body, 0)


def clear_pads(ref, lo, hi, height):
    zero = jnp.zeros((PAD, LANES), F32)

    def body(i, carry):
        for lead in range(ref.shape[0]):
            ref[lead, i, 0:PAD, :] = zero
            ref[lead, i, PAD + height : 2 * PAD + height, :] = zero
        return carry

    lax.fori_loop(lo, hi, body, 0)


def clear_pads_flat(ref, lo, hi, height):
    zero = jnp.zeros((PAD, LANES), F32)

    def body(i, carry):
        ref[i, 0:PAD, :] = zero
        ref[i, PAD + height : 2 * PAD + height, :] = zero
        return carry

    lax.fori_loop(lo, hi, body, 0)


def pair_lanes(e):
    even = lanes_of(e.shape) % 2 == 0
    return e + jnp.where(even, spin(e, -1), spin(e, 1))


def coarse_row(load):
    return 0.125 * pair_lanes((load(0, 0) + load(0, 1)) + (load(1, 0) + load(1, 1)))


def pack2(a, b):
    return jnp.where(lanes_of(a.shape) % 2 == 0, a, b)


def unpack_a(v):
    return jnp.where(lanes_of(v.shape) % 2 == 0, v, spin(v, 1))


def unpack_b(v):
    return jnp.where(lanes_of(v.shape) % 2 == 0, spin(v, -1), v)


def odd_here():
    return lax.axis_index("space") % 2


def pack_kernel(states, kappa, rate, send_out, send_in):
    odd = odd_here()
    near_out = 2 * odd
    near_in = 2 - 2 * odd
    for ref, near in ((send_out, near_out), (send_in, near_in)):
        for w in range(2):
            for i in range(HALO):
                ref[HALO * w + i] = states[w, near + i]
        for i in range(ROWS):
            ref[2 * HALO + i] = kappa[i]
            ref[2 * HALO + ROWS + i] = rate[i]


def place_coefs(kappa, rate, got_out, got_in, k_ext, r_ext):
    odd = odd_here()
    at_out = 16 * odd
    at_in = 16 - 16 * odd

    def body(i, carry):
        k_ext[BASE + i, PAD : PAD + 64, :] = kappa[i]
        r_ext[BASE + i, PAD : PAD + 64, :] = rate[i]
        for got, at in ((got_out, at_out), (got_in, at_in)):
            k_ext[at + i, PAD : PAD + 64, :] = got[2 * HALO + i]
            r_ext[at + i, PAD : PAD + 64, :] = got[2 * HALO + ROWS + i]
        return carry

    lax.fori_loop(0, ROWS, body, 0)


def place_states(states, got_out, got_in, field):
    odd = odd_here()
    at_out = 2 + 14 * odd
    at_in = 16 - 14 * odd
    for w in range(2):

        def own(i, carry):
            field[w, BASE + i, PAD : PAD + 64, :] = states[w, i]
            return carry

        def halo(i, carry):
            field[w, at_out + i, PAD : PAD + 64, :] = got_out[HALO * w + i]
            field[w, at_in + i, PAD : PAD + 64, :] = got_in[HALO * w + i]
            return carry

        lax.fori_loop(0, ROWS, own, 0)
        lax.fori_loop(0, HALO, halo, 0)


def lines_of(ref, lead, row):
    return lambda part, first: ref[lead + (row + part, pl.ds(PAD + first, 32, stride=2))]


def first_kernel(states, kappa, rate, got_out, got_in, send, diag, cx, cy, cz, cw, r_ext, k_ext, field, other):
    clear_pads_flat(k_ext, 0, EXT, 64)
    place_coefs(kappa, rate, got_out, got_in, k_ext, r_ext)
    clear_pads(field, 0, EXT, 64)
    clear_pads(other, 0, EXT, 64)
    place_states(states, got_out, got_in, field)
    coefs = (diag, cx, cy, cz, cw)
    build_coefs(k_ext, r_ext, coefs, 1, EXT - 1, 64, 1)
    src, dst = field, other
    for n in range(6):
        reach = 5 - n
        advance(src, dst, coefs, r_ext, BASE - reach, BASE + ROWS + reach, 64, 1, 2)
        src, dst = dst, src
    for w in range(2):
        for i in range(ROWS):
            send[ROWS * w + i] = src[w, BASE + i, PAD : PAD + 64, :]
    for slot, row in enumerate((-2, -1, 4, 5)):
        fine = BASE + 2 * row
        packed = pack2(
            coarse_row(lines_of(k_ext, (), fine)), 4.0 * coarse_row(lines_of(r_ext, (), fine))
        )
        send[16 + slot // 2, 32 * (slot % 2) : 32 * (slot % 2) + 32, :] = packed


def old_kernel(states, got_out, got_in, k_ext, r_ext, old, kc, rc, field, diag, cx, cy, cz, cw, here, there):
    place_states(states, got_out, got_in, field)
    clear_pads_flat(kc, 0, CEXT, 32)
    clear_pads(here, 0, CEXT, 32)
    clear_pads(there, 0, CEXT, 32)

    def row_coefs(i, carry):
        kc[CBASE - 4 + i, PAD : PAD + 32, :] = coarse_row(lines_of(k_ext, (), 2 * i))
        rc[CBASE - 4 + i, PAD : PAD + 32, :] = 4.0 * coarse_row(lines_of(r_ext, (), 2 * i))
        return carry

    lax.fori_loop(0, 12, row_coefs, 0)

    def row_states(i, carry):
        for w in range(2):
            here[w, CBASE - 3 + i, PAD : PAD + 32, :] = coarse_row(lines_of(field, (w,), 2 + 2 * i))
        return carry

    lax.fori_loop(0, 10, row_states, 0)
    coefs = (diag, cx, cy, cz, cw)
    build_coefs(kc, rc, coefs, CBASE - 2, CBASE + CROWS + 2, 32, 2)
    src, dst = here, there
    for n in range(3):
        reach = 2 - n
        advance(src, dst, coefs, rc, CBASE - reach, CBASE + CROWS + reach, 32, 2, 2)
        src, dst = dst, src
    for w in range(2):
        for i in range(CROWS):
            old[w, i] = src[w, CBASE + i, PAD : PAD + 32, :]


def second_kernel(
    sent, got_out, got_in, diag, cx, cy, cz, cw, r_ext, old, fine_end, send, field, other
):
    odd = odd_here()
    clear_pads(field, 0, EXT, 64)
    clear_pads(other, 0, EXT, 64)
    for w in range(2):

        def own(i, carry):
            field[w, BASE + i, PAD : PAD + 64, :] = sent[ROWS * w + i]
            field[w, 16 * odd + i, PAD : PAD + 64, :] = got_out[ROWS * w + i]
            field[w, 16 - 16 * odd + i, PAD : PAD + 64, :] = got_in[ROWS * w + i]
            return carry

        lax.fori_loop(0, ROWS, own, 0)
    coefs = (diag, cx, cy, cz, cw)
    src, dst = field, other
    for n in range(6):
        reach = 7 - n
        advance(src, dst, coefs, r_ext, BASE - reach, BASE + ROWS + reach, 64, 1, 2)
        src, dst = dst, src
    later = (lax.axis_index("tm") > 0).astype(F32)
    for i in range(-1, 5):
        rows = []
        for w in range(2):
            value = coarse_row(lines_of(src, (w,), BASE + 2 * i))
            if 0 <= i < CROWS:
                value = value - (old[w, i] if w else later * old[w, i])
            rows.append(value)
        send[1 + i] = pack2(*rows)
    for w in range(2):
        for i in range(ROWS):
            fine_end[w, i] = src[w, BASE + i, PAD : PAD + 64, :]


def third_kernel(
    sent, got_out, got_in, kc_near, rc_near, sent2, got_out2, got_in2,
    tm_mid, tm_up, tm_down, first, newer, rc, diag, cx, cy, cz, cw, kc, here, there,
):
    odd = odd_here()
    clear_pads_flat(kc, 0, CEXT, 32)
    clear_pads(here, 0, CEXT, 32)
    clear_pads(there, 0, CEXT, 32)

    def near(i, carry):
        kc[i, PAD : PAD + 32, :] = kc_near[i, PAD : PAD + 32, :]
        rc[i, PAD : PAD + 32, :] = rc_near[i, PAD : PAD + 32, :]
        return carry

    lax.fori_loop(CBASE - 4, CBASE + 8, near, 0)
    for got, above in ((got_out2, odd), (got_in2, 1 - odd)):
        for j in range(2):
            packed = got[16 + above, 32 * j : 32 * j + 32, :]
            row = CBASE - 6 + 14 * above + j
            kc[row, PAD : PAD + 32, :] = unpack_a(packed)
            rc[row, PAD : PAD + 32, :] = unpack_b(packed)
    coefs = (diag, cx, cy, cz, cw)
    build_coefs(kc, rc, coefs, CBASE - 5, CBASE + CROWS + 5, 32, 2)

    for i in range(CROWS):
        here[0, CBASE + i, PAD : PAD + 32, :] = unpack_a(sent[1 + i])
        there[1, CBASE + i, PAD : PAD + 32, :] = unpack_b(sent[1 + i])
    for got, above in ((got_out, odd), (got_in, 1 - odd)):
        for j in range(5):
            packed = got[above + j]
            row = CBASE - 5 + 9 * above + j
            here[0, row, PAD : PAD + 32, :] = unpack_a(packed)
            there[1, row, PAD : PAD + 32, :] = unpack_b(packed)
    for i in range(-3, 7):
        first[3 + i] = here[0, CBASE + i, PAD : PAD + 32, :]
    advance(here, there, coefs, rc, CBASE - 4, CBASE + CROWS + 4, 32, 2, 1)
    advance(there, here, coefs, rc, CBASE - 3, CBASE + CROWS + 3, 32, 2, 1)
    advance(here, there, coefs, rc, CBASE - 2, CBASE + CROWS + 2, 32, 2, 1)
    carried = []
    for i in range(-2, 6):
        moved = there[0, CBASE + i, PAD : PAD + 32, :]
        if 0 <= i < CROWS:
            newer[i] = moved
        carried.append(moved + there[1, CBASE + i, PAD : PAD + 32, :])
    for j in range(4):
        tm_mid[j] = pack2(carried[2 * j], carried[2 * j + 1])
    for j in range(2):
        tm_up[j] = pack2(carried[2 * j], carried[2 * j + 1])
        tm_down[j] = pack2(carried[4 + 2 * j], carried[5 + 2 * j])


def last_kernel(
    fine_end, old, first, newer, tm_mid, from_below, from_above, rc, diag, cx, cy, cz, cw, ends, here, there
):
    clear_pads(here, 0, CEXT, 32)
    clear_pads(there, 0, CEXT, 32)
    for ref, start, count in ((from_below, -6, 2), (tm_mid, -2, 4), (from_above, 6, 2)):
        for j in range(count):
            row = CBASE + start + 2 * j
            here[0, row, PAD : PAD + 32, :] = unpack_a(ref[j])
            here[0, row + 1, PAD : PAD + 32, :] = unpack_b(ref[j])
    coefs = (diag, cx, cy, cz, cw)
    advance(here, there, coefs, rc, CBASE - 5, CBASE + CROWS + 5, 32, 2, 1)
    advance(there, here, coefs, rc, CBASE - 4, CBASE + CROWS + 4, 32, 2, 1)
    advance(here, there, coefs, rc, CBASE - 3, CBASE + CROWS + 3, 32, 2, 1)
    second = []
    for i in range(-3, 7):
        moved = there[0, CBASE + i, PAD : PAD + 32, :]
        if 0 <= i < CROWS:
            second.append(moved)
        here[0, CBASE + i, PAD : PAD + 32, :] = first[3 + i] + moved
    advance(here, there, coefs, rc, CBASE - 2, CBASE + CROWS + 2, 32, 2, 1)
    advance(there, here, coefs, rc, CBASE - 1, CBASE + CROWS + 1, 32, 2, 1)
    advance(here, there, coefs, rc, CBASE, CBASE + CROWS, 32, 2, 1)
    later = lax.axis_index("tm") > 0
    for i in range(CROWS):
        third = there[0, CBASE + i, PAD : PAD + 32, :]
        shifts = (
            jnp.where(later, second[i] - old[0, i], 0.0),
            jnp.where(later, third, newer[i]) - old[1, i],
        )
        for w in range(2):
            for part in range(2):
                for line in range(2):
                    lines = pl.ds(line, 32, stride=2)
                    ends[w, 2 * i + part, lines, :] = fine_end[w, 2 * i + part, lines, :] + shifts[w]


def shape(*sizes):
    return jax.ShapeDtypeStruct(sizes, F32)


def call(kernel, outs, scratch, flops, *args):
    return pl.pallas_call(
        kernel,
        out_shape=outs,
        in_specs=[pl.BlockSpec(memory_space=pltpu.VMEM)] * len(args),
        out_specs=[pl.BlockSpec(memory_space=pltpu.VMEM)] * len(outs),
        scratch_shapes=[pltpu.VMEM(sizes, F32) for sizes in scratch],
        compiler_params=pltpu.CompilerParams(vmem_limit_bytes=24 * 1024 * 1024),
        cost_estimate=pl.CostEstimate(flops=flops, bytes_accessed=1 << 20, transcendentals=0),
    )(*args)


def swap(value, odd_pairs):
    count, groups = lax.axis_size("space"), lax.axis_size("tm")
    pairs = []
    for group in range(groups):
        for low in range(1 if odd_pairs else 0, count - 1, 2):
            a, b = group * count + low, group * count + low + 1
            pairs += [(a, b), (b, a)]
    return lax.ppermute(value, ("tm", "space"), pairs)


def over_tm(value, offset):
    count = lax.axis_size("space")
    pairs = [(s, count + s + offset) for s in range(count) if 0 <= s + offset < count]
    return lax.ppermute(value, ("tm", "space"), pairs)


FINE_COEFS = [(EXT, 64, LANES), (EXT, 64, LANES), (EXT, 64 + 2 * PAD, LANES), (EXT, 64, LANES), (EXT, 64, LANES)]
COARSE_COEFS = [(CEXT, 32, LANES), (CEXT, 32, LANES), (CEXT, 32 + 2 * PAD, LANES), (CEXT, 32, LANES), (CEXT, 32, LANES)]
FINE_FIELD = (2, EXT, 64 + 2 * PAD, LANES)
FINE_FLAT = (EXT, 64 + 2 * PAD, LANES)
COARSE_FIELD = (2, CEXT, 32 + 2 * PAD, LANES)
COARSE_FLAT = (CEXT, 32 + 2 * PAD, LANES)


def shards(states, kappa, rate):
    units = 2 * HALO + 2 * ROWS
    send_out, send_in = call(
        pack_kernel, [shape(units, 64, LANES)] * 2, [], 1000, states, kappa, rate
    )
    got_out, got_in = swap(send_out, True), swap(send_in, False)
    send, diag, cx, cy, cz, cw, r_ext, k_ext = call(
        first_kernel,
        [shape(18, 64, LANES)] + [shape(*s) for s in FINE_COEFS] + [shape(*FINE_FLAT)] * 2,
        [FINE_FIELD] * 2,
        10_000_000,
        states, kappa, rate, got_out, got_in,
    )
    got_out2, got_in2 = swap(send, True), swap(send, False)
    old, kc, rc = call(
        old_kernel,
        [shape(2, CROWS, 32, LANES), shape(*COARSE_FLAT), shape(*COARSE_FLAT)],
        [FINE_FIELD] + COARSE_COEFS + [COARSE_FIELD] * 2,
        10_000_000,
        states, got_out, got_in, k_ext, r_ext,
    )
    fine_end, send3 = call(
        second_kernel,
        [shape(2, ROWS, 64, LANES), shape(6, 32, LANES)],
        [FINE_FIELD] * 2,
        10_000_000,
        send, got_out2, got_in2, diag, cx, cy, cz, cw, r_ext, old,
    )
    got_out3, got_in3 = swap(send3, True), swap(send3, False)
    tm_mid, tm_up, tm_down, first, newer, rc2, *coarse = call(
        third_kernel,
        [shape(4, 32, LANES), shape(2, 32, LANES), shape(2, 32, LANES), shape(10, 32, LANES), shape(CROWS, 32, LANES)]
        + [shape(*COARSE_FLAT)] + [shape(*s) for s in COARSE_COEFS],
        [COARSE_FLAT] + [COARSE_FIELD] * 2,
        10_000_000,
        send3, got_out3, got_in3, kc, rc, send, got_out2, got_in2,
    )
    mid, from_below, from_above = over_tm(tm_mid, 0), over_tm(tm_up, 1), over_tm(tm_down, -1)
    (ends,) = call(
        last_kernel,
        [shape(2, ROWS, 64, LANES)],
        [COARSE_FIELD] * 2,
        10_000_000,
        fine_end, old, first, newer, mid, from_below, from_above, rc2, *coarse,
    )
    return ends


def solution(mesh):
    in_specs = (P("tm", "space", None, None), P("space", None, None), P("space", None, None))
    out_specs = P("tm", "space", None, None)
    return jax.shard_map(shards, mesh=mesh, in_specs=in_specs, out_specs=out_specs, check_vma=False)
```

time: 183 us -> 86.3 us (0.47)
  starting transfers between devices: 83 us -> 19.9 us
  waiting for transfers between devices: 65.3 us -> 33.3 us
  Pallas kernels: 0 us -> 29.7 us
  other arithmetic: 20.9 us -> 0 us
  local copies, waits for them, and re-layouts: 8.73 us -> 2.94 us
  matrix products: 2.13 us -> 0 us
    ppermute x27 -> x9, starting transfers between devices: 83 us -> 19.9 us  [the longest x6 16 us: swap(): return lax.ppermute(value, ('tm', 'space'), pairs)]
    ppermute x27 -> x9, waiting for transfers between devices: 65.3 us -> 33.3 us  [the longest x6 24 us: swap(): return lax.ppermute(value, ('tm', 'space'), pairs)]
    pallas_call x0 -> x6, Pallas kernels: none -> 29.7 us  [call(): pl.pallas_call(kernel, out_shape=outs, in_specs=[pl.BlockSpec(memory_spac...]
    mul x24 -> x0, other arithmetic: 12.5 us -> none  [the longest x23 12.3 us: deep_run(): padded = padded * inside[None, :, None, None]]
    slice x23 -> x0, local copies, waits for them, and re-layouts: 5.03 us -> none  [the longest x4 3.48 us: extended_2(): head = lax.slice_in_dim(cells, 0, width, axis=dim)]
    reduce_sum x5 -> x0, other arithmetic: 3.02 us -> none  [restrict(): summed = jnp.sum(blocks, axis=(-4, -2))]
    add x4 -> x0, other arithmetic: 2.45 us -> none  [the longest x1 1.36 us: shards(): return field_now + prolong(newer - old_coarse)]
    dot_general x6 -> x0, matrix products: 2.13 us -> none  [the longest x5 1.93 us: restrict(): jnp.matmul(summed, pair_table(sizes[2]), precision=lax.Precision.HIGHEST)]
  transfers between devices with their start and end apart: 27 -> 9, of which waited for: 9 -> 5; matrix products, arithmetic and copies ran while one was open for 5% -> 0% of each run, Pallas kernels for 0% -> 5%
where the time goes in v1:
time: 86.3 us; the launch traced here: 86 us
  waiting for transfers between devices  33.3 us (39%)
  Pallas kernels  29.7 us (34%)
  starting transfers between devices  19.9 us (23%)
  local copies, waits for them, and re-layouts  2.94 us (3%)
    pallas_call x6, Pallas kernels, call(): pl.pallas_call(kernel, out_shape=outs, in_specs=[pl.BlockSpec(memory_spac...  29.7 us
    ppermute x6, waiting for transfers between devices, swap(): return lax.ppermute(value, ('tm', 'space'), pairs)  24 us
    ppermute x6, starting transfers between devices, swap(): return lax.ppermute(value, ('tm', 'space'), pairs)  16 us
    ppermute x3, waiting for transfers between devices, over_tm(): return lax.ppermute(value, ('tm', 'space'), pairs)  9.37 us
    ppermute x3, starting transfers between devices, over_tm(): return lax.ppermute(value, ('tm', 'space'), pairs)  3.88 us
    unnamed x6, local copies, waits for them, and re-layouts  2.94 us
  transfers between devices with their start and end apart: 9, of which 5 were waited for; matrix products, arithmetic and copies ran while one was open for 0% of the time, Pallas kernels for 5%

profile of v1, /device:TPU:127, one launch (start us, length us, event | category | flops | bytes accessed | tf_op | source)
XLA Modules:
  0.0 86.0 jit_solution(17233914938005079858)
XLA Ops:
  0.0 0.0 copy-start
  0.0 1.0 %copy-done = f32[2,8,64,128]{3,2,1,0:T(8,128)S(1)} copy-done((f32[2,8,64,128]{3,2,1,0:T(8,128)S(1)}, f32[2,8,64,128]{3,2,1,0:T(8,128)}, u32[]{:S(2)}) %copy-start) | copy-done | bytes 524312
  1.0 0.0 copy-start.1
  1.0 0.9 %copy-done.1 = f32[8,64,128]{2,1,0:T(8,128)S(1)} copy-done((f32[8,64,128]{2,1,0:T(8,128)S(1)}, f32[8,64,128]{2,1,0:T(8,128)}, u32[]{:S(2)}) %copy-start.1) | copy-done | bytes 262168
  2.0 0.0 copy-start.2
  2.0 0.9 %copy-done.2 = f32[8,64,128]{2,1,0:T(8,128)S(1)} copy-done((f32[8,64,128]{2,1,0:T(8,128)S(1)}, f32[8,64,128]{2,1,0:T(8,128)}, u32[]{:S(2)}) %copy-start.2) | copy-done | bytes 262168
  2.9 0.1 shard_map.37
  3.1 5.2 %collective-permute-start = (f32[28,64,128]{2,1,0:T(8,128)S(1)}, f32[28,64,128]{2,1,0:T(8,128)S(1)}, u32[]{:S(2)}, u32[]{:S(2)}) collective-permute-start(f32[28,64,128]{2,1,0:T(8,128)S(1)} %get-tuple-element.31), channel_id=1, source_target_pairs={{1,2},{2,1},{3,4},{4,3},{5,6},{6,5},{7,8},{8,7},{9,10},{10,9},{11,... | collective-permute-start | bytes 2752520 | tf_op jit(solution)/shard_map/ppermute | solution.py:396
  8.3 0.1 collective-permute-start.1
  8.4 13.6 %collective-permute-done.got_out = f32[28,64,128]{2,1,0:T(8,128)S(1)} collective-permute-done((f32[28,64,128]{2,1,0:T(8,128)S(1)}, f32[28,64,128]{2,1,0:T(8,128)S(1)}, u32[]{:S(2)}, u32[]{:S(2)}) %collective-permute-start) | collective-permute-done | bytes 917536 | tf_op jit(solution)/shard_map/ppermute | solution.py:396
  22.0 0.0 collective-permute-done.1.got_in
  22.0 9.6 %shard_map.38 = (f32[18,64,128]{2,1,0:T(8,128)S(1)}, f32[24,64,128]{2,1,0:T(8,128)S(1)}, f32[24,64,128]{2,1,0:T(8,128)S(1)}, f32[24,80,128]{2,1,0:T(8,128)S(1)},...) custom-call(f32[2,8,64,128]{3,2,1,0:T(8,128)S(1)} %copy-done, ...), custom_call_target="tpu_custom_call" | custom-call | flops 10000000 | bytes 1048576 | tf_op jit(solution)/shard_map/pallas_call | solution.py:378
  31.6 0.1 collective-permute-start.3
  31.7 5.2 %collective-permute-start.2 = (f32[18,64,128]{2,1,0:T(8,128)S(1)}, f32[18,64,128]{2,1,0:T(8,128)S(1)}, u32[]{:S(2)}, u32[]{:S(2)}) collective-permute-start(f32[18,64,128]{2,1,0:T(8,128)S(1)} %get-tuple-element.33.sent.sent2), channel_id=1, source_target_pairs={{1,2},{2,1},{3,4},{4,3},{5,6},{6,5},{7,8},{8,7},{9,10},{10,9},{11,... | collective-permute-start | bytes 1769480 | tf_op jit(solution)/shard_map/ppermute | solution.py:396
  37.0 4.7 %shard_map.39 = (f32[2,4,32,128]{3,2,1,0:T(8,128)S(1)}, f32[20,48,128]{2,1,0:T(8,128)S(1)}, f32[20,48,128]{2,1,0:T(8,128)S(1)}) custom-call(f32[2,8,64,128]{3,2,1,0:T(8,128)S(1)} %copy-done, f32[28,64,128]{2,1,0:T(8,128)S(1)} %collective-permute-done.got_out, f32[28,64,128]{2,1,0:T(8,128)S(1)} %collective-permute-done.1.got_in, ...), custom_call_target="tpu_custom_call" | custom-call | flops 10000000 | bytes 1048576 | tf_op jit(solution)/shard_map/pallas_call | solution.py:378
  41.6 0.0 collective-permute-done.3.got_in.got_in2
  41.6 5.5 %collective-permute-done.2.got_out.got_out2 = f32[18,64,128]{2,1,0:T(8,128)S(1)} collective-permute-done((f32[18,64,128]{2,1,0:T(8,128)S(1)}, f32[18,64,128]{2,1,0:T(8,128)S(1)}, u32[]{:S(2)}, u32[]{:S(2)}) %collective-permute-start.2) | collective-permute-done | bytes 589856 | tf_op jit(solution)/shard_map/ppermute | solution.py:396
  47.1 7.7 %shard_map.40 = (f32[2,8,64,128]{3,2,1,0:T(8,128)S(1)}, f32[6,32,128]{2,1,0:T(8,128)S(1)}) custom-call(f32[18,64,128]{2,1,0:T(8,128)S(1)} %get-tuple-element.33.sent.sent2, f32[18,64,128]{2,1,0:T(8,128)S(1)} %collective-permute-done.2.got_out.got_out2, f32[18,64,128]{2,1,0:T(8,128)S(1)} %collective-permute-done.3.got_in.got_in2, ...), custom_call_target="tpu_custom_call" | custom-call | flops 10000000 | bytes 1048576 | tf_op jit(solution)/shard_map/pallas_call | solution.py:378
  54.8 0.1 collective-permute-start.5
  54.9 5.2 %collective-permute-start.4 = (f32[6,32,128]{2,1,0:T(8,128)S(1)}, f32[6,32,128]{2,1,0:T(8,128)S(1)}, u32[]{:S(2)}, u32[]{:S(2)}) collective-permute-start(f32[6,32,128]{2,1,0:T(8,128)S(1)} %get-tuple-element.43.sent), channel_id=1, source_target_pairs={{1,2},{2,1},{3,4},{4,3},{5,6},{6,5},{7,8},{8,7},{9,10},{10,9},{11,... | collective-permute-start | bytes 294920 | tf_op jit(solution)/shard_map/ppermute | solution.py:396
  60.2 0.0 collective-permute-done.5.got_in
  60.2 4.9 %collective-permute-done.4.got_out = f32[6,32,128]{2,1,0:T(8,128)S(1)} collective-permute-done((f32[6,32,128]{2,1,0:T(8,128)S(1)}, f32[6,32,128]{2,1,0:T(8,128)S(1)}, u32[]{:S(2)}, u32[]{:S(2)}) %collective-permute-start.4) | collective-permute-done | bytes 98336 | tf_op jit(solution)/shard_map/ppermute | solution.py:396
  65.1 4.0 %shard_map.41 = (f32[4,32,128]{2,1,0:T(8,128)S(1)}, f32[2,32,128]{2,1,0:T(8,128)S(1)}, f32[2,32,128]{2,1,0:T(8,128)S(1)}, f32[10,32,128]{2,1,0:T(8,128)S(1)}, f3...) custom-call(f32[6,32,128]{2,1,0:T(8,128)S(1)} %get-tuple-element.43., ...), custom_call_target="tpu_custom_call" | custom-call | flops 10000000 | bytes 1048576 | tf_op jit(solution)/shard_map/pallas_call | solution.py:378
  69.1 1.3 %collective-permute-start.6 = (f32[4,32,128]{2,1,0:T(8,128)S(1)}, f32[4,32,128]{2,1,0:T(8,128)S(1)}, u32[]{:S(2)}, u32[]{:S(2)}) collective-permute-start(f32[4,32,128]{2,1,0:T(8,128)S(1)} %get-tuple-element.48), channel_id=1, source_target_pairs={{0,128},{1,129},{2,130},{3,131},{4,132},{5,133},{6,134},{7,135},{8... | collective-permute-start | bytes 196616 | tf_op jit(solution)/shard_map/ppermute | solution.py:402
  70.4 1.3 %collective-permute-start.7 = (f32[2,32,128]{2,1,0:T(8,128)S(1)}, f32[2,32,128]{2,1,0:T(8,128)S(1)}, u32[]{:S(2)}, u32[]{:S(2)}) collective-permute-start(f32[2,32,128]{2,1,0:T(8,128)S(1)} %get-tuple-element.49), channel_id=1, source_target_pairs={{0,129},{1,130},{2,131},{3,132},{4,133},{5,134},{6,135},{7,136},{8... | collective-permute-start | bytes 98312 | tf_op jit(solution)/shard_map/ppermute | solution.py:402
  71.7 1.3 %collective-permute-start.8 = (f32[2,32,128]{2,1,0:T(8,128)S(1)}, f32[2,32,128]{2,1,0:T(8,128)S(1)}, u32[]{:S(2)}, u32[]{:S(2)}) collective-permute-start(f32[2,32,128]{2,1,0:T(8,128)S(1)} %get-tuple-element.50), channel_id=1, source_target_pairs={{1,128},{2,129},{3,130},{4,131},{5,132},{6,133},{7,134},{8,135},{9... | collective-permute-start | bytes 98312 | tf_op jit(solution)/shard_map/ppermute | solution.py:402
  73.0 4.1 %collective-permute-done.7.from_below = f32[2,32,128]{2,1,0:T(8,128)S(1)} collective-permute-done((f32[2,32,128]{2,1,0:T(8,128)S(1)}, f32[2,32,128]{2,1,0:T(8,128)S(1)}, u32[]{:S(2)}, u32[]{:S(2)}) %collective-permute-start.7) | collective-permute-done | bytes 32800 | tf_op jit(solution)/shard_map/ppermute | solution.py:402
  77.2 5.2 %collective-permute-done.8.from_above = f32[2,32,128]{2,1,0:T(8,128)S(1)} collective-permute-done((f32[2,32,128]{2,1,0:T(8,128)S(1)}, f32[2,32,128]{2,1,0:T(8,128)S(1)}, u32[]{:S(2)}, u32[]{:S(2)}) %collective-permute-start.8) | collective-permute-done | bytes 32800 | tf_op jit(solution)/shard_map/ppermute | solution.py:402
  82.4 0.0 collective-permute-done.6.tm_mid
  82.4 3.6 %shard_map.42 = f32[2,8,64,128]{3,2,1,0:T(8,128)} custom-call(f32[2,8,64,128]{3,2,1,0:T(8,128)S(1)} %get-tuple-element.42.fine_end, f32[2,4,32,128]{3,2,1,0:T(8,128)S(1)} %get-tuple-element.41.old, f32[10,32,128]{2,1,0:T(8,128)S(1)} %get-tuple-element.46.first, f32[4,32,128]{2,1,0:T(8,128)S(1)} %get-tuple-element.47.newer, ...), custom_call_target="tpu_custom_call" | custom-call | flops 10000000 | bytes 1048576 | tf_op jit(solution)/shard_map/pallas_call | solution.py:378
Async XLA Ops:
  0.0 1.0 %copy-start = (f32[2,8,64,128]{3,2,1,0:T(8,128)S(1)}, f32[2,8,64,128]{3,2,1,0:T(8,128)}, u32[]{:S(2)}) copy-start(f32[2,8,64,128]{3,2,1,0:T(8,128)} %states.5) | copy-start | bytes 1572868
  1.0 0.9 %copy-start.1 = (f32[8,64,128]{2,1,0:T(8,128)S(1)}, f32[8,64,128]{2,1,0:T(8,128)}, u32[]{:S(2)}) copy-start(f32[8,64,128]{2,1,0:T(8,128)} %kappa.3) | copy-start | bytes 786436
  2.0 0.9 %copy-start.2 = (f32[8,64,128]{2,1,0:T(8,128)S(1)}, f32[8,64,128]{2,1,0:T(8,128)}, u32[]{:S(2)}) copy-start(f32[8,64,128]{2,1,0:T(8,128)} %rate.3) | copy-start | bytes 786436
  3.1 18.9 %collective-permute-start = (f32[28,64,128]{2,1,0:T(8,128)S(1)}, f32[28,64,128]{2,1,0:T(8,128)S(1)}, u32[]{:S(2)}, u32[]{:S(2)}) collective-permute-start(f32[28,64,128]{2,1,0:T(8,128)S(1)} %get-tuple-element.31), channel_id=1, source_target_pairs={{1,2},{2,1},{3,4},{4,3},{5,6},{6,5},{7,8},{8,7},{9,10},{10,9},{11,... | collective-permute-start | bytes 2752520 | tf_op jit(solution)/shard_map/ppermute | solution.py:396
  8.3 13.7 %collective-permute-start.1 = (f32[28,64,128]{2,1,0:T(8,128)S(1)}, f32[28,64,128]{2,1,0:T(8,128)S(1)}, u32[]{:S(2)}, u32[]{:S(2)}) collective-permute-start(f32[28,64,128]{2,1,0:T(8,128)S(1)} %get-tuple-element.32), channel_id=1, source_target_pairs={{0,1},{1,0},{2,3},{3,2},{4,5},{5,4},{6,7},{7,6},{8,9},{9,8},{10,11... | collective-permute-start | bytes 2752520 | tf_op jit(solution)/shard_map/ppermute | solution.py:396
  31.6 10.0 %collective-permute-start.3 = (f32[18,64,128]{2,1,0:T(8,128)S(1)}, f32[18,64,128]{2,1,0:T(8,128)S(1)}, u32[]{:S(2)}, u32[]{:S(2)}) collective-permute-start(f32[18,64,128]{2,1,0:T(8,128)S(1)} %get-tuple-element.33.sent.sent2), channel_id=1, source_target_pairs={{0,1},{1,0},{2,3},{3,2},{4,5},{5,4},{6,7},{7,6},{8,9},{9,8},{10,11... | collective-permute-start | bytes 1769480 | tf_op jit(solution)/shard_map/ppermute | solution.py:396
  31.7 15.4 %collective-permute-start.2 = (f32[18,64,128]{2,1,0:T(8,128)S(1)}, f32[18,64,128]{2,1,0:T(8,128)S(1)}, u32[]{:S(2)}, u32[]{:S(2)}) collective-permute-start(f32[18,64,128]{2,1,0:T(8,128)S(1)} %get-tuple-element.33.sent.sent2), channel_id=1, source_target_pairs={{1,2},{2,1},{3,4},{4,3},{5,6},{6,5},{7,8},{8,7},{9,10},{10,9},{11,... | collective-permute-start | bytes 1769480 | tf_op jit(solution)/shard_map/ppermute | solution.py:396
  54.8 5.4 %collective-permute-start.5 = (f32[6,32,128]{2,1,0:T(8,128)S(1)}, f32[6,32,128]{2,1,0:T(8,128)S(1)}, u32[]{:S(2)}, u32[]{:S(2)}) collective-permute-start(f32[6,32,128]{2,1,0:T(8,128)S(1)} %get-tuple-element.43.sent), channel_id=1, source_target_pairs={{0,1},{1,0},{2,3},{3,2},{4,5},{5,4},{6,7},{7,6},{8,9},{9,8},{10,11... | collective-permute-start | bytes 294920 | tf_op jit(solution)/shard_map/ppermute | solution.py:396
  54.9 10.2 %collective-permute-start.4 = (f32[6,32,128]{2,1,0:T(8,128)S(1)}, f32[6,32,128]{2,1,0:T(8,128)S(1)}, u32[]{:S(2)}, u32[]{:S(2)}) collective-permute-start(f32[6,32,128]{2,1,0:T(8,128)S(1)} %get-tuple-element.43.sent), channel_id=1, source_target_pairs={{1,2},{2,1},{3,4},{4,3},{5,6},{6,5},{7,8},{8,7},{9,10},{10,9},{11,... | collective-permute-start | bytes 294920 | tf_op jit(solution)/shard_map/ppermute | solution.py:396
  69.1 13.3 %collective-permute-start.6 = (f32[4,32,128]{2,1,0:T(8,128)S(1)}, f32[4,32,128]{2,1,0:T(8,128)S(1)}, u32[]{:S(2)}, u32[]{:S(2)}) collective-permute-start(f32[4,32,128]{2,1,0:T(8,128)S(1)} %get-tuple-element.48), channel_id=1, source_target_pairs={{0,128},{1,129},{2,130},{3,131},{4,132},{5,133},{6,134},{7,135},{8... | collective-permute-start | bytes 196616 | tf_op jit(solution)/shard_map/ppermute | solution.py:402
  70.4 6.7 %collective-permute-start.7 = (f32[2,32,128]{2,1,0:T(8,128)S(1)}, f32[2,32,128]{2,1,0:T(8,128)S(1)}, u32[]{:S(2)}, u32[]{:S(2)}) collective-permute-start(f32[2,32,128]{2,1,0:T(8,128)S(1)} %get-tuple-element.49), channel_id=1, source_target_pairs={{0,129},{1,130},{2,131},{3,132},{4,133},{5,134},{6,135},{7,136},{8... | collective-permute-start | bytes 98312 | tf_op jit(solution)/shard_map/ppermute | solution.py:402
  71.7 10.7 %collective-permute-start.8 = (f32[2,32,128]{2,1,0:T(8,128)S(1)}, f32[2,32,128]{2,1,0:T(8,128)S(1)}, u32[]{:S(2)}, u32[]{:S(2)}) collective-permute-start(f32[2,32,128]{2,1,0:T(8,128)S(1)} %get-tuple-element.50), channel_id=1, source_target_pairs={{1,128},{2,129},{3,130},{4,131},{5,132},{6,133},{7,134},{8,135},{9... | collective-permute-start | bytes 98312 | tf_op jit(solution)/shard_map/ppermute | solution.py:402

commit v2 on v1

v2 whole, which is shorter than its diff:
```python
import jax
import jax.numpy as jnp
from jax import lax
from jax.experimental import pallas as pl
from jax.experimental.pallas import tpu as pltpu
from jax.sharding import PartitionSpec as P

F32 = jnp.float32
LANES = 128
PAD = 8
ROWS = 8
BASE = 8
EXT = 24
CROWS = 4
CBASE = 8
CEXT = 20
HALO = 6


def lanes_of(shape):
    return lax.broadcasted_iota(jnp.int32, shape, len(shape) - 1)


def spin(value, shift):
    return pltpu.roll(value, shift % LANES, 1)


def coef_tile(i, m, k_ref, r_ref, coefs, zs):
    diag, cx, cy, cz, cw = coefs
    y = PAD + 8 * m
    k = k_ref[i, y : y + 8, :]
    k_next = k_ref[i + 1, y : y + 8, :]
    k_prev = k_ref[i - 1, y : y + 8, :]
    lane = lanes_of(k.shape)
    x_next = 0.5 * (k + k_next)
    x_prev = 0.5 * (k + k_prev)
    y_next = 0.5 * (k + k_ref[i, y + 1 : y + 9, :])
    y_prev = 0.5 * (k + k_ref[i, y - 1 : y + 7, :])
    z_next = jnp.where(lane < LANES - zs, 0.5 * (k + spin(k, -zs)), 0.0)
    z_prev = jnp.where(lane >= zs, 0.5 * (k + spin(k, zs)), 0.0)
    edge = jnp.where((lane < zs) | (lane >= LANES - zs), 0.5 * k, 0.0)
    total = x_next + x_prev + y_next + y_prev + z_next + z_prev + edge
    diag[i, 8 * m : 8 * m + 8, :] = 1.0 + r_ref[i, y : y + 8, :] - total
    cx[i, 8 * m : 8 * m + 8, :] = jnp.where(jnp.minimum(k, k_next) > 0.0, x_next, 0.0)
    cy[i, y : y + 8, :] = y_next
    cz[i, 8 * m : 8 * m + 8, :] = z_next
    cw[i, 8 * m : 8 * m + 8, :] = z_prev


def blocks(count, unroll, block):
    if count <= unroll:
        block(0, count)
        return
    trips = -(-count // unroll)
    rows = -(-count // trips)
    whole = count // rows

    def body(j, carry):
        block(j * rows, rows)
        return carry

    lax.fori_loop(0, whole, body, 0)
    if count - whole * rows:
        block(whole * rows, count - whole * rows)


def build_coefs(k_ref, r_ref, coefs, lo, count, height, zs):
    _, cx, cy, _, _ = coefs
    for m in range(height // 8):
        y = PAD + 8 * m
        k = k_ref[lo - 1, y : y + 8, :]
        k_next = k_ref[lo, y : y + 8, :]
        cx[lo - 1, 8 * m : 8 * m + 8, :] = jnp.where(
            jnp.minimum(k, k_next) > 0.0, 0.5 * (k + k_next), 0.0
        )

    def block(first, rows):
        for i in range(rows):
            cy[lo + first + i, 0:PAD, :] = jnp.zeros((PAD, LANES), F32)
            for m in range(height // 8):
                coef_tile(lo + first + i, m, k_ref, r_ref, coefs, zs)

    blocks(count, 8 if height == 64 else 14, block)


def advance(src, dst, coefs, r_ref, lo, count, height, zs, windows, unroll=8):
    diag, cx, cy, cz, cw = coefs

    def block(first, rows):
        base = lo + first
        for m in range(height // 8):
            y = PAD + 8 * m
            here = slice(y, y + 8)
            tile = slice(8 * m, 8 * m + 8)
            line = [[src[w, base + i, here, :] for i in range(-1, rows + 1)] for w in range(windows)]
            across = [cx[base + i, tile, :] for i in range(-1, rows)]
            for i in range(rows):
                row = base + i
                a = diag[row, tile, :]
                r = r_ref[row, here, :]
                y_next, y_prev = cy[row, here, :], cy[row, y - 1 : y + 7, :]
                z_next, z_prev = cz[row, tile, :], cw[row, tile, :]
                for w in range(windows):
                    u = line[w][i + 1]
                    out = u * (a - r * (u * u))
                    out = out + (across[i + 1] * line[w][i + 2] + across[i] * line[w][i])
                    out = out + (y_next * src[w, row, y + 1 : y + 9, :] + y_prev * src[w, row, y - 1 : y + 7, :])
                    out = out + (z_next * spin(u, -zs) + z_prev * spin(u, zs))
                    dst[w, row, here, :] = out

    blocks(count, unroll, block)


def clear_pads(ref, lo, hi, height):
    zero = jnp.zeros((PAD, LANES), F32)

    def body(i, carry):
        for lead in range(ref.shape[0]):
            ref[lead, i, 0:PAD, :] = zero
            ref[lead, i, PAD + height : 2 * PAD + height, :] = zero
        return carry

    lax.fori_loop(lo, hi, body, 0)


def clear_pads_flat(ref, lo, hi, height):
    zero = jnp.zeros((PAD, LANES), F32)

    def body(i, carry):
        ref[i, 0:PAD, :] = zero
        ref[i, PAD + height : 2 * PAD + height, :] = zero
        return carry

    lax.fori_loop(lo, hi, body, 0)


def pair_lanes(e):
    even = lanes_of(e.shape) % 2 == 0
    return e + jnp.where(even, spin(e, -1), spin(e, 1))


def coarse_row(load):
    return 0.125 * pair_lanes((load(0, 0) + load(0, 1)) + (load(1, 0) + load(1, 1)))


def pack2(a, b):
    return jnp.where(lanes_of(a.shape) % 2 == 0, a, b)


def unpack_a(v):
    return jnp.where(lanes_of(v.shape) % 2 == 0, v, spin(v, 1))


def unpack_b(v):
    return jnp.where(lanes_of(v.shape) % 2 == 0, spin(v, -1), v)


def odd_here():
    return lax.axis_index("space") % 2


def pack_kernel(states, kappa, rate, send_out, send_in):
    odd = odd_here()
    for ref, near in ((send_out, 2 * odd), (send_in, 2 - 2 * odd)):
        for w in range(2):
            for i in range(HALO):
                ref[HALO * w + i] = states[w, near + i]
        for i in range(ROWS):
            ref[2 * HALO + i] = kappa[i]
            ref[2 * HALO + ROWS + i] = rate[i]


def place_halo(got, field, k_ext, r_ext, above):
    for w in range(2):

        def halo(i, carry):
            field[w, 2 + 14 * above + i, PAD : PAD + 64, :] = got[HALO * w + i]
            return carry

        lax.fori_loop(0, HALO, halo, 0)

    def coef(i, carry):
        k_ext[16 * above + i, PAD : PAD + 64, :] = got[2 * HALO + i]
        r_ext[16 * above + i, PAD : PAD + 64, :] = got[2 * HALO + ROWS + i]
        return carry

    lax.fori_loop(0, ROWS, coef, 0)


def place_own(states, field):
    def own(i, carry):
        for w in range(2):
            field[w, BASE + i, PAD : PAD + 64, :] = states[w, i]
        return carry

    lax.fori_loop(0, ROWS, own, 0)


def lines_of(ref, lead, row):
    return lambda part, first: ref[lead + (row + part, pl.ds(PAD + first, 32, stride=2))]


def inner_first_kernel(states, kappa, rate, got_in, field, other, diag, cx, cy, cz, cw, r_ext, k_ext):
    odd = odd_here()
    clear_pads_flat(k_ext, 0, EXT, 64)
    clear_pads(field, 0, EXT, 64)
    clear_pads(other, 0, EXT, 64)
    place_own(states, field)

    def own(i, carry):
        k_ext[BASE + i, PAD : PAD + 64, :] = kappa[i]
        r_ext[BASE + i, PAD : PAD + 64, :] = rate[i]
        return carry

    lax.fori_loop(0, ROWS, own, 0)
    place_halo(got_in, field, k_ext, r_ext, 1 - odd)
    coefs = (diag, cx, cy, cz, cw)
    build_coefs(k_ext, r_ext, coefs, 9 - 8 * odd, 14, 64, 1)
    src, dst = field, other
    for n in range(1, 7):
        advance(src, dst, coefs, r_ext, BASE + n - 6 * odd, 14 - 2 * n, 64, 1, 2)
        src, dst = dst, src


def outer_first_kernel(got_out, *refs):
    refs = refs[9:]
    send, field, other, diag, cx, cy, cz, cw, r_ext, k_ext = refs
    odd = odd_here()
    place_halo(got_out, field, k_ext, r_ext, odd)
    coefs = (diag, cx, cy, cz, cw)
    build_coefs(k_ext, r_ext, coefs, 1 + 14 * odd, 8, 64, 1)
    src, dst = field, other
    for n in range(1, 7):
        advance(src, dst, coefs, r_ext, 2 + n + (14 - 2 * n) * odd, 6, 64, 1, 2)
        src, dst = dst, src

    def own(i, carry):
        for w in range(2):
            send[ROWS * w + i] = src[w, BASE + i, PAD : PAD + 64, :]
        return carry

    lax.fori_loop(0, ROWS, own, 0)
    for slot, row in enumerate((-2, -1, 4, 5)):
        fine = BASE + 2 * row
        packed = pack2(
            coarse_row(lines_of(k_ext, (), fine)), 4.0 * coarse_row(lines_of(r_ext, (), fine))
        )
        send[16 + slot // 2, 32 * (slot % 2) : 32 * (slot % 2) + 32, :] = packed


def inner_second_kernel(got_in, *refs):
    _, _, diag, cx, cy, cz, cw, r_ext, field, other = refs
    odd = odd_here()

    def halo(i, carry):
        for w in range(2):
            field[w, 16 - 16 * odd + i, PAD : PAD + 64, :] = got_in[ROWS * w + i]
        return carry

    lax.fori_loop(0, ROWS, halo, 0)
    coefs = (diag, cx, cy, cz, cw)
    src, dst = field, other
    for n in range(1, 7):
        advance(src, dst, coefs, r_ext, BASE + n - 8 * odd, 16 - 2 * n, 64, 1, 2)
        src, dst = dst, src


def outer_second_kernel(got_out, *refs):
    _, _, diag, cx, cy, cz, cw, r_ext, old, field, other, send = refs
    odd = odd_here()

    def halo(i, carry):
        for w in range(2):
            field[w, 16 * odd + i, PAD : PAD + 64, :] = got_out[ROWS * w + i]
        return carry

    lax.fori_loop(0, ROWS, halo, 0)
    coefs = (diag, cx, cy, cz, cw)
    src, dst = field, other
    for n in range(1, 7):
        advance(src, dst, coefs, r_ext, n + (16 - 2 * n) * odd, 8, 64, 1, 2)
        src, dst = dst, src
    later = (lax.axis_index("tm") > 0).astype(F32)
    for i in range(-1, 5):
        rows = []
        for w in range(2):
            value = coarse_row(lines_of(src, (w,), BASE + 2 * i))
            if 0 <= i < CROWS:
                value = value - (old[w, i] if w else later * old[w, i])
            rows.append(value)
        send[1 + i] = pack2(*rows)


def old_kernel(states, got_out, got_in, k_ext, r_ext, old, kc, rc, field, diag, cx, cy, cz, cw, here, there):
    odd = odd_here()
    place_own(states, field)
    for got, above in ((got_out, odd), (got_in, 1 - odd)):
        for w in range(2):

            def halo(i, carry):
                field[w, 2 + 14 * above + i, PAD : PAD + 64, :] = got[HALO * w + i]
                return carry

            lax.fori_loop(0, HALO, halo, 0)
    clear_pads_flat(kc, 0, CEXT, 32)
    clear_pads(here, 0, CEXT, 32)
    clear_pads(there, 0, CEXT, 32)

    def row_coefs(first, rows):
        for i in range(rows):
            at = first + i
            kc[CBASE - 4 + at, PAD : PAD + 32, :] = coarse_row(lines_of(k_ext, (), 2 * at))
            rc[CBASE - 4 + at, PAD : PAD + 32, :] = 4.0 * coarse_row(lines_of(r_ext, (), 2 * at))

    blocks(12, 6, row_coefs)

    def row_states(first, rows):
        for i in range(rows):
            for w in range(2):
                value = coarse_row(lines_of(field, (w,), 2 + 2 * (first + i)))
                here[w, CBASE - 3 + first + i, PAD : PAD + 32, :] = value

    blocks(10, 5, row_states)
    coefs = (diag, cx, cy, cz, cw)
    build_coefs(kc, rc, coefs, CBASE - 2, CROWS + 4, 32, 2)
    src, dst = here, there
    for n in range(3):
        reach = 2 - n
        advance(src, dst, coefs, rc, CBASE - reach, CROWS + 2 * reach, 32, 2, 2)
        src, dst = dst, src
    for w in range(2):
        for i in range(CROWS):
            old[w, i] = src[w, CBASE + i, PAD : PAD + 32, :]


def chain_coefs_kernel(kc_near, rc_near, sent2, got_out2, got_in2, rc, diag, cx, cy, cz, cw, kc):
    odd = odd_here()
    clear_pads_flat(kc, 0, CEXT, 32)

    def near(i, carry):
        kc[i, PAD : PAD + 32, :] = kc_near[i, PAD : PAD + 32, :]
        rc[i, PAD : PAD + 32, :] = rc_near[i, PAD : PAD + 32, :]
        return carry

    lax.fori_loop(CBASE - 4, CBASE + 8, near, 0)
    for got, above in ((got_out2, odd), (got_in2, 1 - odd)):
        for j in range(2):
            packed = got[16 + above, 32 * j : 32 * j + 32, :]
            row = CBASE - 6 + 14 * above + j
            kc[row, PAD : PAD + 32, :] = unpack_a(packed)
            rc[row, PAD : PAD + 32, :] = unpack_b(packed)
    build_coefs(kc, rc, (diag, cx, cy, cz, cw), CBASE - 5, CROWS + 10, 32, 2)


def third_kernel(
    sent, got_out, got_in, rc, diag, cx, cy, cz, cw,
    tm_mid, tm_up, tm_down, first, newer, here, there,
):
    odd = odd_here()
    clear_pads(here, 0, CEXT, 32)
    clear_pads(there, 0, CEXT, 32)
    coefs = (diag, cx, cy, cz, cw)
    for i in range(CROWS):
        here[0, CBASE + i, PAD : PAD + 32, :] = unpack_a(sent[1 + i])
        there[1, CBASE + i, PAD : PAD + 32, :] = unpack_b(sent[1 + i])
    for got, above in ((got_out, odd), (got_in, 1 - odd)):
        for j in range(5):
            packed = got[above + j]
            row = CBASE - 5 + 9 * above + j
            here[0, row, PAD : PAD + 32, :] = unpack_a(packed)
            there[1, row, PAD : PAD + 32, :] = unpack_b(packed)
    for i in range(-3, 7):
        first[3 + i] = here[0, CBASE + i, PAD : PAD + 32, :]
    advance(here, there, coefs, rc, CBASE - 4, CROWS + 8, 32, 2, 1, 14)
    advance(there, here, coefs, rc, CBASE - 3, CROWS + 6, 32, 2, 1, 14)
    advance(here, there, coefs, rc, CBASE - 2, CROWS + 4, 32, 2, 1, 14)
    carried = []
    for i in range(-2, 6):
        moved = there[0, CBASE + i, PAD : PAD + 32, :]
        if 0 <= i < CROWS:
            newer[i] = moved
        carried.append(moved + there[1, CBASE + i, PAD : PAD + 32, :])
    for j in range(4):
        tm_mid[j] = pack2(carried[2 * j], carried[2 * j + 1])
    for j in range(2):
        tm_up[j] = pack2(carried[2 * j], carried[2 * j + 1])
        tm_down[j] = pack2(carried[4 + 2 * j], carried[5 + 2 * j])


def last_kernel(
    fine, old, first, newer, tm_mid, from_below, from_above, rc, diag, cx, cy, cz, cw, ends, here, there
):
    clear_pads(here, 0, CEXT, 32)
    clear_pads(there, 0, CEXT, 32)
    for ref, start, count in ((from_below, -6, 2), (tm_mid, -2, 4), (from_above, 6, 2)):
        for j in range(count):
            row = CBASE + start + 2 * j
            here[0, row, PAD : PAD + 32, :] = unpack_a(ref[j])
            here[0, row + 1, PAD : PAD + 32, :] = unpack_b(ref[j])
    coefs = (diag, cx, cy, cz, cw)
    advance(here, there, coefs, rc, CBASE - 5, CROWS + 10, 32, 2, 1, 14)
    advance(there, here, coefs, rc, CBASE - 4, CROWS + 8, 32, 2, 1, 14)
    advance(here, there, coefs, rc, CBASE - 3, CROWS + 6, 32, 2, 1, 14)
    second = []
    for i in range(-3, 7):
        moved = there[0, CBASE + i, PAD : PAD + 32, :]
        if 0 <= i < CROWS:
            second.append(moved)
        here[0, CBASE + i, PAD : PAD + 32, :] = first[3 + i] + moved
    advance(here, there, coefs, rc, CBASE - 2, CROWS + 4, 32, 2, 1, 14)
    advance(there, here, coefs, rc, CBASE - 1, CROWS + 2, 32, 2, 1, 14)
    advance(here, there, coefs, rc, CBASE, CROWS, 32, 2, 1, 14)
    later = lax.axis_index("tm") > 0
    for i in range(CROWS):
        third = there[0, CBASE + i, PAD : PAD + 32, :]
        shifts = (
            jnp.where(later, second[i] - old[0, i], 0.0),
            jnp.where(later, third, newer[i]) - old[1, i],
        )
        for w in range(2):
            for part in range(2):
                for line in range(2):
                    value = fine[w, BASE + 2 * i + part, pl.ds(PAD + line, 32, stride=2), :]
                    ends[w, 2 * i + part, pl.ds(line, 32, stride=2), :] = value + shifts[w]


def shape(*sizes):
    return jax.ShapeDtypeStruct(sizes, F32)


def call(kernel, outs, scratch, cost, *args, aliases=None):
    return pl.pallas_call(
        kernel,
        out_shape=outs,
        in_specs=[pl.BlockSpec(memory_space=pltpu.VMEM)] * len(args),
        out_specs=[pl.BlockSpec(memory_space=pltpu.VMEM)] * len(outs),
        scratch_shapes=[pltpu.VMEM(sizes, F32) for sizes in scratch],
        input_output_aliases=aliases or {},
        compiler_params=pltpu.CompilerParams(vmem_limit_bytes=24 * 1024 * 1024),
        cost_estimate=pl.CostEstimate(flops=cost, bytes_accessed=1 << 20, transcendentals=0),
    )(*args)


def swap(value, odd_pairs):
    count, groups = lax.axis_size("space"), lax.axis_size("tm")
    pairs = []
    for group in range(groups):
        for low in range(1 if odd_pairs else 0, count - 1, 2):
            a, b = group * count + low, group * count + low + 1
            pairs += [(a, b), (b, a)]
    return lax.ppermute(value, ("tm", "space"), pairs)


def over_tm(value, offset):
    count = lax.axis_size("space")
    pairs = [(s, count + s + offset) for s in range(count) if 0 <= s + offset < count]
    return lax.ppermute(value, ("tm", "space"), pairs)


FINE_COEFS = [(EXT, 64, LANES), (EXT, 64, LANES), (EXT, 64 + 2 * PAD, LANES), (EXT, 64, LANES), (EXT, 64, LANES)]
COARSE_COEFS = [(CEXT, 32, LANES), (CEXT, 32, LANES), (CEXT, 32 + 2 * PAD, LANES), (CEXT, 32, LANES), (CEXT, 32, LANES)]
FINE_FIELD = (2, EXT, 64 + 2 * PAD, LANES)
FINE_FLAT = (EXT, 64 + 2 * PAD, LANES)
COARSE_FIELD = (2, CEXT, 32 + 2 * PAD, LANES)
COARSE_FLAT = (CEXT, 32 + 2 * PAD, LANES)


def swaps(value_out, value_in):
    got_out = swap(value_out, True)
    got_in = swap(value_in, False)
    return got_out, got_in


COST = 10_000_000


def shards(states, kappa, rate):
    units = 2 * HALO + 2 * ROWS
    fields = [shape(*FINE_FIELD)] * 2
    fine_coefs = [shape(*sizes) for sizes in FINE_COEFS]
    coarse_coefs = [shape(*sizes) for sizes in COARSE_COEFS]
    send_out, send_in = call(
        pack_kernel, [shape(units, 64, LANES)] * 2, [], 1000, states, kappa, rate
    )
    got_out, got_in = swaps(send_out, send_in)
    work = call(
        inner_first_kernel,
        fields + fine_coefs + [shape(*FINE_FLAT)] * 2,
        [], COST, states, kappa, rate, got_in,
    )
    send, *work = call(
        outer_first_kernel,
        [shape(18, 64, LANES)] + fields + fine_coefs + [shape(*FINE_FLAT)] * 2,
        [], COST, got_out, *work, aliases={1 + n: 1 + n for n in range(9)},
    )
    field, other, *coefs, r_ext, k_ext = work
    got_out2, got_in2 = swaps(send, send)
    old, kc, rc = call(
        old_kernel,
        [shape(2, CROWS, 32, LANES), shape(*COARSE_FLAT), shape(*COARSE_FLAT)],
        [FINE_FIELD] + COARSE_COEFS + [COARSE_FIELD] * 2,
        COST, states, got_out, got_in, k_ext, r_ext,
    )
    field, other = call(
        inner_second_kernel, fields, [], COST, got_in2, field, other, *coefs, r_ext,
        aliases={1: 0, 2: 1},
    )
    field, other, send3 = call(
        outer_second_kernel,
        fields + [shape(6, 32, LANES)],
        [], COST, got_out2, field, other, *coefs, r_ext, old, aliases={1: 0, 2: 1},
    )
    got_out3, got_in3 = swaps(send3, send3)
    rc2, *coarse = call(
        chain_coefs_kernel, [shape(*COARSE_FLAT)] + coarse_coefs, [COARSE_FLAT],
        COST, kc, rc, send, got_out2, got_in2,
    )
    tm_mid, tm_up, tm_down, first, newer = call(
        third_kernel,
        [shape(4, 32, LANES), shape(2, 32, LANES), shape(2, 32, LANES), shape(10, 32, LANES), shape(CROWS, 32, LANES)],
        [COARSE_FIELD] * 2,
        COST, send3, got_out3, got_in3, rc2, *coarse,
    )
    mid, from_below, from_above = over_tm(tm_mid, 0), over_tm(tm_up, 1), over_tm(tm_down, -1)
    (ends,) = call(
        last_kernel,
        [shape(2, ROWS, 64, LANES)],
        [COARSE_FIELD] * 2,
        COST, field, old, first, newer, mid, from_below, from_above, rc2, *coarse,
    )
    return ends


def solution(mesh):
    in_specs = (P("tm", "space", None, None), P("space", None, None), P("space", None, None))
    out_specs = P("tm", "space", None, None)
    return jax.shard_map(shards, mesh=mesh, in_specs=in_specs, out_specs=out_specs, check_vma=False)
```

time: 86.3 us -> 69.3 us (0.80)
  Pallas kernels: 29.7 us -> 15.6 us
  waiting for transfers between devices: 33.3 us -> 31.7 us
  starting transfers between devices: 19.9 us -> 18.6 us
    pallas_call x6 -> x9, Pallas kernels: 29.7 us -> 15.6 us  [call(): pl.pallas_call(kernel, out_shape=outs, in_specs=[pl.BlockSpec(memory_spac...]
    ppermute x6, waiting for transfers between devices: 24 us -> 22.3 us  [swap(): return lax.ppermute(value, ('tm', 'space'), pairs)]
    ppermute x6, starting transfers between devices: 16 us -> 14.7 us  [swap(): return lax.ppermute(value, ('tm', 'space'), pairs)]
  transfers between devices with their start and end apart: 9 -> 9, of which waited for: 5 -> 5; matrix products, arithmetic and copies ran while one was open for 0% -> 0% of each run, Pallas kernels for 5% -> 12%
where the time goes in v2:
time: 69.3 us; the launch traced here: 68.9 us
  waiting for transfers between devices  31.7 us (46%)
  starting transfers between devices  18.6 us (27%)
  Pallas kernels  15.6 us (23%)
  local copies, waits for them, and re-layouts  2.94 us (4%)
    ppermute x6, waiting for transfers between devices, swap(): return lax.ppermute(value, ('tm', 'space'), pairs)  22.3 us
    pallas_call x9, Pallas kernels, call(): pl.pallas_call(kernel, out_shape=outs, in_specs=[pl.BlockSpec(memory_spac...  15.6 us
    ppermute x6, starting transfers between devices, swap(): return lax.ppermute(value, ('tm', 'space'), pairs)  14.7 us
    ppermute x3, waiting for transfers between devices, over_tm(): return lax.ppermute(value, ('tm', 'space'), pairs)  9.37 us
    ppermute x3, starting transfers between devices, over_tm(): return lax.ppermute(value, ('tm', 'space'), pairs)  3.88 us
    unnamed x6, local copies, waits for them, and re-layouts  2.94 us
  transfers between devices with their start and end apart: 9, of which 5 were waited for; matrix products, arithmetic and copies ran while one was open for 0% of the time, Pallas kernels for 12%

profile of v2, /device:TPU:127, one launch (start us, length us, event | category | flops | bytes accessed | tf_op | source)
XLA Modules:
  0.0 68.9 jit_solution(6910792835645637791)
XLA Ops:
  0.0 1.0 %copy-done = f32[2,8,64,128]{3,2,1,0:T(8,128)S(1)} copy-done((f32[2,8,64,128]{3,2,1,0:T(8,128)S(1)}, f32[2,8,64,128]{3,2,1,0:T(8,128)}, u32[]{:S(2)}) %copy-start) | copy-done | bytes 524312
  1.0 0.0 copy-start.1
  1.0 0.9 %copy-done.1 = f32[8,64,128]{2,1,0:T(8,128)S(1)} copy-done((f32[8,64,128]{2,1,0:T(8,128)S(1)}, f32[8,64,128]{2,1,0:T(8,128)}, u32[]{:S(2)}) %copy-start.1) | copy-done | bytes 262168
  2.0 0.0 copy-start.2
  2.0 0.9 %copy-done.2 = f32[8,64,128]{2,1,0:T(8,128)S(1)} copy-done((f32[8,64,128]{2,1,0:T(8,128)S(1)}, f32[8,64,128]{2,1,0:T(8,128)}, u32[]{:S(2)}) %copy-start.2) | copy-done | bytes 262168
  2.9 0.1 shard_map.37
  3.1 0.8 %collective-permute-start.1 = (f32[28,64,128]{2,1,0:T(8,128)S(1)}, f32[28,64,128]{2,1,0:T(8,128)S(1)}, u32[]{:S(2)}, u32[]{:S(2)}) collective-permute-start(f32[28,64,128]{2,1,0:T(8,128)S(1)} %get-tuple-element.45), channel_id=1, source_target_pairs={{0,1},{1,0},{2,3},{3,2},{4,5},{5,4},{6,7},{7,6},{8,9},{9,8},{10,11... | collective-permute-start | bytes 2752520 | tf_op jit(solution)/shard_map/ppermute | solution.py:451
  3.8 4.6 %collective-permute-start = (f32[28,64,128]{2,1,0:T(8,128)S(1)}, f32[28,64,128]{2,1,0:T(8,128)S(1)}, u32[]{:S(2)}, u32[]{:S(2)}) collective-permute-start(f32[28,64,128]{2,1,0:T(8,128)S(1)} %get-tuple-element.44), channel_id=1, source_target_pairs={{1,2},{2,1},{3,4},{4,3},{5,6},{6,5},{7,8},{8,7},{9,10},{10,9},{11,... | collective-permute-start | bytes 2752520 | tf_op jit(solution)/shard_map/ppermute | solution.py:451
  8.4 0.0 collective-permute-done.1.got_in
  8.4 3.4 %shard_map.38 = (f32[2,24,80,128]{3,2,1,0:T(8,128)S(1)}, f32[2,24,80,128]{3,2,1,0:T(8,128)S(1)}, f32[24,64,128]{2,1,0:T(8,128)S(1)}, f32[24,64,128]{2,1,0:T(8,12...) custom-call(f32[2,8,64,128]{3,2,1,0:T(8,128)S(1)} %copy-done, ...), custom_call_target="tpu_custom_call" | custom-call | flops 10000000 | bytes 1048576 | tf_op jit(solution)/shard_map/pallas_call | solution.py:432
  11.8 10.9 %collective-permute-done.got_out = f32[28,64,128]{2,1,0:T(8,128)S(1)} collective-permute-done((f32[28,64,128]{2,1,0:T(8,128)S(1)}, f32[28,64,128]{2,1,0:T(8,128)S(1)}, u32[]{:S(2)}, u32[]{:S(2)}) %collective-permute-start) | collective-permute-done | bytes 917536 | tf_op jit(solution)/shard_map/ppermute | solution.py:451
  22.7 2.3 %shard_map.39 = (f32[18,64,128]{2,1,0:T(8,128)S(1)}, f32[2,24,80,128]{3,2,1,0:T(8,128)S(1)}, f32[2,24,80,128]{3,2,1,0:T(8,128)S(1)}, f32[24,64,128]{2,1,0:T(8,12...) custom-call(f32[28,64,128]{2,1,0:T(8,128)S(1)} %collective-permute-d, ...), custom_call_target="tpu_custom_call", output_to_operand_aliasing={{1}: (1, {}), {2}: (2, {}), {3}: (3, {}), {4}: (4, {}), {5}... | custom-call | flops 10000000 | bytes 1048576 | tf_op jit(solution)/shard_map/pallas_call | solution.py:432
  25.1 0.1 collective-permute-start.3
  25.2 4.6 %collective-permute-start.2 = (f32[18,64,128]{2,1,0:T(8,128)S(1)}, f32[18,64,128]{2,1,0:T(8,128)S(1)}, u32[]{:S(2)}, u32[]{:S(2)}) collective-permute-start(f32[18,64,128]{2,1,0:T(8,128)S(1)} %get-tuple-element.55.sent2), channel_id=1, source_target_pairs={{1,2},{2,1},{3,4},{4,3},{5,6},{6,5},{7,8},{8,7},{9,10},{10,9},{11,... | collective-permute-start | bytes 1769480 | tf_op jit(solution)/shard_map/ppermute | solution.py:451
  29.8 1.7 %shard_map.41 = (f32[2,4,32,128]{3,2,1,0:T(8,128)S(1)}, f32[20,48,128]{2,1,0:T(8,128)S(1)}, f32[20,48,128]{2,1,0:T(8,128)S(1)}) custom-call(f32[2,8,64,128]{3,2,1,0:T(8,128)S(1)} %copy-done, f32[28,64,128]{2,1,0:T(8,128)S(1)} %collective-permute-done.got_out, f32[28,64,128]{2,1,0:T(8,128)S(1)} %collective-permute-done.1.got_in, ...), custom_call_target="tpu_custom_call" | custom-call | flops 10000000 | bytes 1048576 | tf_op jit(solution)/shard_map/pallas_call | solution.py:432
  31.5 0.0 collective-permute-done.3.got_in.got_in2
  31.5 2.8 %shard_map.40 = (f32[2,24,80,128]{3,2,1,0:T(8,128)S(1)}, f32[2,24,80,128]{3,2,1,0:T(8,128)S(1)}) custom-call(f32[18,64,128]{2,1,0:T(8,128)S(1)} %collective-permute-done.3.got_in.got_in2, f32[2,24,80,128]{3,2,1,0:T(8,128)S(1)} %get-tuple-element.56.refs_0_, ...), custom_call_target="tpu_custom_call", output_to_operand_aliasing={{0}: (1, {}), {1}: (2, {})} | custom-call | flops 10000000 | bytes 1048576 | tf_op jit(solution)/shard_map/pallas_call | solution.py:432
  34.3 6.3 %collective-permute-done.2.got_out.got_out2 = f32[18,64,128]{2,1,0:T(8,128)S(1)} collective-permute-done((f32[18,64,128]{2,1,0:T(8,128)S(1)}, f32[18,64,128]{2,1,0:T(8,128)S(1)}, u32[]{:S(2)}, u32[]{:S(2)}) %collective-permute-start.2) | collective-permute-done | bytes 589856 | tf_op jit(solution)/shard_map/ppermute | solution.py:451
  40.6 2.3 %shard_map.42 = (f32[2,24,80,128]{3,2,1,0:T(8,128)S(1)}, f32[2,24,80,128]{3,2,1,0:T(8,128)S(1)}, f32[6,32,128]{2,1,0:T(8,128)S(1)}) custom-call(f32[18,64,128]{2,1,0:T(8,128)S(1)} %collective-permute-done.2.got_out.got_out2, f32[2,24,80,128]{3,2,1,0:T(8,128)S(1)} %get-tuple-element.64.refs_0_, ...), custom_call_target="tpu_custom_call", output_to_operand_aliasing={{0}: (1, {}), {1}: (2, {})} | custom-call | flops 10000000 | bytes 1048576 | tf_op jit(solution)/shard_map/pallas_call | solution.py:432
  43.0 0.1 collective-permute-start.5
  43.0 4.6 %collective-permute-start.4 = (f32[6,32,128]{2,1,0:T(8,128)S(1)}, f32[6,32,128]{2,1,0:T(8,128)S(1)}, u32[]{:S(2)}, u32[]{:S(2)}) collective-permute-start(f32[6,32,128]{2,1,0:T(8,128)S(1)} %get-tuple-element.69.sent), channel_id=1, source_target_pairs={{1,2},{2,1},{3,4},{4,3},{5,6},{6,5},{7,8},{8,7},{9,10},{10,9},{11,... | collective-permute-start | bytes 294920 | tf_op jit(solution)/shard_map/ppermute | solution.py:451
  47.6 0.5 shard_map.43
  48.1 0.0 collective-permute-done.5.got_in
  48.1 5.1 %collective-permute-done.4.got_out = f32[6,32,128]{2,1,0:T(8,128)S(1)} collective-permute-done((f32[6,32,128]{2,1,0:T(8,128)S(1)}, f32[6,32,128]{2,1,0:T(8,128)S(1)}, u32[]{:S(2)}, u32[]{:S(2)}) %collective-permute-start.4) | collective-permute-done | bytes 98336 | tf_op jit(solution)/shard_map/ppermute | solution.py:451
  53.2 0.7 %shard_map.44 = (f32[4,32,128]{2,1,0:T(8,128)S(1)}, f32[2,32,128]{2,1,0:T(8,128)S(1)}, f32[2,32,128]{2,1,0:T(8,128)S(1)}, f32[10,32,128]{2,1,0:T(8,128)S(1)}, f32[4,32,128]{2,1,0:T(8,128)S(1)}) custom-call(f32[6,32,128]{2,1,0:T(8,128)S(1)} %get-tuple-element.69.sent, f32[6,32,128]{2,1,0:T(8,128)S(1)} %collective-permute-done.4.got_out, ...), custom_call_target="tpu_custom_call" | custom-call | flops 10000000 | bytes 1048576 | tf_op jit(solution)/shard_map/pallas_call | solution.py:432
  54.0 1.3 %collective-permute-start.6 = (f32[4,32,128]{2,1,0:T(8,128)S(1)}, f32[4,32,128]{2,1,0:T(8,128)S(1)}, u32[]{:S(2)}, u32[]{:S(2)}) collective-permute-start(f32[4,32,128]{2,1,0:T(8,128)S(1)} %get-tuple-element.80), channel_id=1, source_target_pairs={{0,128},{1,129},{2,130},{3,131},{4,132},{5,133},{6,134},{7,135},{8... | collective-permute-start | bytes 196616 | tf_op jit(solution)/shard_map/ppermute | solution.py:457
  55.3 1.3 %collective-permute-start.7 = (f32[2,32,128]{2,1,0:T(8,128)S(1)}, f32[2,32,128]{2,1,0:T(8,128)S(1)}, u32[]{:S(2)}, u32[]{:S(2)}) collective-permute-start(f32[2,32,128]{2,1,0:T(8,128)S(1)} %get-tuple-element.81), channel_id=1, source_target_pairs={{0,129},{1,130},{2,131},{3,132},{4,133},{5,134},{6,135},{7,136},{8... | collective-permute-start | bytes 98312 | tf_op jit(solution)/shard_map/ppermute | solution.py:457
  56.6 1.3 %collective-permute-start.8 = (f32[2,32,128]{2,1,0:T(8,128)S(1)}, f32[2,32,128]{2,1,0:T(8,128)S(1)}, u32[]{:S(2)}, u32[]{:S(2)}) collective-permute-start(f32[2,32,128]{2,1,0:T(8,128)S(1)} %get-tuple-element.82), channel_id=1, source_target_pairs={{1,128},{2,129},{3,130},{4,131},{5,132},{6,133},{7,134},{8,135},{9... | collective-permute-start | bytes 98312 | tf_op jit(solution)/shard_map/ppermute | solution.py:457
  57.9 4.1 %collective-permute-done.7.from_below = f32[2,32,128]{2,1,0:T(8,128)S(1)} collective-permute-done((f32[2,32,128]{2,1,0:T(8,128)S(1)}, f32[2,32,128]{2,1,0:T(8,128)S(1)}, u32[]{:S(2)}, u32[]{:S(2)}) %collective-permute-start.7) | collective-permute-done | bytes 32800 | tf_op jit(solution)/shard_map/ppermute | solution.py:457
  62.0 5.2 %collective-permute-done.8.from_above = f32[2,32,128]{2,1,0:T(8,128)S(1)} collective-permute-done((f32[2,32,128]{2,1,0:T(8,128)S(1)}, f32[2,32,128]{2,1,0:T(8,128)S(1)}, u32[]{:S(2)}, u32[]{:S(2)}) %collective-permute-start.8) | collective-permute-done | bytes 32800 | tf_op jit(solution)/shard_map/ppermute | solution.py:457
  67.2 0.0 collective-permute-done.6.tm_mid
  67.2 1.7 %shard_map.45 = f32[2,8,64,128]{3,2,1,0:T(8,128)} custom-call(f32[2,24,80,128]{3,2,1,0:T(8,128)S(1)} %get-tuple-element.68.fine, f32[2,4,32,128]{3,2,1,0:T(8,128)S(1)} %get-tuple-element.67.refs_8_.old, f32[10,32,128]{2,1,0:T(8,128)S(1)} %get-tuple-element.78.first, f32[4,32,128]{2,1,0:T(8,128)S(1)} %get-tuple-element.79.newer, ...), custom_call_target="tpu_custom_call" | custom-call | flops 10000000 | bytes 1048576 | tf_op jit(solution)/shard_map/pallas_call | solution.py:432
  (1 shorter events, 0.0 us)
Async XLA Ops:
  0.0 1.0 %copy-start = (f32[2,8,64,128]{3,2,1,0:T(8,128)S(1)}, f32[2,8,64,128]{3,2,1,0:T(8,128)}, u32[]{:S(2)}) copy-start(f32[2,8,64,128]{3,2,1,0:T(8,128)} %states.5) | copy-start | bytes 1572868
  1.0 0.9 %copy-start.1 = (f32[8,64,128]{2,1,0:T(8,128)S(1)}, f32[8,64,128]{2,1,0:T(8,128)}, u32[]{:S(2)}) copy-start(f32[8,64,128]{2,1,0:T(8,128)} %kappa.3) | copy-start | bytes 786436
  2.0 0.9 %copy-start.2 = (f32[8,64,128]{2,1,0:T(8,128)S(1)}, f32[8,64,128]{2,1,0:T(8,128)}, u32[]{:S(2)}) copy-start(f32[8,64,128]{2,1,0:T(8,128)} %rate.3) | copy-start | bytes 786436
  3.1 5.4 %collective-permute-start.1 = (f32[28,64,128]{2,1,0:T(8,128)S(1)}, f32[28,64,128]{2,1,0:T(8,128)S(1)}, u32[]{:S(2)}, u32[]{:S(2)}) collective-permute-start(f32[28,64,128]{2,1,0:T(8,128)S(1)} %get-tuple-element.45), channel_id=1, source_target_pairs={{0,1},{1,0},{2,3},{3,2},{4,5},{5,4},{6,7},{7,6},{8,9},{9,8},{10,11... | collective-permute-start | bytes 2752520 | tf_op jit(solution)/shard_map/ppermute | solution.py:451
  3.8 18.9 %collective-permute-start = (f32[28,64,128]{2,1,0:T(8,128)S(1)}, f32[28,64,128]{2,1,0:T(8,128)S(1)}, u32[]{:S(2)}, u32[]{:S(2)}) collective-permute-start(f32[28,64,128]{2,1,0:T(8,128)S(1)} %get-tuple-element.44), channel_id=1, source_target_pairs={{1,2},{2,1},{3,4},{4,3},{5,6},{6,5},{7,8},{8,7},{9,10},{10,9},{11,... | collective-permute-start | bytes 2752520 | tf_op jit(solution)/shard_map/ppermute | solution.py:451
  25.1 6.4 %collective-permute-start.3 = (f32[18,64,128]{2,1,0:T(8,128)S(1)}, f32[18,64,128]{2,1,0:T(8,128)S(1)}, u32[]{:S(2)}, u32[]{:S(2)}) collective-permute-start(f32[18,64,128]{2,1,0:T(8,128)S(1)} %get-tuple-element.55.sent2), channel_id=1, source_target_pairs={{0,1},{1,0},{2,3},{3,2},{4,5},{5,4},{6,7},{7,6},{8,9},{9,8},{10,11... | collective-permute-start | bytes 1769480 | tf_op jit(solution)/shard_map/ppermute | solution.py:451
  25.2 15.4 %collective-permute-start.2 = (f32[18,64,128]{2,1,0:T(8,128)S(1)}, f32[18,64,128]{2,1,0:T(8,128)S(1)}, u32[]{:S(2)}, u32[]{:S(2)}) collective-permute-start(f32[18,64,128]{2,1,0:T(8,128)S(1)} %get-tuple-element.55.sent2), channel_id=1, source_target_pairs={{1,2},{2,1},{3,4},{4,3},{5,6},{6,5},{7,8},{8,7},{9,10},{10,9},{11,... | collective-permute-start | bytes 1769480 | tf_op jit(solution)/shard_map/ppermute | solution.py:451
  43.0 5.2 %collective-permute-start.5 = (f32[6,32,128]{2,1,0:T(8,128)S(1)}, f32[6,32,128]{2,1,0:T(8,128)S(1)}, u32[]{:S(2)}, u32[]{:S(2)}) collective-permute-start(f32[6,32,128]{2,1,0:T(8,128)S(1)} %get-tuple-element.69.sent), channel_id=1, source_target_pairs={{0,1},{1,0},{2,3},{3,2},{4,5},{5,4},{6,7},{7,6},{8,9},{9,8},{10,11... | collective-permute-start | bytes 294920 | tf_op jit(solution)/shard_map/ppermute | solution.py:451
  43.0 10.2 %collective-permute-start.4 = (f32[6,32,128]{2,1,0:T(8,128)S(1)}, f32[6,32,128]{2,1,0:T(8,128)S(1)}, u32[]{:S(2)}, u32[]{:S(2)}) collective-permute-start(f32[6,32,128]{2,1,0:T(8,128)S(1)} %get-tuple-element.69.sent), channel_id=1, source_target_pairs={{1,2},{2,1},{3,4},{4,3},{5,6},{6,5},{7,8},{8,7},{9,10},{10,9},{11,... | collective-permute-start | bytes 294920 | tf_op jit(solution)/shard_map/ppermute | solution.py:451
  54.0 13.3 %collective-permute-start.6 = (f32[4,32,128]{2,1,0:T(8,128)S(1)}, f32[4,32,128]{2,1,0:T(8,128)S(1)}, u32[]{:S(2)}, u32[]{:S(2)}) collective-permute-start(f32[4,32,128]{2,1,0:T(8,128)S(1)} %get-tuple-element.80), channel_id=1, source_target_pairs={{0,128},{1,129},{2,130},{3,131},{4,132},{5,133},{6,134},{7,135},{8... | collective-permute-start | bytes 196616 | tf_op jit(solution)/shard_map/ppermute | solution.py:457
  55.3 6.7 %collective-permute-start.7 = (f32[2,32,128]{2,1,0:T(8,128)S(1)}, f32[2,32,128]{2,1,0:T(8,128)S(1)}, u32[]{:S(2)}, u32[]{:S(2)}) collective-permute-start(f32[2,32,128]{2,1,0:T(8,128)S(1)} %get-tuple-element.81), channel_id=1, source_target_pairs={{0,129},{1,130},{2,131},{3,132},{4,133},{5,134},{6,135},{7,136},{8... | collective-permute-start | bytes 98312 | tf_op jit(solution)/shard_map/ppermute | solution.py:457
  56.6 10.7 %collective-permute-start.8 = (f32[2,32,128]{2,1,0:T(8,128)S(1)}, f32[2,32,128]{2,1,0:T(8,128)S(1)}, u32[]{:S(2)}, u32[]{:S(2)}) collective-permute-start(f32[2,32,128]{2,1,0:T(8,128)S(1)} %get-tuple-element.82), channel_id=1, source_target_pairs={{1,128},{2,129},{3,130},{4,131},{5,132},{6,133},{7,134},{8,135},{9... | collective-permute-start | bytes 98312 | tf_op jit(solution)/shard_map/ppermute | solution.py:457

commit v3 on v2

--- a/solution.py
+++ b/solution.py
@@ -161,16 +161,19 @@
 
 def pack_kernel(states, kappa, rate, send_out, send_in):
     odd = odd_here()
-    for ref, near in ((send_out, 2 * odd), (send_in, 2 - 2 * odd)):
-        for w in range(2):
-            for i in range(HALO):
-                ref[HALO * w + i] = states[w, near + i]
-        for i in range(ROWS):
-            ref[2 * HALO + i] = kappa[i]
-            ref[2 * HALO + ROWS + i] = rate[i]
-
-
-def place_halo(got, field, k_ext, r_ext, above):
+    out, near = 2 * odd, 2 - 2 * odd
+    for i in range(HALO):
+        for w in range(2):
+            send_out[HALO * w + i] = states[w, out + i]
+            send_in[HALO * w + i] = states[w, near + i]
+        send_out[2 * HALO + i] = kappa[out + i]
+        send_out[3 * HALO + i] = rate[out + i]
+    for i in range(ROWS):
+        send_in[2 * HALO + i] = kappa[i]
+        send_in[2 * HALO + ROWS + i] = rate[i]
+
+
+def place_halo(got, field, k_ext, r_ext, above, depth):
     for w in range(2):
 
         def halo(i, carry):
@@ -178,13 +181,20 @@
             return carry
 
         lax.fori_loop(0, HALO, halo, 0)
+    low = 8 - depth
 
     def coef(i, carry):
-        k_ext[16 * above + i, PAD : PAD + 64, :] = got[2 * HALO + i]
-        r_ext[16 * above + i, PAD : PAD + 64, :] = got[2 * HALO + ROWS + i]
-        return carry
-
-    lax.fori_loop(0, ROWS, coef, 0)
+        k_ext[low + (16 - low) * above + i, PAD : PAD + 64, :] = got[2 * HALO + i]
+        r_ext[low + (16 - low) * above + i, PAD : PAD + 64, :] = got[2 * HALO + depth + i]
+        return carry
+
+    lax.fori_loop(0, depth, coef, 0)
+
+
+def coarse_pair(k_ext, r_ext, fine):
+    return pack2(
+        coarse_row(lines_of(k_ext, (), fine)), 4.0 * coarse_row(lines_of(r_ext, (), fine))
+    )
 
 
 def place_own(states, field):
@@ -200,7 +210,7 @@
     return lambda part, first: ref[lead + (row + part, pl.ds(PAD + first, 32, stride=2))]
 
 
-def inner_first_kernel(states, kappa, rate, got_in, field, other, diag, cx, cy, cz, cw, r_ext, k_ext):
+def inner_first_kernel(states, kappa, rate, got_in, late, field, other, diag, cx, cy, cz, cw, r_ext, k_ext):
     odd = odd_here()
     clear_pads_flat(k_ext, 0, EXT, 64)
     clear_pads(field, 0, EXT, 64)
@@ -213,7 +223,11 @@
         return carry
 
     lax.fori_loop(0, ROWS, own, 0)
-    place_halo(got_in, field, k_ext, r_ext, 1 - odd)
+    place_halo(got_in, field, k_ext, r_ext, 1 - odd, ROWS)
+    for i in range(2):
+        late[i] = kappa[6 - 6 * odd + i]
+        late[2 + i] = rate[6 - 6 * odd + i]
+        late[4, 32 * i : 32 * i + 32, :] = coarse_pair(k_ext, r_ext, 16 - 12 * odd + 2 * i)
     coefs = (diag, cx, cy, cz, cw)
     build_coefs(k_ext, r_ext, coefs, 9 - 8 * odd, 14, 64, 1)
     src, dst = field, other
@@ -224,11 +238,11 @@
 
 def outer_first_kernel(got_out, *refs):
     refs = refs[9:]
-    send, field, other, diag, cx, cy, cz, cw, r_ext, k_ext = refs
-    odd = odd_here()
-    place_halo(got_out, field, k_ext, r_ext, odd)
-    coefs = (diag, cx, cy, cz, cw)
-    build_coefs(k_ext, r_ext, coefs, 1 + 14 * odd, 8, 64, 1)
+    send_out, send_in, field, other, diag, cx, cy, cz, cw, r_ext, k_ext = refs
+    odd = odd_here()
+    place_halo(got_out, field, k_ext, r_ext, odd, HALO)
+    coefs = (diag, cx, cy, cz, cw)
+    build_coefs(k_ext, r_ext, coefs, 3 + 12 * odd, 6, 64, 1)
     src, dst = field, other
     for n in range(1, 7):
         advance(src, dst, coefs, r_ext, 2 + n + (14 - 2 * n) * odd, 6, 64, 1, 2)
@@ -236,20 +250,19 @@
 
     def own(i, carry):
         for w in range(2):
-            send[ROWS * w + i] = src[w, BASE + i, PAD : PAD + 64, :]
+            value = src[w, BASE + i, PAD : PAD + 64, :]
+            send_out[ROWS * w + i] = value
+            send_in[ROWS * w + i] = value
         return carry
 
     lax.fori_loop(0, ROWS, own, 0)
-    for slot, row in enumerate((-2, -1, 4, 5)):
-        fine = BASE + 2 * row
-        packed = pack2(
-            coarse_row(lines_of(k_ext, (), fine)), 4.0 * coarse_row(lines_of(r_ext, (), fine))
-        )
-        send[16 + slot // 2, 32 * (slot % 2) : 32 * (slot % 2) + 32, :] = packed
-
-
-def inner_second_kernel(got_in, *refs):
-    _, _, diag, cx, cy, cz, cw, r_ext, field, other = refs
+    for i in range(2):
+        send_in[16, 32 * i : 32 * i + 32, :] = coarse_pair(k_ext, r_ext, 4 + 12 * odd + 2 * i)
+
+
+def inner_second_kernel(got_in, got_late, *refs):
+    refs = refs[9:]
+    field, other, diag, cx, cy, cz, cw, r_ext, k_ext = refs
     odd = odd_here()
 
     def halo(i, carry):
@@ -258,7 +271,11 @@
         return carry
 
     lax.fori_loop(0, ROWS, halo, 0)
-    coefs = (diag, cx, cy, cz, cw)
+    for i in range(2):
+        k_ext[22 * odd + i, PAD : PAD + 64, :] = got_late[i]
+        r_ext[22 * odd + i, PAD : PAD + 64, :] = got_late[2 + i]
+    coefs = (diag, cx, cy, cz, cw)
+    build_coefs(k_ext, r_ext, coefs, 1 + 20 * odd, 2, 64, 1)
     src, dst = field, other
     for n in range(1, 7):
         advance(src, dst, coefs, r_ext, BASE + n - 8 * odd, 16 - 2 * n, 64, 1, 2)
@@ -333,7 +350,7 @@
             old[w, i] = src[w, CBASE + i, PAD : PAD + 32, :]
 
 
-def chain_coefs_kernel(kc_near, rc_near, sent2, got_out2, got_in2, rc, diag, cx, cy, cz, cw, kc):
+def chain_coefs_kernel(kc_near, rc_near, got_late, got_in2, rc, diag, cx, cy, cz, cw, kc):
     odd = odd_here()
     clear_pads_flat(kc, 0, CEXT, 32)
 
@@ -343,9 +360,9 @@
         return carry
 
     lax.fori_loop(CBASE - 4, CBASE + 8, near, 0)
-    for got, above in ((got_out2, odd), (got_in2, 1 - odd)):
+    for got, slot, above in ((got_late, 4, odd), (got_in2, 16, 1 - odd)):
         for j in range(2):
-            packed = got[16 + above, 32 * j : 32 * j + 32, :]
+            packed = got[slot, 32 * j : 32 * j + 32, :]
             row = CBASE - 6 + 14 * above + j
             kc[row, PAD : PAD + 32, :] = unpack_a(packed)
             rc[row, PAD : PAD + 32, :] = unpack_b(packed)
@@ -475,36 +492,36 @@
 
 
 def shards(states, kappa, rate):
-    units = 2 * HALO + 2 * ROWS
     fields = [shape(*FINE_FIELD)] * 2
     fine_coefs = [shape(*sizes) for sizes in FINE_COEFS]
     coarse_coefs = [shape(*sizes) for sizes in COARSE_COEFS]
     send_out, send_in = call(
-        pack_kernel, [shape(units, 64, LANES)] * 2, [], 1000, states, kappa, rate
+        pack_kernel, [shape(4 * HALO, 64, LANES), shape(2 * HALO + 2 * ROWS, 64, LANES)],
+        [], 1000, states, kappa, rate,
     )
     got_out, got_in = swaps(send_out, send_in)
-    work = call(
+    late, *work = call(
         inner_first_kernel,
-        fields + fine_coefs + [shape(*FINE_FLAT)] * 2,
+        [shape(5, 64, LANES)] + fields + fine_coefs + [shape(*FINE_FLAT)] * 2,
         [], COST, states, kappa, rate, got_in,
     )
-    send, *work = call(
+    got_late = swap(late, True)
+    send_out2, send_in2, *work = call(
         outer_first_kernel,
-        [shape(18, 64, LANES)] + fields + fine_coefs + [shape(*FINE_FLAT)] * 2,
-        [], COST, got_out, *work, aliases={1 + n: 1 + n for n in range(9)},
-    )
-    field, other, *coefs, r_ext, k_ext = work
-    got_out2, got_in2 = swaps(send, send)
+        [shape(16, 64, LANES), shape(17, 64, LANES)] + fields + fine_coefs + [shape(*FINE_FLAT)] * 2,
+        [], COST, got_out, *work, aliases={1 + n: 2 + n for n in range(9)},
+    )
+    got_out2, got_in2 = swaps(send_out2, send_in2)
+    field, other, *coefs, r_ext, k_ext = call(
+        inner_second_kernel, fields + fine_coefs + [shape(*FINE_FLAT)] * 2,
+        [], COST, got_in2, got_late, *work, aliases={2 + n: n for n in range(9)},
+    )
     old, kc, rc = call(
         old_kernel,
         [shape(2, CROWS, 32, LANES), shape(*COARSE_FLAT), shape(*COARSE_FLAT)],
         [FINE_FIELD] + COARSE_COEFS + [COARSE_FIELD] * 2,
         COST, states, got_out, got_in, k_ext, r_ext,
     )
-    field, other = call(
-        inner_second_kernel, fields, [], COST, got_in2, field, other, *coefs, r_ext,
-        aliases={1: 0, 2: 1},
-    )
     field, other, send3 = call(
         outer_second_kernel,
         fields + [shape(6, 32, LANES)],
@@ -513,7 +530,7 @@
     got_out3, got_in3 = swaps(send3, send3)
     rc2, *coarse = call(
         chain_coefs_kernel, [shape(*COARSE_FLAT)] + coarse_coefs, [COARSE_FLAT],
-        COST, kc, rc, send, got_out2, got_in2,
+        COST, kc, rc, got_late, got_in2,
     )
     tm_mid, tm_up, tm_down, first, newer = call(
         third_kernel,
@@ -521,7 +538,9 @@
         [COARSE_FIELD] * 2,
         COST, send3, got_out3, got_in3, rc2, *coarse,
     )
-    mid, from_below, from_above = over_tm(tm_mid, 0), over_tm(tm_up, 1), over_tm(tm_down, -1)
+    from_below = over_tm(tm_up, 1)
+    from_above = over_tm(tm_down, -1)
+    mid = over_tm(tm_mid, 0)
     (ends,) = call(
         last_kernel,
         [shape(2, ROWS, 64, LANES)],

time: 69.3 us -> 73.4 us (1.059)
  starting transfers between devices: 18.6 us -> 23.8 us
  waiting for transfers between devices: 31.7 us -> 30.5 us
    ppermute x6 -> x7, starting transfers between devices: 14.7 us -> 19.9 us  [swap(): return lax.ppermute(value, ('tm', 'space'), pairs)]
    ppermute x6 -> x7, waiting for transfers between devices: 22.3 us -> 21.1 us  [swap(): return lax.ppermute(value, ('tm', 'space'), pairs)]
  transfers between devices with their start and end apart: 9 -> 10, of which waited for: 5 -> 5; matrix products, arithmetic and copies ran while one was open for 0% -> 0% of each run, Pallas kernels for 12% -> 12%
where the time goes in v3:
time: 73.4 us; the launch traced here: 73 us
  waiting for transfers between devices  30.5 us (42%)
  starting transfers between devices  23.8 us (32%)
  Pallas kernels  15.7 us (21%)
  local copies, waits for them, and re-layouts  2.94 us (4%)
    ppermute x7, waiting for transfers between devices, swap(): return lax.ppermute(value, ('tm', 'space'), pairs)  21.1 us
    ppermute x7, starting transfers between devices, swap(): return lax.ppermute(value, ('tm', 'space'), pairs)  19.9 us
    pallas_call x9, Pallas kernels, call(): pl.pallas_call(kernel, out_shape=outs, in_specs=[pl.BlockSpec(memory_spac...  15.7 us
    ppermute x3, waiting for transfers between devices, over_tm(): return lax.ppermute(value, ('tm', 'space'), pairs)  9.37 us
    ppermute x3, starting transfers between devices, over_tm(): return lax.ppermute(value, ('tm', 'space'), pairs)  3.88 us
    unnamed x6, local copies, waits for them, and re-layouts  2.94 us
  transfers between devices with their start and end apart: 10, of which 5 were waited for; matrix products, arithmetic and copies ran while one was open for 0% of the time, Pallas kernels for 12%

profile of v3, /device:TPU:127, one launch (start us, length us, event | category | flops | bytes accessed | tf_op | source)
XLA Modules:
  0.0 73.0 jit_solution(1813859298668599595)
XLA Ops:
  0.0 1.0 %copy-done = f32[2,8,64,128]{3,2,1,0:T(8,128)S(1)} copy-done((f32[2,8,64,128]{3,2,1,0:T(8,128)S(1)}, f32[2,8,64,128]{3,2,1,0:T(8,128)}, u32[]{:S(2)}) %copy-start) | copy-done | bytes 524312
  1.0 0.9 %copy-done.1 = f32[8,64,128]{2,1,0:T(8,128)S(1)} copy-done((f32[8,64,128]{2,1,0:T(8,128)S(1)}, f32[8,64,128]{2,1,0:T(8,128)}, u32[]{:S(2)}) %copy-start.1) | copy-done | bytes 262168
  2.0 0.9 %copy-done.2 = f32[8,64,128]{2,1,0:T(8,128)S(1)} copy-done((f32[8,64,128]{2,1,0:T(8,128)S(1)}, f32[8,64,128]{2,1,0:T(8,128)}, u32[]{:S(2)}) %copy-start.2) | copy-done | bytes 262168
  2.9 0.1 shard_map.37
  3.1 0.8 %collective-permute-start.1 = (f32[28,64,128]{2,1,0:T(8,128)S(1)}, f32[28,64,128]{2,1,0:T(8,128)S(1)}, u32[]{:S(2)}, u32[]{:S(2)}) collective-permute-start(f32[28,64,128]{2,1,0:T(8,128)S(1)} %get-tuple-element.54), channel_id=1, source_target_pairs={{0,1},{1,0},{2,3},{3,2},{4,5},{5,4},{6,7},{7,6},{8,9},{9,8},{10,11... | collective-permute-start | bytes 2752520 | tf_op jit(solution)/shard_map/ppermute | solution.py:468
  3.8 4.6 %collective-permute-start = (f32[24,64,128]{2,1,0:T(8,128)S(1)}, f32[24,64,128]{2,1,0:T(8,128)S(1)}, u32[]{:S(2)}, u32[]{:S(2)}) collective-permute-start(f32[24,64,128]{2,1,0:T(8,128)S(1)} %get-tuple-element.53), channel_id=1, source_target_pairs={{1,2},{2,1},{3,4},{4,3},{5,6},{6,5},{7,8},{8,7},{9,10},{10,9},{11,... | collective-permute-start | bytes 2359304 | tf_op jit(solution)/shard_map/ppermute | solution.py:468
  8.4 0.0 collective-permute-done.1.got_in
  8.4 3.5 %shard_map.38 = (f32[5,64,128]{2,1,0:T(8,128)S(1)}, f32[2,24,80,128]{3,2,1,0:T(8,128)S(1)}, f32[2,24,80,128]{3,2,1,0:T(8,128)S(1)}, f32[24,64,128]{2,1,0:T(8,128...) custom-call(f32[2,8,64,128]{3,2,1,0:T(8,128)S(1)} %copy-done, ...), custom_call_target="tpu_custom_call" | custom-call | flops 10000000 | bytes 1048576 | tf_op jit(solution)/shard_map/pallas_call | solution.py:449
  11.9 9.4 %collective-permute-done.got_out = f32[24,64,128]{2,1,0:T(8,128)S(1)} collective-permute-done((f32[24,64,128]{2,1,0:T(8,128)S(1)}, f32[24,64,128]{2,1,0:T(8,128)S(1)}, u32[]{:S(2)}, u32[]{:S(2)}) %collective-permute-start) | collective-permute-done | bytes 786464 | tf_op jit(solution)/shard_map/ppermute | solution.py:468
  21.3 2.1 %shard_map.39 = (f32[16,64,128]{2,1,0:T(8,128)S(1)}, f32[17,64,128]{2,1,0:T(8,128)S(1)}, f32[2,24,80,128]{3,2,1,0:T(8,128)S(1)}, f32[2,24,80,128]{3,2,1,0:T(8,12...) custom-call(f32[24,64,128]{2,1,0:T(8,128)S(1)} %collective-permute-d, ...), custom_call_target="tpu_custom_call", output_to_operand_aliasing={{2}: (1, {}), {3}: (2, {}), {4}: (3, {}), {5}: (4, {}), {6}... | custom-call | flops 10000000 | bytes 1048576 | tf_op jit(solution)/shard_map/pallas_call | solution.py:449
  23.5 0.1 collective-permute-start.3
  23.6 4.6 %collective-permute-start.2 = (f32[16,64,128]{2,1,0:T(8,128)S(1)}, f32[16,64,128]{2,1,0:T(8,128)S(1)}, u32[]{:S(2)}, u32[]{:S(2)}) collective-permute-start(f32[16,64,128]{2,1,0:T(8,128)S(1)} %get-tuple-element.64), channel_id=1, source_target_pairs={{1,2},{2,1},{3,4},{4,3},{5,6},{6,5},{7,8},{8,7},{9,10},{10,9},{11,... | collective-permute-start | bytes 1572872 | tf_op jit(solution)/shard_map/ppermute | solution.py:468
  28.2 5.2 %collective-permute-start.4 = (f32[5,64,128]{2,1,0:T(8,128)S(1)}, f32[5,64,128]{2,1,0:T(8,128)S(1)}, u32[]{:S(2)}, u32[]{:S(2)}) collective-permute-start(f32[5,64,128]{2,1,0:T(8,128)S(1)} %get-tuple-element.66), channel_id=1, source_target_pairs={{1,2},{2,1},{3,4},{4,3},{5,6},{6,5},{7,8},{8,7},{9,10},{10,9},{11,... | collective-permute-start | bytes 491528 | tf_op jit(solution)/shard_map/ppermute | solution.py:468
  33.4 6.7 %collective-permute-done.4.got_late = f32[5,64,128]{2,1,0:T(8,128)S(1)} collective-permute-done((f32[5,64,128]{2,1,0:T(8,128)S(1)}, f32[5,64,128]{2,1,0:T(8,128)S(1)}, u32[]{:S(2)}, u32[]{:S(2)}) %collective-permute-start.4) | collective-permute-done | bytes 163872 | tf_op jit(solution)/shard_map/ppermute | solution.py:468
  40.0 0.0 collective-permute-done.3.got_in.got_in2
  40.1 2.9 %shard_map.40 = (f32[2,24,80,128]{3,2,1,0:T(8,128)S(1)}, f32[2,24,80,128]{3,2,1,0:T(8,128)S(1)}, f32[24,64,128]{2,1,0:T(8,128)S(1)}, f32[24,64,128]{2,1,0:T(8,12...) custom-call(f32[17,64,128]{2,1,0:T(8,128)S(1)} %collective-permute-d, ...), custom_call_target="tpu_custom_call", output_to_operand_aliasing={{0}: (2, {}), {1}: (3, {}), {2}: (4, {}), {3}: (5, {}), {4}... | custom-call | flops 10000000 | bytes 1048576 | tf_op jit(solution)/shard_map/pallas_call | solution.py:449
  43.0 1.7 %shard_map.41 = (f32[2,4,32,128]{3,2,1,0:T(8,128)S(1)}, f32[20,48,128]{2,1,0:T(8,128)S(1)}, f32[20,48,128]{2,1,0:T(8,128)S(1)}) custom-call(f32[2,8,64,128]{3,2,1,0:T(8,128)S(1)} %copy-done, f32[24,64,128]{2,1,0:T(8,128)S(1)} %collective-permute-done.got_out, f32[28,64,128]{2,1,0:T(8,128)S(1)} %collective-permute-done.1.got_in, ...), custom_call_target="tpu_custom_call" | custom-call | flops 10000000 | bytes 1048576 | tf_op jit(solution)/shard_map/pallas_call | solution.py:449
  44.7 0.0 collective-permute-done.2.got_out
  44.7 2.4 %shard_map.42 = (f32[2,24,80,128]{3,2,1,0:T(8,128)S(1)}, f32[2,24,80,128]{3,2,1,0:T(8,128)S(1)}, f32[6,32,128]{2,1,0:T(8,128)S(1)}) custom-call(f32[16,64,128]{2,1,0:T(8,128)S(1)} %collective-permute-done.2.got_out, f32[2,24,80,128]{3,2,1,0:T(8,128)S(1)} %get-tuple-element.76.refs_0_, ...), custom_call_target="tpu_custom_call", output_to_operand_aliasing={{0}: (1, {}), {1}: (2, {})} | custom-call | flops 10000000 | bytes 1048576 | tf_op jit(solution)/shard_map/pallas_call | solution.py:449
  47.0 0.1 collective-permute-start.6
  47.1 4.6 %collective-permute-start.5 = (f32[6,32,128]{2,1,0:T(8,128)S(1)}, f32[6,32,128]{2,1,0:T(8,128)S(1)}, u32[]{:S(2)}, u32[]{:S(2)}) collective-permute-start(f32[6,32,128]{2,1,0:T(8,128)S(1)} %get-tuple-element.87.sent), channel_id=1, source_target_pairs={{1,2},{2,1},{3,4},{4,3},{5,6},{6,5},{7,8},{8,7},{9,10},{10,9},{11,... | collective-permute-start | bytes 294920 | tf_op jit(solution)/shard_map/ppermute | solution.py:468
  51.7 0.5 shard_map.43
  52.2 0.0 collective-permute-done.6.got_in
  52.2 5.1 %collective-permute-done.5.got_out = f32[6,32,128]{2,1,0:T(8,128)S(1)} collective-permute-done((f32[6,32,128]{2,1,0:T(8,128)S(1)}, f32[6,32,128]{2,1,0:T(8,128)S(1)}, u32[]{:S(2)}, u32[]{:S(2)}) %collective-permute-start.5) | collective-permute-done | bytes 98336 | tf_op jit(solution)/shard_map/ppermute | solution.py:468
  57.3 0.7 %shard_map.44 = (f32[4,32,128]{2,1,0:T(8,128)S(1)}, f32[2,32,128]{2,1,0:T(8,128)S(1)}, f32[2,32,128]{2,1,0:T(8,128)S(1)}, f32[10,32,128]{2,1,0:T(8,128)S(1)}, f32[4,32,128]{2,1,0:T(8,128)S(1)}) custom-call(f32[6,32,128]{2,1,0:T(8,128)S(1)} %get-tuple-element.87.sent, f32[6,32,128]{2,1,0:T(8,128)S(1)} %collective-permute-done.5.got_out, ...), custom_call_target="tpu_custom_call" | custom-call | flops 10000000 | bytes 1048576 | tf_op jit(solution)/shard_map/pallas_call | solution.py:449
  58.0 1.3 %collective-permute-start.7 = (f32[4,32,128]{2,1,0:T(8,128)S(1)}, f32[4,32,128]{2,1,0:T(8,128)S(1)}, u32[]{:S(2)}, u32[]{:S(2)}) collective-permute-start(f32[4,32,128]{2,1,0:T(8,128)S(1)} %get-tuple-element.98), channel_id=1, source_target_pairs={{0,128},{1,129},{2,130},{3,131},{4,132},{5,133},{6,134},{7,135},{8... | collective-permute-start | bytes 196616 | tf_op jit(solution)/shard_map/ppermute | solution.py:474
  59.3 1.3 %collective-permute-start.8 = (f32[2,32,128]{2,1,0:T(8,128)S(1)}, f32[2,32,128]{2,1,0:T(8,128)S(1)}, u32[]{:S(2)}, u32[]{:S(2)}) collective-permute-start(f32[2,32,128]{2,1,0:T(8,128)S(1)} %get-tuple-element.99), channel_id=1, source_target_pairs={{0,129},{1,130},{2,131},{3,132},{4,133},{5,134},{6,135},{7,136},{8... | collective-permute-start | bytes 98312 | tf_op jit(solution)/shard_map/ppermute | solution.py:474
  60.6 1.3 %collective-permute-start.9 = (f32[2,32,128]{2,1,0:T(8,128)S(1)}, f32[2,32,128]{2,1,0:T(8,128)S(1)}, u32[]{:S(2)}, u32[]{:S(2)}) collective-permute-start(f32[2,32,128]{2,1,0:T(8,128)S(1)} %get-tuple-element.100), channel_id=1, source_target_pairs={{1,128},{2,129},{3,130},{4,131},{5,132},{6,133},{7,134},{8,135},{9... | collective-permute-start | bytes 98312 | tf_op jit(solution)/shard_map/ppermute | solution.py:474
  61.9 4.1 %collective-permute-done.8.from_below = f32[2,32,128]{2,1,0:T(8,128)S(1)} collective-permute-done((f32[2,32,128]{2,1,0:T(8,128)S(1)}, f32[2,32,128]{2,1,0:T(8,128)S(1)}, u32[]{:S(2)}, u32[]{:S(2)}) %collective-permute-start.8) | collective-permute-done | bytes 32800 | tf_op jit(solution)/shard_map/ppermute | solution.py:474
  66.1 5.2 %collective-permute-done.9.from_above = f32[2,32,128]{2,1,0:T(8,128)S(1)} collective-permute-done((f32[2,32,128]{2,1,0:T(8,128)S(1)}, f32[2,32,128]{2,1,0:T(8,128)S(1)}, u32[]{:S(2)}, u32[]{:S(2)}) %collective-permute-start.9) | collective-permute-done | bytes 32800 | tf_op jit(solution)/shard_map/ppermute | solution.py:474
  71.3 0.0 collective-permute-done.7.tm_mid
  71.3 1.7 %shard_map.45 = f32[2,8,64,128]{3,2,1,0:T(8,128)} custom-call(f32[2,24,80,128]{3,2,1,0:T(8,128)S(1)} %get-tuple-element.86.fine, f32[2,4,32,128]{3,2,1,0:T(8,128)S(1)} %get-tuple-element.85.refs_8_.old, f32[10,32,128]{2,1,0:T(8,128)S(1)} %get-tuple-element.96.first, f32[4,32,128]{2,1,0:T(8,128)S(1)} %get-tuple-element.97.newer, ...), custom_call_target="tpu_custom_call" | custom-call | flops 10000000 | bytes 1048576 | tf_op jit(solution)/shard_map/pallas_call | solution.py:449
  (3 shorter events, 0.0 us)
Async XLA Ops:
  0.0 1.0 %copy-start = (f32[2,8,64,128]{3,2,1,0:T(8,128)S(1)}, f32[2,8,64,128]{3,2,1,0:T(8,128)}, u32[]{:S(2)}) copy-start(f32[2,8,64,128]{3,2,1,0:T(8,128)} %states.5) | copy-start | bytes 1572868
  1.0 0.9 %copy-start.1 = (f32[8,64,128]{2,1,0:T(8,128)S(1)}, f32[8,64,128]{2,1,0:T(8,128)}, u32[]{:S(2)}) copy-start(f32[8,64,128]{2,1,0:T(8,128)} %kappa.3) | copy-start | bytes 786436
  2.0 0.9 %copy-start.2 = (f32[8,64,128]{2,1,0:T(8,128)S(1)}, f32[8,64,128]{2,1,0:T(8,128)}, u32[]{:S(2)}) copy-start(f32[8,64,128]{2,1,0:T(8,128)} %rate.3) | copy-start | bytes 786436
  3.1 5.4 %collective-permute-start.1 = (f32[28,64,128]{2,1,0:T(8,128)S(1)}, f32[28,64,128]{2,1,0:T(8,128)S(1)}, u32[]{:S(2)}, u32[]{:S(2)}) collective-permute-start(f32[28,64,128]{2,1,0:T(8,128)S(1)} %get-tuple-element.54), channel_id=1, source_target_pairs={{0,1},{1,0},{2,3},{3,2},{4,5},{5,4},{6,7},{7,6},{8,9},{9,8},{10,11... | collective-permute-start | bytes 2752520 | tf_op jit(solution)/shard_map/ppermute | solution.py:468
  3.8 17.5 %collective-permute-start = (f32[24,64,128]{2,1,0:T(8,128)S(1)}, f32[24,64,128]{2,1,0:T(8,128)S(1)}, u32[]{:S(2)}, u32[]{:S(2)}) collective-permute-start(f32[24,64,128]{2,1,0:T(8,128)S(1)} %get-tuple-element.53), channel_id=1, source_target_pairs={{1,2},{2,1},{3,4},{4,3},{5,6},{6,5},{7,8},{8,7},{9,10},{10,9},{11,... | collective-permute-start | bytes 2359304 | tf_op jit(solution)/shard_map/ppermute | solution.py:468
  23.5 16.6 %collective-permute-start.3 = (f32[17,64,128]{2,1,0:T(8,128)S(1)}, f32[17,64,128]{2,1,0:T(8,128)S(1)}, u32[]{:S(2)}, u32[]{:S(2)}) collective-permute-start(f32[17,64,128]{2,1,0:T(8,128)S(1)} %get-tuple-element.65), channel_id=1, source_target_pairs={{0,1},{1,0},{2,3},{3,2},{4,5},{5,4},{6,7},{7,6},{8,9},{9,8},{10,11... | collective-permute-start | bytes 1671176 | tf_op jit(solution)/shard_map/ppermute | solution.py:468
  23.6 21.1 %collective-permute-start.2 = (f32[16,64,128]{2,1,0:T(8,128)S(1)}, f32[16,64,128]{2,1,0:T(8,128)S(1)}, u32[]{:S(2)}, u32[]{:S(2)}) collective-permute-start(f32[16,64,128]{2,1,0:T(8,128)S(1)} %get-tuple-element.64), channel_id=1, source_target_pairs={{1,2},{2,1},{3,4},{4,3},{5,6},{6,5},{7,8},{8,7},{9,10},{10,9},{11,... | collective-permute-start | bytes 1572872 | tf_op jit(solution)/shard_map/ppermute | solution.py:468
  28.2 11.9 %collective-permute-start.4 = (f32[5,64,128]{2,1,0:T(8,128)S(1)}, f32[5,64,128]{2,1,0:T(8,128)S(1)}, u32[]{:S(2)}, u32[]{:S(2)}) collective-permute-start(f32[5,64,128]{2,1,0:T(8,128)S(1)} %get-tuple-element.66), channel_id=1, source_target_pairs={{1,2},{2,1},{3,4},{4,3},{5,6},{6,5},{7,8},{8,7},{9,10},{10,9},{11,... | collective-permute-start | bytes 491528 | tf_op jit(solution)/shard_map/ppermute | solution.py:468
  47.0 5.2 %collective-permute-start.6 = (f32[6,32,128]{2,1,0:T(8,128)S(1)}, f32[6,32,128]{2,1,0:T(8,128)S(1)}, u32[]{:S(2)}, u32[]{:S(2)}) collective-permute-start(f32[6,32,128]{2,1,0:T(8,128)S(1)} %get-tuple-element.87.sent), channel_id=1, source_target_pairs={{0,1},{1,0},{2,3},{3,2},{4,5},{5,4},{6,7},{7,6},{8,9},{9,8},{10,11... | collective-permute-start | bytes 294920 | tf_op jit(solution)/shard_map/ppermute | solution.py:468
  47.1 10.2 %collective-permute-start.5 = (f32[6,32,128]{2,1,0:T(8,128)S(1)}, f32[6,32,128]{2,1,0:T(8,128)S(1)}, u32[]{:S(2)}, u32[]{:S(2)}) collective-permute-start(f32[6,32,128]{2,1,0:T(8,128)S(1)} %get-tuple-element.87.sent), channel_id=1, source_target_pairs={{1,2},{2,1},{3,4},{4,3},{5,6},{6,5},{7,8},{8,7},{9,10},{10,9},{11,... | collective-permute-start | bytes 294920 | tf_op jit(solution)/shard_map/ppermute | solution.py:468
  58.0 13.3 %collective-permute-start.7 = (f32[4,32,128]{2,1,0:T(8,128)S(1)}, f32[4,32,128]{2,1,0:T(8,128)S(1)}, u32[]{:S(2)}, u32[]{:S(2)}) collective-permute-start(f32[4,32,128]{2,1,0:T(8,128)S(1)} %get-tuple-element.98), channel_id=1, source_target_pairs={{0,128},{1,129},{2,130},{3,131},{4,132},{5,133},{6,134},{7,135},{8... | collective-permute-start | bytes 196616 | tf_op jit(solution)/shard_map/ppermute | solution.py:474
  59.3 6.7 %collective-permute-start.8 = (f32[2,32,128]{2,1,0:T(8,128)S(1)}, f32[2,32,128]{2,1,0:T(8,128)S(1)}, u32[]{:S(2)}, u32[]{:S(2)}) collective-permute-start(f32[2,32,128]{2,1,0:T(8,128)S(1)} %get-tuple-element.99), channel_id=1, source_target_pairs={{0,129},{1,130},{2,131},{3,132},{4,133},{5,134},{6,135},{7,136},{8... | collective-permute-start | bytes 98312 | tf_op jit(solution)/shard_map/ppermute | solution.py:474
  60.6 10.7 %collective-permute-start.9 = (f32[2,32,128]{2,1,0:T(8,128)S(1)}, f32[2,32,128]{2,1,0:T(8,128)S(1)}, u32[]{:S(2)}, u32[]{:S(2)}) collective-permute-start(f32[2,32,128]{2,1,0:T(8,128)S(1)} %get-tuple-element.100), channel_id=1, source_target_pairs={{1,128},{2,129},{3,130},{4,131},{5,132},{6,133},{7,134},{8,135},{9... | collective-permute-start | bytes 98312 | tf_op jit(solution)/shard_map/ppermute | solution.py:474

commit v4 on v3

--- a/solution.py
+++ b/solution.py
@@ -250,12 +250,17 @@
 
     def own(i, carry):
         for w in range(2):
-            value = src[w, BASE + i, PAD : PAD + 64, :]
-            send_out[ROWS * w + i] = value
-            send_in[ROWS * w + i] = value
+            send_in[ROWS * w + i] = src[w, BASE + i, PAD : PAD + 64, :]
+        send_out[i] = src[0, BASE + i, PAD : PAD + 64, :]
         return carry
 
     lax.fori_loop(0, ROWS, own, 0)
+
+    def near(i, carry):
+        send_out[ROWS + i] = src[1, BASE + 2 * odd + i, PAD : PAD + 64, :]
+        return carry
+
+    lax.fori_loop(0, HALO, near, 0)
     for i in range(2):
         send_in[16, 32 * i : 32 * i + 32, :] = coarse_pair(k_ext, r_ext, 4 + 12 * odd + 2 * i)
 
@@ -287,11 +292,17 @@
     odd = odd_here()
 
     def halo(i, carry):
-        for w in range(2):
-            field[w, 16 * odd + i, PAD : PAD + 64, :] = got_out[ROWS * w + i]
+        field[0, 16 * odd + i, PAD : PAD + 64, :] = got_out[i]
+        return carry
+
+    def near(i, carry):
+        field[1, 2 + 14 * odd + i, PAD : PAD + 64, :] = got_out[ROWS + i]
         return carry
 
     lax.fori_loop(0, ROWS, halo, 0)
+    lax.fori_loop(0, HALO, near, 0)
+    for i in range(2):
+        field[1, 22 * odd + i, PAD : PAD + 64, :] = jnp.zeros((64, LANES), F32)
     coefs = (diag, cx, cy, cz, cw)
     src, dst = field, other
     for n in range(1, 7):
@@ -371,7 +382,7 @@
 
 def third_kernel(
     sent, got_out, got_in, rc, diag, cx, cy, cz, cw,
-    tm_mid, tm_up, tm_down, first, newer, here, there,
+    tm_mid, tm_out, tm_in, first, newer, here, there,
 ):
     odd = odd_here()
     clear_pads(here, 0, CEXT, 32)
@@ -400,16 +411,19 @@
     for j in range(4):
         tm_mid[j] = pack2(carried[2 * j], carried[2 * j + 1])
     for j in range(2):
-        tm_up[j] = pack2(carried[2 * j], carried[2 * j + 1])
-        tm_down[j] = pack2(carried[4 + 2 * j], carried[5 + 2 * j])
+        low = pack2(carried[2 * j], carried[2 * j + 1])
+        high = pack2(carried[4 + 2 * j], carried[5 + 2 * j])
+        tm_out[j] = jnp.where(odd > 0, low, high)
+        tm_in[j] = jnp.where(odd > 0, high, low)
 
 
 def last_kernel(
-    fine, old, first, newer, tm_mid, from_below, from_above, rc, diag, cx, cy, cz, cw, ends, here, there
+    fine, old, first, newer, tm_mid, from_out, from_in, rc, diag, cx, cy, cz, cw, ends, here, there
 ):
     clear_pads(here, 0, CEXT, 32)
     clear_pads(there, 0, CEXT, 32)
-    for ref, start, count in ((from_below, -6, 2), (tm_mid, -2, 4), (from_above, 6, 2)):
+    odd = odd_here()
+    for ref, start, count in ((from_out, 12 * odd - 6, 2), (tm_mid, -2, 4), (from_in, 6 - 12 * odd, 2)):
         for j in range(count):
             row = CBASE + start + 2 * j
             here[0, row, PAD : PAD + 32, :] = unpack_a(ref[j])
@@ -458,20 +472,23 @@
     )(*args)
 
 
+def partners(odd_pairs):
+    count = lax.axis_size("space")
+    lows = range(1 if odd_pairs else 0, count - 1, 2)
+    return [pair for low in lows for pair in ((low, low + 1), (low + 1, low))]
+
+
 def swap(value, odd_pairs):
-    count, groups = lax.axis_size("space"), lax.axis_size("tm")
-    pairs = []
-    for group in range(groups):
-        for low in range(1 if odd_pairs else 0, count - 1, 2):
-            a, b = group * count + low, group * count + low + 1
-            pairs += [(a, b), (b, a)]
+    count = lax.axis_size("space")
+    starts = [group * count for group in range(lax.axis_size("tm"))]
+    pairs = [(start + a, start + b) for start in starts for a, b in partners(odd_pairs)]
     return lax.ppermute(value, ("tm", "space"), pairs)
 
 
-def over_tm(value, offset):
+def over_tm(value, odd_pairs):
     count = lax.axis_size("space")
-    pairs = [(s, count + s + offset) for s in range(count) if 0 <= s + offset < count]
-    return lax.ppermute(value, ("tm", "space"), pairs)
+    pairs = [(s, s) for s in range(count)] if odd_pairs is None else partners(odd_pairs)
+    return lax.ppermute(value, ("tm", "space"), [(a, count + b) for a, b in pairs])
 
 
 FINE_COEFS = [(EXT, 64, LANES), (EXT, 64, LANES), (EXT, 64 + 2 * PAD, LANES), (EXT, 64, LANES), (EXT, 64, LANES)]
@@ -508,7 +525,7 @@
     got_late = swap(late, True)
     send_out2, send_in2, *work = call(
         outer_first_kernel,
-        [shape(16, 64, LANES), shape(17, 64, LANES)] + fields + fine_coefs + [shape(*FINE_FLAT)] * 2,
+        [shape(ROWS + HALO, 64, LANES), shape(17, 64, LANES)] + fields + fine_coefs + [shape(*FINE_FLAT)] * 2,
         [], COST, got_out, *work, aliases={1 + n: 2 + n for n in range(9)},
     )
     got_out2, got_in2 = swaps(send_out2, send_in2)
@@ -532,20 +549,20 @@
         chain_coefs_kernel, [shape(*COARSE_FLAT)] + coarse_coefs, [COARSE_FLAT],
         COST, kc, rc, got_late, got_in2,
     )
-    tm_mid, tm_up, tm_down, first, newer = call(
+    tm_mid, tm_out, tm_in, first, newer = call(
         third_kernel,
         [shape(4, 32, LANES), shape(2, 32, LANES), shape(2, 32, LANES), shape(10, 32, LANES), shape(CROWS, 32, LANES)],
         [COARSE_FIELD] * 2,
         COST, send3, got_out3, got_in3, rc2, *coarse,
     )
-    from_below = over_tm(tm_up, 1)
-    from_above = over_tm(tm_down, -1)
-    mid = over_tm(tm_mid, 0)
+    from_out = over_tm(tm_out, True)
+    from_in = over_tm(tm_in, False)
+    mid = over_tm(tm_mid, None)
     (ends,) = call(
         last_kernel,
         [shape(2, ROWS, 64, LANES)],
         [COARSE_FIELD] * 2,
-        COST, field, old, first, newer, mid, from_below, from_above, rc2, *coarse,
+        COST, field, old, first, newer, mid, from_out, from_in, rc2, *coarse,
     )
     return ends
 

time: 73.4 us -> 71.5 us (0.974)
  waiting for transfers between devices: 30.5 us -> 28.2 us
    ppermute x3, waiting for transfers between devices: 9.37 us -> 8.07 us  [over_tm(): lax.ppermute(value, ('tm', 'space'), [(a, count + b) for a, b in pairs])]
    ppermute x7, waiting for transfers between devices: 21.1 us -> 20.2 us  [swap(): return lax.ppermute(value, ('tm', 'space'), pairs)]
  transfers between devices with their start and end apart: 10 -> 10, of which waited for: 5 -> 4; matrix products, arithmetic and copies ran while one was open for 0% -> 0% of each run, Pallas kernels for 12% -> 12%
where the time goes in v4:
time: 71.5 us; the launch traced here: 71.2 us
  waiting for transfers between devices  28.2 us (39%)
  starting transfers between devices  24.1 us (34%)
  Pallas kernels  15.8 us (22%)
  local copies, waits for them, and re-layouts  2.94 us (4%)
    ppermute x7, starting transfers between devices, swap(): return lax.ppermute(value, ('tm', 'space'), pairs)  20.2 us
    ppermute x7, waiting for transfers between devices, swap(): return lax.ppermute(value, ('tm', 'space'), pairs)  20.2 us
    pallas_call x9, Pallas kernels, call(): pl.pallas_call(kernel, out_shape=outs, in_specs=[pl.BlockSpec(memory_spac...  15.8 us
    ppermute x3, waiting for transfers between devices, over_tm(): lax.ppermute(value, ('tm', 'space'), [(a, count + b) for a, b in pairs])  8.07 us
    ppermute x3, starting transfers between devices, over_tm(): lax.ppermute(value, ('tm', 'space'), [(a, count + b) for a, b in pairs])  3.88 us
    unnamed x6, local copies, waits for them, and re-layouts  2.94 us
  transfers between devices with their start and end apart: 10, of which 4 were waited for; matrix products, arithmetic and copies ran while one was open for 0% of the time, Pallas kernels for 12%

profile of v4, /device:TPU:127, one launch (start us, length us, event | category | flops | bytes accessed | tf_op | source)
XLA Modules:
  0.0 71.2 jit_solution(2224749244684515919)
XLA Ops:
  0.0 1.0 %copy-done = f32[2,8,64,128]{3,2,1,0:T(8,128)S(1)} copy-done((f32[2,8,64,128]{3,2,1,0:T(8,128)S(1)}, f32[2,8,64,128]{3,2,1,0:T(8,128)}, u32[]{:S(2)}) %copy-start) | copy-done | bytes 524312
  1.0 0.9 %copy-done.1 = f32[8,64,128]{2,1,0:T(8,128)S(1)} copy-done((f32[8,64,128]{2,1,0:T(8,128)S(1)}, f32[8,64,128]{2,1,0:T(8,128)}, u32[]{:S(2)}) %copy-start.1) | copy-done | bytes 262168
  2.0 0.9 %copy-done.2 = f32[8,64,128]{2,1,0:T(8,128)S(1)} copy-done((f32[8,64,128]{2,1,0:T(8,128)S(1)}, f32[8,64,128]{2,1,0:T(8,128)}, u32[]{:S(2)}) %copy-start.2) | copy-done | bytes 262168
  2.9 0.1 shard_map.37
  3.1 0.8 %collective-permute-start.1 = (f32[28,64,128]{2,1,0:T(8,128)S(1)}, f32[28,64,128]{2,1,0:T(8,128)S(1)}, u32[]{:S(2)}, u32[]{:S(2)}) collective-permute-start(f32[28,64,128]{2,1,0:T(8,128)S(1)} %get-tuple-element.54), channel_id=1, source_target_pairs={{0,1},{1,0},{2,3},{3,2},{4,5},{5,4},{6,7},{7,6},{8,9},{9,8},{10,11... | collective-permute-start | bytes 2752520 | tf_op jit(solution)/shard_map/ppermute | solution.py:485
  3.8 4.6 %collective-permute-start = (f32[24,64,128]{2,1,0:T(8,128)S(1)}, f32[24,64,128]{2,1,0:T(8,128)S(1)}, u32[]{:S(2)}, u32[]{:S(2)}) collective-permute-start(f32[24,64,128]{2,1,0:T(8,128)S(1)} %get-tuple-element.53), channel_id=1, source_target_pairs={{1,2},{2,1},{3,4},{4,3},{5,6},{6,5},{7,8},{8,7},{9,10},{10,9},{11,... | collective-permute-start | bytes 2359304 | tf_op jit(solution)/shard_map/ppermute | solution.py:485
  8.4 0.0 collective-permute-done.1.got_in
  8.4 3.5 %shard_map.38 = (f32[5,64,128]{2,1,0:T(8,128)S(1)}, f32[2,24,80,128]{3,2,1,0:T(8,128)S(1)}, f32[2,24,80,128]{3,2,1,0:T(8,128)S(1)}, f32[24,64,128]{2,1,0:T(8,128...) custom-call(f32[2,8,64,128]{3,2,1,0:T(8,128)S(1)} %copy-done, ...), custom_call_target="tpu_custom_call" | custom-call | flops 10000000 | bytes 1048576 | tf_op jit(solution)/shard_map/pallas_call | solution.py:463
  11.9 9.4 %collective-permute-done.got_out = f32[24,64,128]{2,1,0:T(8,128)S(1)} collective-permute-done((f32[24,64,128]{2,1,0:T(8,128)S(1)}, f32[24,64,128]{2,1,0:T(8,128)S(1)}, u32[]{:S(2)}, u32[]{:S(2)}) %collective-permute-start) | collective-permute-done | bytes 786464 | tf_op jit(solution)/shard_map/ppermute | solution.py:485
  21.3 2.2 %shard_map.39 = (f32[14,64,128]{2,1,0:T(8,128)S(1)}, f32[17,64,128]{2,1,0:T(8,128)S(1)}, f32[2,24,80,128]{3,2,1,0:T(8,128)S(1)}, f32[2,24,80,128]{3,2,1,0:T(8,12...) custom-call(f32[24,64,128]{2,1,0:T(8,128)S(1)} %collective-permute-d, ...), custom_call_target="tpu_custom_call", output_to_operand_aliasing={{2}: (1, {}), {3}: (2, {}), {4}: (3, {}), {5}: (4, {}), {6}... | custom-call | flops 10000000 | bytes 1048576 | tf_op jit(solution)/shard_map/pallas_call | solution.py:463
  23.5 0.1 collective-permute-start.3
  23.6 4.6 %collective-permute-start.2 = (f32[14,64,128]{2,1,0:T(8,128)S(1)}, f32[14,64,128]{2,1,0:T(8,128)S(1)}, u32[]{:S(2)}, u32[]{:S(2)}) collective-permute-start(f32[14,64,128]{2,1,0:T(8,128)S(1)} %get-tuple-element.64), channel_id=1, source_target_pairs={{1,2},{2,1},{3,4},{4,3},{5,6},{6,5},{7,8},{8,7},{9,10},{10,9},{11,... | collective-permute-start | bytes 1376264 | tf_op jit(solution)/shard_map/ppermute | solution.py:485
  28.2 5.2 %collective-permute-start.4 = (f32[5,64,128]{2,1,0:T(8,128)S(1)}, f32[5,64,128]{2,1,0:T(8,128)S(1)}, u32[]{:S(2)}, u32[]{:S(2)}) collective-permute-start(f32[5,64,128]{2,1,0:T(8,128)S(1)} %get-tuple-element.66), channel_id=1, source_target_pairs={{1,2},{2,1},{3,4},{4,3},{5,6},{6,5},{7,8},{8,7},{9,10},{10,9},{11,... | collective-permute-start | bytes 491528 | tf_op jit(solution)/shard_map/ppermute | solution.py:485
  33.4 6.0 %collective-permute-done.4.got_late = f32[5,64,128]{2,1,0:T(8,128)S(1)} collective-permute-done((f32[5,64,128]{2,1,0:T(8,128)S(1)}, f32[5,64,128]{2,1,0:T(8,128)S(1)}, u32[]{:S(2)}, u32[]{:S(2)}) %collective-permute-start.4) | collective-permute-done | bytes 163872 | tf_op jit(solution)/shard_map/ppermute | solution.py:485
  39.4 0.0 collective-permute-done.3.got_in.got_in2
  39.4 2.9 %shard_map.40 = (f32[2,24,80,128]{3,2,1,0:T(8,128)S(1)}, f32[2,24,80,128]{3,2,1,0:T(8,128)S(1)}, f32[24,64,128]{2,1,0:T(8,128)S(1)}, f32[24,64,128]{2,1,0:T(8,12...) custom-call(f32[17,64,128]{2,1,0:T(8,128)S(1)} %collective-permute-d, ...), custom_call_target="tpu_custom_call", output_to_operand_aliasing={{0}: (2, {}), {1}: (3, {}), {2}: (4, {}), {3}: (5, {}), {4}... | custom-call | flops 10000000 | bytes 1048576 | tf_op jit(solution)/shard_map/pallas_call | solution.py:463
  42.3 1.7 %shard_map.41 = (f32[2,4,32,128]{3,2,1,0:T(8,128)S(1)}, f32[20,48,128]{2,1,0:T(8,128)S(1)}, f32[20,48,128]{2,1,0:T(8,128)S(1)}) custom-call(f32[2,8,64,128]{3,2,1,0:T(8,128)S(1)} %copy-done, f32[24,64,128]{2,1,0:T(8,128)S(1)} %collective-permute-done.got_out, f32[28,64,128]{2,1,0:T(8,128)S(1)} %collective-permute-done.1.got_in, ...), custom_call_target="tpu_custom_call" | custom-call | flops 10000000 | bytes 1048576 | tf_op jit(solution)/shard_map/pallas_call | solution.py:463
  44.0 0.0 collective-permute-done.2.got_out
  44.0 2.4 %shard_map.42 = (f32[2,24,80,128]{3,2,1,0:T(8,128)S(1)}, f32[2,24,80,128]{3,2,1,0:T(8,128)S(1)}, f32[6,32,128]{2,1,0:T(8,128)S(1)}) custom-call(f32[14,64,128]{2,1,0:T(8,128)S(1)} %collective-permute-done.2.got_out, f32[2,24,80,128]{3,2,1,0:T(8,128)S(1)} %get-tuple-element.76.refs_0_, ...), custom_call_target="tpu_custom_call", output_to_operand_aliasing={{0}: (1, {}), {1}: (2, {})} | custom-call | flops 10000000 | bytes 1048576 | tf_op jit(solution)/shard_map/pallas_call | solution.py:463
  46.4 0.1 collective-permute-start.6
  46.5 4.9 %collective-permute-start.5 = (f32[6,32,128]{2,1,0:T(8,128)S(1)}, f32[6,32,128]{2,1,0:T(8,128)S(1)}, u32[]{:S(2)}, u32[]{:S(2)}) collective-permute-start(f32[6,32,128]{2,1,0:T(8,128)S(1)} %get-tuple-element.87.sent), channel_id=1, source_target_pairs={{1,2},{2,1},{3,4},{4,3},{5,6},{6,5},{7,8},{8,7},{9,10},{10,9},{11,... | collective-permute-start | bytes 294920 | tf_op jit(solution)/shard_map/ppermute | solution.py:485
  51.4 0.5 shard_map.43
  51.9 0.0 collective-permute-done.6.got_in
  51.9 4.8 %collective-permute-done.5.got_out = f32[6,32,128]{2,1,0:T(8,128)S(1)} collective-permute-done((f32[6,32,128]{2,1,0:T(8,128)S(1)}, f32[6,32,128]{2,1,0:T(8,128)S(1)}, u32[]{:S(2)}, u32[]{:S(2)}) %collective-permute-start.5) | collective-permute-done | bytes 98336 | tf_op jit(solution)/shard_map/ppermute | solution.py:485
  56.7 0.7 %shard_map.44 = (f32[4,32,128]{2,1,0:T(8,128)S(1)}, f32[2,32,128]{2,1,0:T(8,128)S(1)}, f32[2,32,128]{2,1,0:T(8,128)S(1)}, f32[10,32,128]{2,1,0:T(8,128)S(1)}, f32[4,32,128]{2,1,0:T(8,128)S(1)}) custom-call(f32[6,32,128]{2,1,0:T(8,128)S(1)} %get-tuple-element.87.sent, f32[6,32,128]{2,1,0:T(8,128)S(1)} %collective-permute-done.5.got_out, ...), custom_call_target="tpu_custom_call" | custom-call | flops 10000000 | bytes 1048576 | tf_op jit(solution)/shard_map/pallas_call | solution.py:463
  57.4 1.3 %collective-permute-start.7 = (f32[4,32,128]{2,1,0:T(8,128)S(1)}, f32[4,32,128]{2,1,0:T(8,128)S(1)}, u32[]{:S(2)}, u32[]{:S(2)}) collective-permute-start(f32[4,32,128]{2,1,0:T(8,128)S(1)} %get-tuple-element.98), channel_id=1, source_target_pairs={{0,128},{1,129},{2,130},{3,131},{4,132},{5,133},{6,134},{7,135},{8... | collective-permute-start | bytes 196616 | tf_op jit(solution)/shard_map/ppermute | solution.py:491
  58.7 1.3 %collective-permute-start.8 = (f32[2,32,128]{2,1,0:T(8,128)S(1)}, f32[2,32,128]{2,1,0:T(8,128)S(1)}, u32[]{:S(2)}, u32[]{:S(2)}) collective-permute-start(f32[2,32,128]{2,1,0:T(8,128)S(1)} %get-tuple-element.99), channel_id=1, source_target_pairs={{1,130},{2,129},{3,132},{4,131},{5,134},{6,133},{7,136},{8,135},{9... | collective-permute-start | bytes 98312 | tf_op jit(solution)/shard_map/ppermute | solution.py:491
  60.0 1.3 %collective-permute-start.9 = (f32[2,32,128]{2,1,0:T(8,128)S(1)}, f32[2,32,128]{2,1,0:T(8,128)S(1)}, u32[]{:S(2)}, u32[]{:S(2)}) collective-permute-start(f32[2,32,128]{2,1,0:T(8,128)S(1)} %get-tuple-element.100), channel_id=1, source_target_pairs={{0,129},{1,128},{2,131},{3,130},{4,133},{5,132},{6,135},{7,134},{8... | collective-permute-start | bytes 98312 | tf_op jit(solution)/shard_map/ppermute | solution.py:491
  61.3 8.1 %collective-permute-done.8.from_out = f32[2,32,128]{2,1,0:T(8,128)S(1)} collective-permute-done((f32[2,32,128]{2,1,0:T(8,128)S(1)}, f32[2,32,128]{2,1,0:T(8,128)S(1)}, u32[]{:S(2)}, u32[]{:S(2)}) %collective-permute-start.8) | collective-permute-done | bytes 32800 | tf_op jit(solution)/shard_map/ppermute | solution.py:491
  69.4 0.0 collective-permute-done.9.from_in
  69.4 0.0 collective-permute-done.7.tm_mid
  69.4 1.8 %shard_map.45 = f32[2,8,64,128]{3,2,1,0:T(8,128)} custom-call(f32[2,24,80,128]{3,2,1,0:T(8,128)S(1)} %get-tuple-element.86.fine, f32[2,4,32,128]{3,2,1,0:T(8,128)S(1)} %get-tuple-element.85.refs_8_.old, f32[10,32,128]{2,1,0:T(8,128)S(1)} %get-tuple-element.96.first, f32[4,32,128]{2,1,0:T(8,128)S(1)} %get-tuple-element.97.newer, ...), custom_call_target="tpu_custom_call" | custom-call | flops 10000000 | bytes 1048576 | tf_op jit(solution)/shard_map/pallas_call | solution.py:463
  (3 shorter events, 0.0 us)
Async XLA Ops:
  0.0 1.0 %copy-start = (f32[2,8,64,128]{3,2,1,0:T(8,128)S(1)}, f32[2,8,64,128]{3,2,1,0:T(8,128)}, u32[]{:S(2)}) copy-start(f32[2,8,64,128]{3,2,1,0:T(8,128)} %states.5) | copy-start | bytes 1572868
  1.0 0.9 %copy-start.1 = (f32[8,64,128]{2,1,0:T(8,128)S(1)}, f32[8,64,128]{2,1,0:T(8,128)}, u32[]{:S(2)}) copy-start(f32[8,64,128]{2,1,0:T(8,128)} %kappa.3) | copy-start | bytes 786436
  2.0 0.9 %copy-start.2 = (f32[8,64,128]{2,1,0:T(8,128)S(1)}, f32[8,64,128]{2,1,0:T(8,128)}, u32[]{:S(2)}) copy-start(f32[8,64,128]{2,1,0:T(8,128)} %rate.3) | copy-start | bytes 786436
  3.1 5.4 %collective-permute-start.1 = (f32[28,64,128]{2,1,0:T(8,128)S(1)}, f32[28,64,128]{2,1,0:T(8,128)S(1)}, u32[]{:S(2)}, u32[]{:S(2)}) collective-permute-start(f32[28,64,128]{2,1,0:T(8,128)S(1)} %get-tuple-element.54), channel_id=1, source_target_pairs={{0,1},{1,0},{2,3},{3,2},{4,5},{5,4},{6,7},{7,6},{8,9},{9,8},{10,11... | collective-permute-start | bytes 2752520 | tf_op jit(solution)/shard_map/ppermute | solution.py:485
  3.8 17.5 %collective-permute-start = (f32[24,64,128]{2,1,0:T(8,128)S(1)}, f32[24,64,128]{2,1,0:T(8,128)S(1)}, u32[]{:S(2)}, u32[]{:S(2)}) collective-permute-start(f32[24,64,128]{2,1,0:T(8,128)S(1)} %get-tuple-element.53), channel_id=1, source_target_pairs={{1,2},{2,1},{3,4},{4,3},{5,6},{6,5},{7,8},{8,7},{9,10},{10,9},{11,... | collective-permute-start | bytes 2359304 | tf_op jit(solution)/shard_map/ppermute | solution.py:485
  23.5 15.9 %collective-permute-start.3 = (f32[17,64,128]{2,1,0:T(8,128)S(1)}, f32[17,64,128]{2,1,0:T(8,128)S(1)}, u32[]{:S(2)}, u32[]{:S(2)}) collective-permute-start(f32[17,64,128]{2,1,0:T(8,128)S(1)} %get-tuple-element.65), channel_id=1, source_target_pairs={{0,1},{1,0},{2,3},{3,2},{4,5},{5,4},{6,7},{7,6},{8,9},{9,8},{10,11... | collective-permute-start | bytes 1671176 | tf_op jit(solution)/shard_map/ppermute | solution.py:485
  23.6 20.4 %collective-permute-start.2 = (f32[14,64,128]{2,1,0:T(8,128)S(1)}, f32[14,64,128]{2,1,0:T(8,128)S(1)}, u32[]{:S(2)}, u32[]{:S(2)}) collective-permute-start(f32[14,64,128]{2,1,0:T(8,128)S(1)} %get-tuple-element.64), channel_id=1, source_target_pairs={{1,2},{2,1},{3,4},{4,3},{5,6},{6,5},{7,8},{8,7},{9,10},{10,9},{11,... | collective-permute-start | bytes 1376264 | tf_op jit(solution)/shard_map/ppermute | solution.py:485
  28.2 11.2 %collective-permute-start.4 = (f32[5,64,128]{2,1,0:T(8,128)S(1)}, f32[5,64,128]{2,1,0:T(8,128)S(1)}, u32[]{:S(2)}, u32[]{:S(2)}) collective-permute-start(f32[5,64,128]{2,1,0:T(8,128)S(1)} %get-tuple-element.66), channel_id=1, source_target_pairs={{1,2},{2,1},{3,4},{4,3},{5,6},{6,5},{7,8},{8,7},{9,10},{10,9},{11,... | collective-permute-start | bytes 491528 | tf_op jit(solution)/shard_map/ppermute | solution.py:485
  46.4 5.5 %collective-permute-start.6 = (f32[6,32,128]{2,1,0:T(8,128)S(1)}, f32[6,32,128]{2,1,0:T(8,128)S(1)}, u32[]{:S(2)}, u32[]{:S(2)}) collective-permute-start(f32[6,32,128]{2,1,0:T(8,128)S(1)} %get-tuple-element.87.sent), channel_id=1, source_target_pairs={{0,1},{1,0},{2,3},{3,2},{4,5},{5,4},{6,7},{7,6},{8,9},{9,8},{10,11... | collective-permute-start | bytes 294920 | tf_op jit(solution)/shard_map/ppermute | solution.py:485
  46.5 10.2 %collective-permute-start.5 = (f32[6,32,128]{2,1,0:T(8,128)S(1)}, f32[6,32,128]{2,1,0:T(8,128)S(1)}, u32[]{:S(2)}, u32[]{:S(2)}) collective-permute-start(f32[6,32,128]{2,1,0:T(8,128)S(1)} %get-tuple-element.87.sent), channel_id=1, source_target_pairs={{1,2},{2,1},{3,4},{4,3},{5,6},{6,5},{7,8},{8,7},{9,10},{10,9},{11,... | collective-permute-start | bytes 294920 | tf_op jit(solution)/shard_map/ppermute | solution.py:485
  57.4 12.0 %collective-permute-start.7 = (f32[4,32,128]{2,1,0:T(8,128)S(1)}, f32[4,32,128]{2,1,0:T(8,128)S(1)}, u32[]{:S(2)}, u32[]{:S(2)}) collective-permute-start(f32[4,32,128]{2,1,0:T(8,128)S(1)} %get-tuple-element.98), channel_id=1, source_target_pairs={{0,128},{1,129},{2,130},{3,131},{4,132},{5,133},{6,134},{7,135},{8... | collective-permute-start | bytes 196616 | tf_op jit(solution)/shard_map/ppermute | solution.py:491
  58.7 10.7 %collective-permute-start.8 = (f32[2,32,128]{2,1,0:T(8,128)S(1)}, f32[2,32,128]{2,1,0:T(8,128)S(1)}, u32[]{:S(2)}, u32[]{:S(2)}) collective-permute-start(f32[2,32,128]{2,1,0:T(8,128)S(1)} %get-tuple-element.99), channel_id=1, source_target_pairs={{1,130},{2,129},{3,132},{4,131},{5,134},{6,133},{7,136},{8,135},{9... | collective-permute-start | bytes 98312 | tf_op jit(solution)/shard_map/ppermute | solution.py:491
  60.0 9.4 %collective-permute-start.9 = (f32[2,32,128]{2,1,0:T(8,128)S(1)}, f32[2,32,128]{2,1,0:T(8,128)S(1)}, u32[]{:S(2)}, u32[]{:S(2)}) collective-permute-start(f32[2,32,128]{2,1,0:T(8,128)S(1)} %get-tuple-element.100), channel_id=1, source_target_pairs={{0,129},{1,128},{2,131},{3,130},{4,133},{5,132},{6,135},{7,134},{8... | collective-permute-start | bytes 98312 | tf_op jit(solution)/shard_map/ppermute | solution.py:491

commit v5 on v4

--- a/solution.py
+++ b/solution.py
@@ -159,18 +159,27 @@
     return lax.axis_index("space") % 2
 
 
-def pack_kernel(states, kappa, rate, send_out, send_in):
+def fetch(pairs, sems):
+    copies = [pltpu.make_async_copy(a, b, sems.at[n]) for n, (a, b) in enumerate(pairs)]
+    for copy in copies:
+        copy.start()
+    for copy in copies:
+        copy.wait()
+
+
+def pack_kernel(states, kappa, rate, send_out, send_in, sems):
     odd = odd_here()
     out, near = 2 * odd, 2 - 2 * odd
-    for i in range(HALO):
-        for w in range(2):
-            send_out[HALO * w + i] = states[w, out + i]
-            send_in[HALO * w + i] = states[w, near + i]
-        send_out[2 * HALO + i] = kappa[out + i]
-        send_out[3 * HALO + i] = rate[out + i]
-    for i in range(ROWS):
-        send_in[2 * HALO + i] = kappa[i]
-        send_in[2 * HALO + ROWS + i] = rate[i]
+    copies = [
+        (kappa.at[pl.ds(out, HALO)], send_out.at[pl.ds(2 * HALO, HALO)]),
+        (rate.at[pl.ds(out, HALO)], send_out.at[pl.ds(3 * HALO, HALO)]),
+        (kappa, send_in.at[pl.ds(2 * HALO, ROWS)]),
+        (rate, send_in.at[pl.ds(2 * HALO + ROWS, ROWS)]),
+    ]
+    for w in range(2):
+        copies.append((states.at[w, pl.ds(out, HALO)], send_out.at[pl.ds(HALO * w, HALO)]))
+        copies.append((states.at[w, pl.ds(near, HALO)], send_in.at[pl.ds(HALO * w, HALO)]))
+    fetch(copies, sems)
 
 
 def place_halo(got, field, k_ext, r_ext, above, depth):
@@ -197,36 +206,27 @@
     )
 
 
-def place_own(states, field):
-    def own(i, carry):
-        for w in range(2):
-            field[w, BASE + i, PAD : PAD + 64, :] = states[w, i]
-        return carry
-
-    lax.fori_loop(0, ROWS, own, 0)
-
-
 def lines_of(ref, lead, row):
     return lambda part, first: ref[lead + (row + part, pl.ds(PAD + first, 32, stride=2))]
 
 
-def inner_first_kernel(states, kappa, rate, got_in, late, field, other, diag, cx, cy, cz, cw, r_ext, k_ext):
+def inner_first_kernel(
+    states, kappa, rate, got_in, late, field, other, diag, cx, cy, cz, cw, r_ext, k_ext, sems
+):
     odd = odd_here()
     clear_pads_flat(k_ext, 0, EXT, 64)
     clear_pads(field, 0, EXT, 64)
     clear_pads(other, 0, EXT, 64)
-    place_own(states, field)
-
-    def own(i, carry):
-        k_ext[BASE + i, PAD : PAD + 64, :] = kappa[i]
-        r_ext[BASE + i, PAD : PAD + 64, :] = rate[i]
-        return carry
-
-    lax.fori_loop(0, ROWS, own, 0)
+    rows, lines = pl.ds(BASE, ROWS), pl.ds(PAD, 64)
+    fetch(
+        [(states.at[w], field.at[w, rows, lines]) for w in range(2)]
+        + [(kappa, k_ext.at[rows, lines]), (rate, r_ext.at[rows, lines])],
+        sems,
+    )
     place_halo(got_in, field, k_ext, r_ext, 1 - odd, ROWS)
     for i in range(2):
-        late[i] = kappa[6 - 6 * odd + i]
-        late[2 + i] = rate[6 - 6 * odd + i]
+        late[i] = k_ext[BASE + 6 - 6 * odd + i, PAD : PAD + 64, :]
+        late[2 + i] = r_ext[BASE + 6 - 6 * odd + i, PAD : PAD + 64, :]
         late[4, 32 * i : 32 * i + 32, :] = coarse_pair(k_ext, r_ext, 16 - 12 * odd + 2 * i)
     coefs = (diag, cx, cy, cz, cw)
     build_coefs(k_ext, r_ext, coefs, 9 - 8 * odd, 14, 64, 1)
@@ -319,9 +319,9 @@
         send[1 + i] = pack2(*rows)
 
 
-def old_kernel(states, got_out, got_in, k_ext, r_ext, old, kc, rc, field, diag, cx, cy, cz, cw, here, there):
-    odd = odd_here()
-    place_own(states, field)
+def old_kernel(states, got_out, got_in, k_ext, r_ext, old, kc, rc, field, diag, cx, cy, cz, cw, here, there, sems):
+    odd = odd_here()
+    fetch([(states.at[w], field.at[w, pl.ds(BASE, ROWS), pl.ds(PAD, 64)]) for w in range(2)], sems)
     for got, above in ((got_out, odd), (got_in, 1 - odd)):
         for w in range(2):
 
@@ -459,13 +459,16 @@
     return jax.ShapeDtypeStruct(sizes, F32)
 
 
-def call(kernel, outs, scratch, cost, *args, aliases=None):
+def call(kernel, outs, scratch, cost, *args, aliases=None, far=0, copies=0):
+    spaces = [pltpu.HBM] * far + [pltpu.VMEM] * (len(args) - far)
+    args = [pltpu.with_memory_space_constraint(a, pltpu.HBM) for a in args[:far]] + list(args[far:])
     return pl.pallas_call(
         kernel,
         out_shape=outs,
-        in_specs=[pl.BlockSpec(memory_space=pltpu.VMEM)] * len(args),
+        in_specs=[pl.BlockSpec(memory_space=space) for space in spaces],
         out_specs=[pl.BlockSpec(memory_space=pltpu.VMEM)] * len(outs),
-        scratch_shapes=[pltpu.VMEM(sizes, F32) for sizes in scratch],
+        scratch_shapes=[pltpu.VMEM(sizes, F32) for sizes in scratch]
+        + ([pltpu.SemaphoreType.DMA((copies,))] if copies else []),
         input_output_aliases=aliases or {},
         compiler_params=pltpu.CompilerParams(vmem_limit_bytes=24 * 1024 * 1024),
         cost_estimate=pl.CostEstimate(flops=cost, bytes_accessed=1 << 20, transcendentals=0),
@@ -514,13 +517,13 @@
     coarse_coefs = [shape(*sizes) for sizes in COARSE_COEFS]
     send_out, send_in = call(
         pack_kernel, [shape(4 * HALO, 64, LANES), shape(2 * HALO + 2 * ROWS, 64, LANES)],
-        [], 1000, states, kappa, rate,
+        [], 1000, states, kappa, rate, far=3, copies=8,
     )
     got_out, got_in = swaps(send_out, send_in)
     late, *work = call(
         inner_first_kernel,
         [shape(5, 64, LANES)] + fields + fine_coefs + [shape(*FINE_FLAT)] * 2,
-        [], COST, states, kappa, rate, got_in,
+        [], COST, states, kappa, rate, got_in, far=3, copies=4,
     )
     got_late = swap(late, True)
     send_out2, send_in2, *work = call(
@@ -537,7 +540,7 @@
         old_kernel,
         [shape(2, CROWS, 32, LANES), shape(*COARSE_FLAT), shape(*COARSE_FLAT)],
         [FINE_FIELD] + COARSE_COEFS + [COARSE_FIELD] * 2,
-        COST, states, got_out, got_in, k_ext, r_ext,
+        COST, states, got_out, got_in, k_ext, r_ext, far=1, copies=2,
     )
     field, other, send3 = call(
         outer_second_kernel,

time: 71.5 us -> 70.9 us (level)
  Pallas kernels: 15.8 us -> 19.3 us
  local copies, waits for them, and re-layouts: 2.94 us -> 0 us
  waiting for transfers between devices: 28.2 us -> 27.1 us
    pallas_call x9, Pallas kernels: 15.8 us -> 19.3 us  [call(): pl.pallas_call(kernel, out_shape=outs, in_specs=[pl.BlockSpec(memory_spac...]
    unnamed x6 -> x0, local copies, waits for them, and re-layouts: 2.94 us -> none
    ppermute x7, waiting for transfers between devices: 20.2 us -> 19.1 us  [swap(): return lax.ppermute(value, ('tm', 'space'), pairs)]
  transfers between devices with their start and end apart: 10 -> 10, of which waited for: 4 -> 4; matrix products, arithmetic and copies ran while one was open for 0% -> 0% of each run, Pallas kernels for 12% -> 15%
where the time goes in v5:
time: 70.9 us; the launch traced here: 70.6 us
  waiting for transfers between devices  27.1 us (38%)
  starting transfers between devices  24.1 us (34%)
  Pallas kernels  19.3 us (27%)
    ppermute x7, starting transfers between devices, swap(): return lax.ppermute(value, ('tm', 'space'), pairs)  20.2 us
    pallas_call x9, Pallas kernels, call(): pl.pallas_call(kernel, out_shape=outs, in_specs=[pl.BlockSpec(memory_spac...  19.3 us
    ppermute x7, waiting for transfers between devices, swap(): return lax.ppermute(value, ('tm', 'space'), pairs)  19.1 us
    ppermute x3, waiting for transfers between devices, over_tm(): lax.ppermute(value, ('tm', 'space'), [(a, count + b) for a, b in pairs])  8.07 us
    ppermute x3, starting transfers between devices, over_tm(): lax.ppermute(value, ('tm', 'space'), [(a, count + b) for a, b in pairs])  3.88 us
  transfers between devices with their start and end apart: 10, of which 4 were waited for; matrix products, arithmetic and copies ran while one was open for 0% of the time, Pallas kernels for 15%

profile of v5, /device:TPU:127, one launch (start us, length us, event | category | flops | bytes accessed | tf_op | source)
XLA Modules:
  0.0 70.6 jit_solution(1796745254353674568)
XLA Ops:
  0.0 1.5 %shard_map.37 = (f32[24,64,128]{2,1,0:T(8,128)S(1)}, f32[28,64,128]{2,1,0:T(8,128)S(1)}) custom-call(f32[2,8,64,128]{3,2,1,0:T(8,128)} %states.5, f32[8,64,128]{2,1,0:T(8,128)} %kappa.3, f32[8,64,128]{2,1,0:T(8,128)} %rate.3), custom_call_target="tpu_custom_call" | custom-call | flops 1000 | bytes 1048576 | tf_op jit(solution)/shard_map/pallas_call | solution.py:465
  1.5 0.8 %collective-permute-start.1 = (f32[28,64,128]{2,1,0:T(8,128)S(1)}, f32[28,64,128]{2,1,0:T(8,128)S(1)}, u32[]{:S(2)}, u32[]{:S(2)}) collective-permute-start(f32[28,64,128]{2,1,0:T(8,128)S(1)} %get-tuple-element.54), channel_id=1, source_target_pairs={{0,1},{1,0},{2,3},{3,2},{4,5},{5,4},{6,7},{7,6},{8,9},{9,8},{10,11... | collective-permute-start | bytes 2752520 | tf_op jit(solution)/shard_map/ppermute | solution.py:488
  2.3 4.6 %collective-permute-start = (f32[24,64,128]{2,1,0:T(8,128)S(1)}, f32[24,64,128]{2,1,0:T(8,128)S(1)}, u32[]{:S(2)}, u32[]{:S(2)}) collective-permute-start(f32[24,64,128]{2,1,0:T(8,128)S(1)} %get-tuple-element.53), channel_id=1, source_target_pairs={{1,2},{2,1},{3,4},{4,3},{5,6},{6,5},{7,8},{8,7},{9,10},{10,9},{11,... | collective-permute-start | bytes 2359304 | tf_op jit(solution)/shard_map/ppermute | solution.py:488
  6.9 0.0 collective-permute-done.1.got_in
  6.9 4.6 %shard_map.38 = (f32[5,64,128]{2,1,0:T(8,128)S(1)}, f32[2,24,80,128]{3,2,1,0:T(8,128)S(1)}, f32[2,24,80,128]{3,2,1,0:T(8,128)S(1)}, f32[24,64,128]{2,1,0:T(8,128...) custom-call(f32[2,8,64,128]{3,2,1,0:T(8,128)} %states.5, ...), custom_call_target="tpu_custom_call" | custom-call | flops 10000000 | bytes 1048576 | tf_op jit(solution)/shard_map/pallas_call | solution.py:465
  11.5 8.3 %collective-permute-done.got_out = f32[24,64,128]{2,1,0:T(8,128)S(1)} collective-permute-done((f32[24,64,128]{2,1,0:T(8,128)S(1)}, f32[24,64,128]{2,1,0:T(8,128)S(1)}, u32[]{:S(2)}, u32[]{:S(2)}) %collective-permute-start) | collective-permute-done | bytes 786464 | tf_op jit(solution)/shard_map/ppermute | solution.py:488
  19.8 2.2 %shard_map.39 = (f32[14,64,128]{2,1,0:T(8,128)S(1)}, f32[17,64,128]{2,1,0:T(8,128)S(1)}, f32[2,24,80,128]{3,2,1,0:T(8,128)S(1)}, f32[2,24,80,128]{3,2,1,0:T(8,12...) custom-call(f32[24,64,128]{2,1,0:T(8,128)S(1)} %collective-permute-d, ...), custom_call_target="tpu_custom_call", output_to_operand_aliasing={{2}: (1, {}), {3}: (2, {}), {4}: (3, {}), {5}: (4, {}), {6}... | custom-call | flops 10000000 | bytes 1048576 | tf_op jit(solution)/shard_map/pallas_call | solution.py:465
  22.0 0.1 collective-permute-start.3
  22.1 4.6 %collective-permute-start.2 = (f32[14,64,128]{2,1,0:T(8,128)S(1)}, f32[14,64,128]{2,1,0:T(8,128)S(1)}, u32[]{:S(2)}, u32[]{:S(2)}) collective-permute-start(f32[14,64,128]{2,1,0:T(8,128)S(1)} %get-tuple-element.64), channel_id=1, source_target_pairs={{1,2},{2,1},{3,4},{4,3},{5,6},{6,5},{7,8},{8,7},{9,10},{10,9},{11,... | collective-permute-start | bytes 1376264 | tf_op jit(solution)/shard_map/ppermute | solution.py:488
  26.7 5.2 %collective-permute-start.4 = (f32[5,64,128]{2,1,0:T(8,128)S(1)}, f32[5,64,128]{2,1,0:T(8,128)S(1)}, u32[]{:S(2)}, u32[]{:S(2)}) collective-permute-start(f32[5,64,128]{2,1,0:T(8,128)S(1)} %get-tuple-element.66), channel_id=1, source_target_pairs={{1,2},{2,1},{3,4},{4,3},{5,6},{6,5},{7,8},{8,7},{9,10},{10,9},{11,... | collective-permute-start | bytes 491528 | tf_op jit(solution)/shard_map/ppermute | solution.py:488
  31.9 6.0 %collective-permute-done.4.got_late = f32[5,64,128]{2,1,0:T(8,128)S(1)} collective-permute-done((f32[5,64,128]{2,1,0:T(8,128)S(1)}, f32[5,64,128]{2,1,0:T(8,128)S(1)}, u32[]{:S(2)}, u32[]{:S(2)}) %collective-permute-start.4) | collective-permute-done | bytes 163872 | tf_op jit(solution)/shard_map/ppermute | solution.py:488
  37.8 0.0 collective-permute-done.3.got_in.got_in2
  37.9 2.9 %shard_map.40 = (f32[2,24,80,128]{3,2,1,0:T(8,128)S(1)}, f32[2,24,80,128]{3,2,1,0:T(8,128)S(1)}, f32[24,64,128]{2,1,0:T(8,128)S(1)}, f32[24,64,128]{2,1,0:T(8,12...) custom-call(f32[17,64,128]{2,1,0:T(8,128)S(1)} %collective-permute-d, ...), custom_call_target="tpu_custom_call", output_to_operand_aliasing={{0}: (2, {}), {1}: (3, {}), {2}: (4, {}), {3}: (5, {}), {4}... | custom-call | flops 10000000 | bytes 1048576 | tf_op jit(solution)/shard_map/pallas_call | solution.py:465
  40.8 2.7 %shard_map.41 = (f32[2,4,32,128]{3,2,1,0:T(8,128)S(1)}, f32[20,48,128]{2,1,0:T(8,128)S(1)}, f32[20,48,128]{2,1,0:T(8,128)S(1)}) custom-call(f32[2,8,64,128]{3,2,1,0:T(8,128)} %states.5, f32[24,64,128]{2,1,0:T(8,128)S(1)} %collective-permute-done.got_out, f32[28,64,128]{2,1,0:T(8,128)S(1)} %collective-permute-done.1.got_in, ...), custom_call_target="tpu_custom_call" | custom-call | flops 10000000 | bytes 1048576 | tf_op jit(solution)/shard_map/pallas_call | solution.py:465
  43.4 0.0 collective-permute-done.2.got_out
  43.4 2.4 %shard_map.42 = (f32[2,24,80,128]{3,2,1,0:T(8,128)S(1)}, f32[2,24,80,128]{3,2,1,0:T(8,128)S(1)}, f32[6,32,128]{2,1,0:T(8,128)S(1)}) custom-call(f32[14,64,128]{2,1,0:T(8,128)S(1)} %collective-permute-done.2.got_out, f32[2,24,80,128]{3,2,1,0:T(8,128)S(1)} %get-tuple-element.76.refs_0_, ...), custom_call_target="tpu_custom_call", output_to_operand_aliasing={{0}: (1, {}), {1}: (2, {})} | custom-call | flops 10000000 | bytes 1048576 | tf_op jit(solution)/shard_map/pallas_call | solution.py:465
  45.9 0.1 collective-permute-start.6
  46.0 4.9 %collective-permute-start.5 = (f32[6,32,128]{2,1,0:T(8,128)S(1)}, f32[6,32,128]{2,1,0:T(8,128)S(1)}, u32[]{:S(2)}, u32[]{:S(2)}) collective-permute-start(f32[6,32,128]{2,1,0:T(8,128)S(1)} %get-tuple-element.87.sent), channel_id=1, source_target_pairs={{1,2},{2,1},{3,4},{4,3},{5,6},{6,5},{7,8},{8,7},{9,10},{10,9},{11,... | collective-permute-start | bytes 294920 | tf_op jit(solution)/shard_map/ppermute | solution.py:488
  50.9 0.5 shard_map.43
  51.4 0.0 collective-permute-done.6.got_in
  51.4 4.8 %collective-permute-done.5.got_out = f32[6,32,128]{2,1,0:T(8,128)S(1)} collective-permute-done((f32[6,32,128]{2,1,0:T(8,128)S(1)}, f32[6,32,128]{2,1,0:T(8,128)S(1)}, u32[]{:S(2)}, u32[]{:S(2)}) %collective-permute-start.5) | collective-permute-done | bytes 98336 | tf_op jit(solution)/shard_map/ppermute | solution.py:488
  56.1 0.7 %shard_map.44 = (f32[4,32,128]{2,1,0:T(8,128)S(1)}, f32[2,32,128]{2,1,0:T(8,128)S(1)}, f32[2,32,128]{2,1,0:T(8,128)S(1)}, f32[10,32,128]{2,1,0:T(8,128)S(1)}, f32[4,32,128]{2,1,0:T(8,128)S(1)}) custom-call(f32[6,32,128]{2,1,0:T(8,128)S(1)} %get-tuple-element.87.sent, f32[6,32,128]{2,1,0:T(8,128)S(1)} %collective-permute-done.5.got_out, ...), custom_call_target="tpu_custom_call" | custom-call | flops 10000000 | bytes 1048576 | tf_op jit(solution)/shard_map/pallas_call | solution.py:465
  56.9 1.3 %collective-permute-start.7 = (f32[4,32,128]{2,1,0:T(8,128)S(1)}, f32[4,32,128]{2,1,0:T(8,128)S(1)}, u32[]{:S(2)}, u32[]{:S(2)}) collective-permute-start(f32[4,32,128]{2,1,0:T(8,128)S(1)} %get-tuple-element.98), channel_id=1, source_target_pairs={{0,128},{1,129},{2,130},{3,131},{4,132},{5,133},{6,134},{7,135},{8... | collective-permute-start | bytes 196616 | tf_op jit(solution)/shard_map/ppermute | solution.py:494
  58.2 1.3 %collective-permute-start.8 = (f32[2,32,128]{2,1,0:T(8,128)S(1)}, f32[2,32,128]{2,1,0:T(8,128)S(1)}, u32[]{:S(2)}, u32[]{:S(2)}) collective-permute-start(f32[2,32,128]{2,1,0:T(8,128)S(1)} %get-tuple-element.99), channel_id=1, source_target_pairs={{1,130},{2,129},{3,132},{4,131},{5,134},{6,133},{7,136},{8,135},{9... | collective-permute-start | bytes 98312 | tf_op jit(solution)/shard_map/ppermute | solution.py:494
  59.5 1.3 %collective-permute-start.9 = (f32[2,32,128]{2,1,0:T(8,128)S(1)}, f32[2,32,128]{2,1,0:T(8,128)S(1)}, u32[]{:S(2)}, u32[]{:S(2)}) collective-permute-start(f32[2,32,128]{2,1,0:T(8,128)S(1)} %get-tuple-element.100), channel_id=1, source_target_pairs={{0,129},{1,128},{2,131},{3,130},{4,133},{5,132},{6,135},{7,134},{8... | collective-permute-start | bytes 98312 | tf_op jit(solution)/shard_map/ppermute | solution.py:494
  60.8 8.1 %collective-permute-done.8.from_out = f32[2,32,128]{2,1,0:T(8,128)S(1)} collective-permute-done((f32[2,32,128]{2,1,0:T(8,128)S(1)}, f32[2,32,128]{2,1,0:T(8,128)S(1)}, u32[]{:S(2)}, u32[]{:S(2)}) %collective-permute-start.8) | collective-permute-done | bytes 32800 | tf_op jit(solution)/shard_map/ppermute | solution.py:494
  68.9 0.0 collective-permute-done.9.from_in
  68.9 0.0 collective-permute-done.7.tm_mid
  68.9 1.8 %shard_map.45 = f32[2,8,64,128]{3,2,1,0:T(8,128)} custom-call(f32[2,24,80,128]{3,2,1,0:T(8,128)S(1)} %get-tuple-element.86.fine, f32[2,4,32,128]{3,2,1,0:T(8,128)S(1)} %get-tuple-element.85.refs_8_.old, f32[10,32,128]{2,1,0:T(8,128)S(1)} %get-tuple-element.96.first, f32[4,32,128]{2,1,0:T(8,128)S(1)} %get-tuple-element.97.newer, ...), custom_call_target="tpu_custom_call" | custom-call | flops 10000000 | bytes 1048576 | tf_op jit(solution)/shard_map/pallas_call | solution.py:465
Async XLA Ops:
  1.5 5.4 %collective-permute-start.1 = (f32[28,64,128]{2,1,0:T(8,128)S(1)}, f32[28,64,128]{2,1,0:T(8,128)S(1)}, u32[]{:S(2)}, u32[]{:S(2)}) collective-permute-start(f32[28,64,128]{2,1,0:T(8,128)S(1)} %get-tuple-element.54), channel_id=1, source_target_pairs={{0,1},{1,0},{2,3},{3,2},{4,5},{5,4},{6,7},{7,6},{8,9},{9,8},{10,11... | collective-permute-start | bytes 2752520 | tf_op jit(solution)/shard_map/ppermute | solution.py:488
  2.3 17.5 %collective-permute-start = (f32[24,64,128]{2,1,0:T(8,128)S(1)}, f32[24,64,128]{2,1,0:T(8,128)S(1)}, u32[]{:S(2)}, u32[]{:S(2)}) collective-permute-start(f32[24,64,128]{2,1,0:T(8,128)S(1)} %get-tuple-element.53), channel_id=1, source_target_pairs={{1,2},{2,1},{3,4},{4,3},{5,6},{6,5},{7,8},{8,7},{9,10},{10,9},{11,... | collective-permute-start | bytes 2359304 | tf_op jit(solution)/shard_map/ppermute | solution.py:488
  22.0 15.9 %collective-permute-start.3 = (f32[17,64,128]{2,1,0:T(8,128)S(1)}, f32[17,64,128]{2,1,0:T(8,128)S(1)}, u32[]{:S(2)}, u32[]{:S(2)}) collective-permute-start(f32[17,64,128]{2,1,0:T(8,128)S(1)} %get-tuple-element.65), channel_id=1, source_target_pairs={{0,1},{1,0},{2,3},{3,2},{4,5},{5,4},{6,7},{7,6},{8,9},{9,8},{10,11... | collective-permute-start | bytes 1671176 | tf_op jit(solution)/shard_map/ppermute | solution.py:488
  22.1 21.4 %collective-permute-start.2 = (f32[14,64,128]{2,1,0:T(8,128)S(1)}, f32[14,64,128]{2,1,0:T(8,128)S(1)}, u32[]{:S(2)}, u32[]{:S(2)}) collective-permute-start(f32[14,64,128]{2,1,0:T(8,128)S(1)} %get-tuple-element.64), channel_id=1, source_target_pairs={{1,2},{2,1},{3,4},{4,3},{5,6},{6,5},{7,8},{8,7},{9,10},{10,9},{11,... | collective-permute-start | bytes 1376264 | tf_op jit(solution)/shard_map/ppermute | solution.py:488
  26.7 11.2 %collective-permute-start.4 = (f32[5,64,128]{2,1,0:T(8,128)S(1)}, f32[5,64,128]{2,1,0:T(8,128)S(1)}, u32[]{:S(2)}, u32[]{:S(2)}) collective-permute-start(f32[5,64,128]{2,1,0:T(8,128)S(1)} %get-tuple-element.66), channel_id=1, source_target_pairs={{1,2},{2,1},{3,4},{4,3},{5,6},{6,5},{7,8},{8,7},{9,10},{10,9},{11,... | collective-permute-start | bytes 491528 | tf_op jit(solution)/shard_map/ppermute | solution.py:488
  45.9 5.5 %collective-permute-start.6 = (f32[6,32,128]{2,1,0:T(8,128)S(1)}, f32[6,32,128]{2,1,0:T(8,128)S(1)}, u32[]{:S(2)}, u32[]{:S(2)}) collective-permute-start(f32[6,32,128]{2,1,0:T(8,128)S(1)} %get-tuple-element.87.sent), channel_id=1, source_target_pairs={{0,1},{1,0},{2,3},{3,2},{4,5},{5,4},{6,7},{7,6},{8,9},{9,8},{10,11... | collective-permute-start | bytes 294920 | tf_op jit(solution)/shard_map/ppermute | solution.py:488
  46.0 10.2 %collective-permute-start.5 = (f32[6,32,128]{2,1,0:T(8,128)S(1)}, f32[6,32,128]{2,1,0:T(8,128)S(1)}, u32[]{:S(2)}, u32[]{:S(2)}) collective-permute-start(f32[6,32,128]{2,1,0:T(8,128)S(1)} %get-tuple-element.87.sent), channel_id=1, source_target_pairs={{1,2},{2,1},{3,4},{4,3},{5,6},{6,5},{7,8},{8,7},{9,10},{10,9},{11,... | collective-permute-start | bytes 294920 | tf_op jit(solution)/shard_map/ppermute | solution.py:488
  56.9 12.0 %collective-permute-start.7 = (f32[4,32,128]{2,1,0:T(8,128)S(1)}, f32[4,32,128]{2,1,0:T(8,128)S(1)}, u32[]{:S(2)}, u32[]{:S(2)}) collective-permute-start(f32[4,32,128]{2,1,0:T(8,128)S(1)} %get-tuple-element.98), channel_id=1, source_target_pairs={{0,128},{1,129},{2,130},{3,131},{4,132},{5,133},{6,134},{7,135},{8... | collective-permute-start | bytes 196616 | tf_op jit(solution)/shard_map/ppermute | solution.py:494
  58.2 10.7 %collective-permute-start.8 = (f32[2,32,128]{2,1,0:T(8,128)S(1)}, f32[2,32,128]{2,1,0:T(8,128)S(1)}, u32[]{:S(2)}, u32[]{:S(2)}) collective-permute-start(f32[2,32,128]{2,1,0:T(8,128)S(1)} %get-tuple-element.99), channel_id=1, source_target_pairs={{1,130},{2,129},{3,132},{4,131},{5,134},{6,133},{7,136},{8,135},{9... | collective-permute-start | bytes 98312 | tf_op jit(solution)/shard_map/ppermute | solution.py:494
  59.5 9.4 %collective-permute-start.9 = (f32[2,32,128]{2,1,0:T(8,128)S(1)}, f32[2,32,128]{2,1,0:T(8,128)S(1)}, u32[]{:S(2)}, u32[]{:S(2)}) collective-permute-start(f32[2,32,128]{2,1,0:T(8,128)S(1)} %get-tuple-element.100), channel_id=1, source_target_pairs={{0,129},{1,128},{2,131},{3,130},{4,133},{5,132},{6,135},{7,134},{8... | collective-permute-start | bytes 98312 | tf_op jit(solution)/shard_map/ppermute | solution.py:494
